TPU v7x, 256 devices: a whole 4x4x8 slice. The times are simulated.
256 devices in a mesh: row: 32 (over z_lo, y, core), col: 8 (over x, z_hi).
Axes of the slice: x: 4, y: 4, z: 8 (z_hi: 2, z_lo: 4; z = z_hi * 4 + z_lo), core: 2. Of those that a mesh axis runs over, the one named last changes fastest.
Arguments:
- pair_rep: bfloat16 [2048, 2048, 128], P('row', 'col'), may hold values from -6 to 6
- bias_weight: bfloat16 [128, 12], replicated, may hold values from -0.5 to 0.5
- head_weight: float32 [12], replicated, may hold values from -1 to 1
- queries: float32 [192, 2048], P(None, 'row'), may hold values from -48 to 48, as said below
- key_vectors: float32 [192, 2048], P(None, 'col'), may hold values from -48 to 48, as said below
- values: float32 [192, 2048], P(None, 'col'), may hold values from -6 to 6
- query_points: float32 [3, 48, 2048], P(None, None, 'row'), may hold values from -6 to 6
- key_points: float32 [3, 48, 2048], P(None, None, 'col'), may hold values from -6 to 6
- value_points: float32 [3, 96, 2048], P(None, None, 'col'), may hold values from -6 to 6
- rotations: float32 [3, 3, 2048], replicated, may hold values from -1 to 1, as said below
- translations: float32 [3, 2048], replicated, may hold values from -12 to 12
- residue_count: int32 [1], replicated, may hold values from 1024 to 2048
- grad_output: float32 [192, 2048], P(None, 'row'), may hold values from -6 to 6
- grad_points: float32 [3, 96, 2048], P(None, None, 'row'), may hold values from -6 to 6
- grad_pair: bfloat16 [2048, 12, 128], P('row'), may hold values from -2 to 2
Outputs:
- pair_grad: bfloat16 [2048, 2048, 128], P('row', 'col')
- query_grad: float32 [192, 2048], P(None, ('row', 'col'))
- query_point_grad: float32 [3, 48, 2048], P(None, None, ('row', 'col'))
- query_frame_grad: float32 [3, 4, 2048], P(None, None, ('row', 'col'))
- key_grad: float32 [192, 2048], P(None, ('col', 'row'))
- value_grad: float32 [192, 2048], P(None, ('col', 'row'))
- key_point_grad: float32 [3, 48, 2048], P(None, None, ('col', 'row'))
- value_point_grad: float32 [3, 96, 2048], P(None, None, ('col', 'row'))
- key_frame_grad: float32 [3, 4, 2048], P(None, None, ('col', 'row'))
- bias_weight_grad: float32 [128, 12], replicated
- head_weight_grad: float32 [12], replicated
Inputs may be any that keep to these rules, and one draw needn't show every extreme that they name: `queries`: entries of order one, except a few residues whose vectors are much larger. `key_vectors`: entries of order one, except a few residues whose vectors are much larger. `rotations`: each residue's 3 x 3 matrix is a rotation: orthonormal with determinant one.
All inputs are finite; a program needn't handle non-finite values.
Results may differ from a plain program's by a relative error of at most 0.0049.
Values sent between devices are 32-bit elements; how exact they have to be, the bound alone decides.
No kernel may reach another device: no remote copies, remote signals or barrier semaphores. Data moves between devices by JAX's collectives and lax.ppermute only.
A program may use at most 128 MiB of HBM per device.

v0:
```python
import functools
import math

import jax
import jax.numpy as jnp
from jax import lax
from jax.sharding import Mesh
from jax.sharding import PartitionSpec as P

ROW = ("row_0", "row_1", "row_2")
COL = ("col_0", "col_1")
ROW_COL = ("row_0", "row_1", "row_2", "col_0", "col_1")
COL_ROW = ("col_0", "col_1", "row_0", "row_1", "row_2")


HIGHEST = lax.Precision.HIGHEST


def from_everyone(shard, axis):
    count = lax.axis_size(axis)
    return lax.all_to_all(
        jnp.broadcast_to(shard[None], (count, *shard.shape)), axis, 0, 0, tiled=True
    )


def over_copies(shard, axis):
    return from_everyone(shard, axis).max(axis=0)


def over_copies_2(shard, axis):
    return from_everyone(shard, axis).sum(axis=0)


def packed_total(arrays, axis):
    ends = [0]
    for a in arrays:
        ends.append(ends[-1] + a.size)
    total = over_copies_2(jnp.concatenate([a.ravel() for a in arrays]), axis)
    return tuple((total[b:e].reshape(a.shape) for a, b, e in zip(arrays, ends, ends[1:])))


def split_up(shard, dim, count):
    before, after = (shard.shape[:dim], shard.shape[dim + 1 :])
    return jnp.moveaxis(shard.reshape(*before, count, -1, *after), dim, 0)


def sum_at_owner(shard, axis, dim):
    count = lax.axis_size(axis)
    parts = lax.all_to_all(split_up(shard, dim, count), axis, 0, 0, tiled=True)
    return jnp.sum(parts, axis=0)


def sum_packed(arrays, axis, dims):
    count = lax.axis_size(axis)
    parts = [split_up(a, dim, count) for a, dim in zip(arrays, dims)]
    lines = jnp.concatenate([b.reshape(count, -1) for b in parts], axis=1)
    rows = max(16, -(-lines.shape[1] // 1024) * 8)
    lines = jnp.pad(lines, ((0, 0), (0, rows * 128 - lines.shape[1]))).reshape(-1, 128)
    flat, at, finished = (lax.psum_scatter(lines, axis, tiled=True).reshape(-1), 0, [])
    for b in parts:
        part = b[0]
        finished.append(flat[at : at + part.size].reshape(part.shape))
        at += part.size
    return tuple(finished)


def by_axis(shard, axes):
    return functools.reduce(lax.psum, axes, shard)


def globalize(rotation, offset, local):
    return jnp.einsum("xym,ykm->xkm", rotation, local, precision=HIGHEST) + offset[:, None, :]


def rotate_back(rotation, vector):
    return jnp.einsum("xym,xkm->ykm", rotation, vector, precision=HIGHEST)


def frame_terms(grad_global, local):
    rotation_part = jnp.einsum("xkm,ykm->xym", grad_global, local, precision=HIGHEST)
    return jnp.concatenate([rotation_part, jnp.sum(grad_global, axis=1)[:, None, :]], axis=1)


def output_frame_terms(point_out, offset, cotan_local, grad_rotated):
    rotation_part = jnp.einsum(
        "xkm,ykm->xym", point_out - offset[:, None, :], cotan_local, precision=HIGHEST
    )
    return jnp.concatenate([rotation_part, -jnp.sum(grad_rotated, axis=1)[:, None, :]], axis=1)


def per_device(
    pair_rep,
    bias_weight,
    head_weight,
    queries,
    key_vectors,
    values,
    query_points,
    key_points,
    value_points,
    rotations,
    translations,
    residue_count,
    grad_output,
    grad_points,
    grad_pair,
):
    heads = bias_weight.shape[1]
    width = queries.shape[0] // heads
    qpoints = query_points.shape[1] // heads
    vpoints = value_points.shape[1] // heads
    rows_here = queries.shape[1]
    cols_here = key_vectors.shape[1]
    logit_scale = math.sqrt(1.0 / 3.0)
    point_scale = math.sqrt(2.0 / (9.0 * qpoints))
    inner_scale = 1.0 / math.sqrt(width)
    distance_coef = 0.5 * logit_scale * point_scale * jax.nn.softplus(head_weight)
    row_start = lax.axis_index(ROW) * rows_here
    col_start = lax.axis_index(COL) * cols_here
    rot_rows = lax.dynamic_slice_in_dim(rotations, row_start, rows_here, 2)
    shift_rows = lax.dynamic_slice_in_dim(translations, row_start, rows_here, 1)
    rot_cols = lax.dynamic_slice_in_dim(rotations, col_start, cols_here, 2)
    shift_cols = lax.dynamic_slice_in_dim(translations, col_start, cols_here, 1)
    query_global = globalize(rot_rows, shift_rows, query_points).reshape(
        3, heads, qpoints, rows_here
    )
    key_global = globalize(rot_cols, shift_cols, key_points).reshape(3, heads, qpoints, cols_here)
    value_global = globalize(rot_cols, shift_cols, value_points).reshape(
        3, heads, vpoints, cols_here
    )
    grad_flat = jnp.einsum("xym,ykm->xkm", rot_rows, grad_points, precision=HIGHEST)
    grad_heads = grad_flat.reshape(3, heads, vpoints, rows_here)
    query_heads = queries.reshape(heads, width, rows_here)
    out_heads = grad_output.reshape(heads, width, rows_here)
    key_heads = key_vectors.reshape(heads, width, cols_here)
    value_heads = values.reshape(heads, width, cols_here)
    valid = col_start + lax.iota(jnp.int32, cols_here) < residue_count[0]
    inner = jnp.einsum("hci,hcj->hij", query_heads, key_heads, precision=HIGHEST)
    cross = jnp.einsum("xhpi,xhpj->hij", query_global, key_global, precision=HIGHEST)
    distance = (
        jnp.sum(query_global**2, axis=(0, 2))[:, :, None]
        + jnp.sum(key_global**2, axis=(0, 2))[:, None, :]
        - 2.0 * cross
    )
    bias = jnp.einsum("ijc,ch->hij", pair_rep, bias_weight, preferred_element_type=jnp.float32)
    logits = logit_scale * (inner_scale * inner + bias) - distance_coef[:, None, None] * distance
    logits = jnp.where(valid[None, None, :], logits, jnp.float32(-1000000000.0))
    product = (
        jnp.einsum("hci,hcj->hij", out_heads, value_heads, precision=HIGHEST)
        + jnp.einsum("xhvi,xhvj->hij", grad_heads, value_global, precision=HIGHEST)
        + jnp.einsum("ijc,ihc->hij", pair_rep, grad_pair, preferred_element_type=jnp.float32)
    )
    row_peak = over_copies(jnp.max(logits, axis=2), COL)
    exponent = jnp.exp(logits - row_peak[:, :, None])
    row_total, row_upper, row_points = packed_total(
        (
            jnp.sum(exponent, axis=2),
            jnp.sum(exponent * product, axis=2),
            jnp.einsum("hij,xhvj->xhvi", exponent, value_global, precision=HIGHEST),
        ),
        COL,
    )
    attention = exponent / row_total[:, :, None]
    delta = row_upper / row_total
    point_out = (row_points / row_total[None, :, None, :]).reshape(3, heads * vpoints, rows_here)
    logit_grad = attention * (product - delta[:, :, None])
    grad_rounded = logit_grad.astype(jnp.bfloat16)
    attn_rounded = attention.astype(jnp.bfloat16)
    pair_grad = (
        logit_scale
        * jnp.einsum("hij,ch->ijc", grad_rounded, bias_weight, preferred_element_type=jnp.float32)
        + jnp.einsum("hij,ihc->ijc", attn_rounded, grad_pair, preferred_element_type=jnp.float32)
    ).astype(jnp.bfloat16)
    weight_part = logit_scale * jnp.einsum(
        "ijc,hij->ch", pair_rep, grad_rounded, preferred_element_type=jnp.float32
    )
    distance_part = jnp.sum(logit_grad * distance, axis=(1, 2))
    query_part = (
        logit_scale
        * inner_scale
        * jnp.einsum("hij,hcj->hci", logit_grad, key_heads, precision=HIGHEST)
    )
    row_sum = jnp.sum(logit_grad, axis=2)
    qpoint_part = (
        -2.0
        * distance_coef[None, :, None, None]
        * (
            query_global * row_sum[None, :, None, :]
            - jnp.einsum("hij,xhpj->xhpi", logit_grad, key_global, precision=HIGHEST)
        )
    )
    query_grad, qpoint_sum = (
        sum_at_owner(query_part.reshape(heads * width, rows_here), COL, 1),
        sum_at_owner(qpoint_part.reshape(3, heads * qpoints, rows_here), COL, 2),
    )
    share = rows_here // lax.axis_size(COL)
    share_start = lax.axis_index(COL) * share
    own_start = row_start + share_start
    rot_own = lax.dynamic_slice_in_dim(rotations, own_start, share, 2)
    shift_own = lax.dynamic_slice_in_dim(translations, own_start, share, 1)
    local_own = lax.dynamic_slice_in_dim(query_points, share_start, share, 2)
    cotan_own = lax.dynamic_slice_in_dim(grad_points, share_start, share, 2)
    out_own = lax.dynamic_slice_in_dim(point_out, share_start, share, 2)
    rotated_own = lax.dynamic_slice_in_dim(grad_flat, share_start, share, 2)
    query_point_grad = rotate_back(rot_own, qpoint_sum)
    query_frame_grad = frame_terms(qpoint_sum, local_own) + output_frame_terms(
        out_own, shift_own, cotan_own, rotated_own
    )
    key_part = (
        logit_scale
        * inner_scale
        * jnp.einsum("hij,hci->hcj", logit_grad, query_heads, precision=HIGHEST)
    )
    value_part = jnp.einsum("hij,hci->hcj", attention, out_heads, precision=HIGHEST)
    col_sum = jnp.sum(logit_grad, axis=1)
    kpoint_part = (
        2.0
        * distance_coef[None, :, None, None]
        * (
            jnp.einsum("hij,xhpi->xhpj", logit_grad, query_global, precision=HIGHEST)
            - key_global * col_sum[None, :, None, :]
        )
    ).reshape(3, heads * qpoints, cols_here)
    vpoint_part = jnp.einsum("hij,xhvi->xhvj", attention, grad_heads, precision=HIGHEST).reshape(
        3, heads * vpoints, cols_here
    )
    key_flat = key_part.reshape(heads * width, cols_here)
    value_flat = value_part.reshape(heads * width, cols_here)
    key_grad, value_grad, kpoint_sum, vpoint_sum = sum_packed(
        (key_flat, value_flat, kpoint_part, vpoint_part), ROW, (1, 1, 2, 2)
    )
    kshare = cols_here // lax.axis_size(ROW)
    kshare_start = lax.axis_index(ROW) * kshare
    rot_keys = lax.dynamic_slice_in_dim(rotations, col_start + kshare_start, kshare, 2)
    klocal_own = lax.dynamic_slice_in_dim(key_points, kshare_start, kshare, 2)
    vlocal_own = lax.dynamic_slice_in_dim(value_points, kshare_start, kshare, 2)
    key_point_grad = rotate_back(rot_keys, kpoint_sum)
    value_point_grad = rotate_back(rot_keys, vpoint_sum)
    key_frame_grad = frame_terms(kpoint_sum, klocal_own) + frame_terms(vpoint_sum, vlocal_own)
    weight_total, distance_total = (by_axis(weight_part, ROW_COL), by_axis(distance_part, ROW_COL))
    head_weight_grad = (
        distance_total * (-0.5 * logit_scale * point_scale) * jax.nn.sigmoid(head_weight)
    )
    return (
        pair_grad,
        query_grad,
        query_point_grad,
        query_frame_grad,
        key_grad,
        value_grad,
        key_point_grad,
        value_point_grad,
        key_frame_grad,
        weight_total,
        head_weight_grad,
    )


def solution(mesh):
    finer = Mesh(mesh.devices.reshape(4, 4, 2, 4, 2), ("row_0", "row_1", "row_2", "col_0", "col_1"))
    in_specs = (
        P(ROW, COL, None),
        P(),
        P(),
        P(None, ROW),
        P(None, COL),
        P(None, COL),
        P(None, None, ROW),
        P(None, None, COL),
        P(None, None, COL),
        P(),
        P(),
        P(),
        P(None, ROW),
        P(None, None, ROW),
        P(ROW, None, None),
    )
    out_specs = (
        P(ROW, COL, None),
        P(None, ROW_COL),
        P(None, None, ROW_COL),
        P(None, None, ROW_COL),
        P(None, COL_ROW),
        P(None, COL_ROW),
        P(None, None, COL_ROW),
        P(None, None, COL_ROW),
        P(None, None, COL_ROW),
        P(),
        P(),
    )
    return jax.shard_map(
        per_device, mesh=finer, in_specs=in_specs, out_specs=out_specs, check_vma=False
    )
```

profile of v0, /device:TPU:2, one launch (start us, length us, event | category | flops | bytes accessed | tf_op | source)
XLA Modules:
  0.0 416.2 jit_solution(17823779164322360788)
XLA Ops:
  17.1 2.0 multiply_reduce_fusion.2
  19.6 3.5 fusion.44
  26.2 11.5 %all-to-all-start = ((f32[8,1,768]{2,1,0:T(1,128)}), f32[8,1,768]{2,1,0:T(1,128)S(1)}, u32[]{:S(2)}, u32[]{:S(2)}) async-start(f32[8,1,768]{2,1,0:T(1,128)} %reshape.192), calls=%async_computation | async-start | bytes 49152 | tf_op jit(solution)/shard_map/all_to_all | solution.py:21
  38.6 2.6 fusion.7
  42.5 3.4 fusion.31
  50.0 3.1 fusion.27
  54.5 9.6 %all-to-all-start.1 = ((f32[8,1,19968]{2,1,0:T(1,128)}), f32[8,1,19968]{2,1,0:T(1,128)S(1)}, u32[]{:S(2)}, u32[]{:S(2)}) async-start(f32[8,1,19968]{2,1,0:T(1,128)} %broadcast_in_dim.25), calls=%async_computation.1 | async-start | bytes 1277952 | tf_op jit(solution)/shard_map/all_to_all | solution.py:21
  69.1 12.9 %all-to-all-done.1 = f32[8,1,19968]{2,1,0:T(1,128)S(1)} async-done(((f32[8,1,19968]{2,1,0:T(1,128)}), f32[8,1,19968]{2,1,0:T(1,128)S(1)}, u32[]{:S(2)}, u32[]{:S(2)}) %all-to-all-start.1) | async-done | bytes 639008 | tf_op jit(solution)/shard_map/all_to_all | solution.py:21
  82.8 2.6 multiply_reduce_fusion
  85.9 1.4 fusion.13
  90.3 4.5 %fusion.23 = f32[64,256,128]{2,1,0:T(8,128)} fusion(bf16[12,64,256]{2,1,0:T(8,128)(2,1)S(1)} %convert_element_type.11, bf16[128,12]{0,1:T(8,128)(2,1)S(1)} %copy-done.31), kind=kOutput, calls=%fused_computation.54 | convolution fusion | flops 50331648 | bytes 8784896 | tf_op jit(solution)/shard_map/hij,ch->ijc/dot_general | solution.py:171
  99.1 3.9 all-to-all-start.3
  112.1 4.7 %reshape_reshape.23 = f32[3,96,32,8]{3,2,1,0:T(8,128)} reshape(f32[3,12,8,256]{3,2,1,0:T(8,128)} %copy.473) | data formatting | bytes 589824 | tf_op jit(solution)/shard_map/reshape;reshape | solution.py:44
  116.8 3.1 copy.474
  121.5 12.9 %all-reduce.4 = (f32[128,12]{0,1:T(8,128)S(1)}, f32[12]{0:T(128)S(1)}) all-reduce(f32[128,12]{0,1:T(8,128)S(1)} %copy-done.29, f32[12]{0:T(128)S(1)} %copy-done.33), channel_id=1, replica_groups=mesh['row_0'=4,'row_1'=4,'row_2'=2,'col_0'=4,'col_1'=2] {'row_0'}, use_global_device_ids=true, to_apply=%region_18.19 | all-reduce | flops 1548 | bytes 12384 | tf_op jit(solution)/shard_map/psum | solution.py:68
  134.4 11.0 %all-reduce.3 = (f32[128,12]{0,1:T(8,128)S(1)}, f32[12]{0:T(128)S(1)}) all-reduce(f32[128,12]{0,1:T(8,128)S(1)} %get-tuple-element.99, f32[12]{0:T(128)S(1)} %get-tuple-element.100), channel_id=1, replica_groups=mesh['row_0'=4,'row_1'=4,'row_2'=2,'col_0'=4,'col_1'=2] {'row_1'}, use_global_device_ids=true, to_apply=%region_19.20 | all-reduce | flops 1548 | bytes 12384 | tf_op jit(solution)/shard_map/psum | solution.py:68
  145.4 2.5 all-reduce.6
  147.9 8.8 %all-reduce.2 = (f32[128,12]{0,1:T(8,128)S(1)}, f32[12]{0:T(128)S(1)}) all-reduce(f32[128,12]{0,1:T(8,128)S(1)} %get-tuple-element.103, f32[12]{0:T(128)S(1)} %get-tuple-element.104), channel_id=1, replica_groups=mesh['row_0'=4,'row_1'=4,'row_2'=2,'col_0'=4,'col_1'=2] {'col_0'}, use_global_device_ids=true, to_apply=%region_21.22 | all-reduce | flops 1548 | bytes 12384 | tf_op jit(solution)/shard_map/psum | solution.py:68
  156.7 9.6 %all-reduce.5 = (f32[128,12]{0,1:T(8,128)}, f32[12]{0:T(128)S(1)}) all-reduce(f32[128,12]{0,1:T(8,128)S(1)} %get-tuple-element.95, f32[12]{0:T(128)S(1)} %get-tuple-element.96), channel_id=1, replica_groups=mesh['row_0'=4,'row_1'=4,'row_2'=2,'col_0'=4,'col_1'=2] {'col_1'}, use_global_device_ids=true, to_apply=%region_22.23 | all-reduce | flops 1548 | bytes 12384 | tf_op jit(solution)/shard_map/psum | solution.py:68
  166.3 7.5 %add_convert_fusion = bf16[64,256,128]{2,1,0:T(8,128)(2,1)} fusion(f32[64,256,128]{2,1,0:T(8,128)} %fusion.23, bf16[12,64,256]{2,1,0:T(8,128)(2,1)S(1)} %get-tuple-element.110, bf16[64,12,128]{2,0,1:T(8,128)(2,1)S(1)} %copy-done.4), kind=kOutput, calls=%fused_computation | convolution fusion | flops 56623104 | bytes 13172736 | tf_op jit(solution)/shard_map/hij,ihc->ijc/dot_general | solution.py:172
  176.4 9.3 %all-to-all-start.2 = ((f32[8,192,8]{1,2,0:T(8,128)}), f32[8,192,8]{1,2,0:T(8,128)S(1)}, u32[]{:S(2)}, u32[]{:S(2)}) async-start(f32[8,192,8]{1,2,0:T(8,128)} %bitcast.21), calls=%async_computation.2 | async-start | bytes 131072 | tf_op jit(solution)/shard_map/all_to_all | solution.py:49
  185.8 1.5 reduce.8
  189.3 5.3 %all-to-all-done.2 = f32[8,192,8]{1,2,0:T(8,128)S(1)} async-done(((f32[8,192,8]{1,2,0:T(8,128)}), f32[8,192,8]{1,2,0:T(8,128)S(1)}, u32[]{:S(2)}, u32[]{:S(2)}) %all-to-all-start.2) | async-done | bytes 49184 | tf_op jit(solution)/shard_map/all_to_all | solution.py:49
  195.2 205.7 %all-reduce.9.cloned.1.call-done = f32[1792,128]{1,0:T(8,128)} async-done(((f32[1792,128]{1,0:T(8,128)}), f32[1792,128]{1,0:T(8,128)}) %all-reduce.9.cloned.1.call-update) | async-done | bytes 917520
  (208 shorter events, 57.0 us)
Async XLA Ops:
  7.2 16.8 %copy-start = (f32[192,256]{1,0:T(8,128)S(1)}, f32[192,256]{1,0:T(8,128)}, u32[]{:S(2)}) copy-start(f32[192,256]{1,0:T(8,128)} %param.19) | copy-start | bytes 589828
  7.2 12.4 %copy-start.30 = (bf16[128,12]{0,1:T(8,128)(2,1)S(1)}, bf16[128,12]{0,1:T(8,128)(2,1)}, u32[]{:S(2)}) copy-start(bf16[128,12]{0,1:T(8,128)(2,1)} %param.16) | copy-start | bytes 9220
  13.6 10.5 %copy-start.7 = (f32[192,64]{1,0:T(8,128)}, f32[192,64]{1,0:T(8,128)S(1)}, u32[]{:S(2)}) copy-start(f32[192,64]{1,0:T(8,128)S(1)} %copy.420) | copy-start | bytes 147460
  13.9 9.2 %copy-start.25 = (f32[3,256]{0,1:T(8,128)}, f32[3,256]{0,1:T(8,128)S(1)}, u32[]{:S(2)}) copy-start(f32[3,256]{0,1:T(8,128)S(1)} %copy.428) | copy-start | bytes 9220
  19.6 18.1 %copy-start.17 = (f32[3,96,64]{1,2,0:T(8,128)S(1)}, f32[3,96,64]{1,2,0:T(8,128)}, u32[]{:S(2)}) copy-start(f32[3,96,64]{1,2,0:T(8,128)} %param.28) | copy-start | bytes 221188
  19.6 18.8 %copy-start.21 = (f32[3,96,256]{2,1,0:T(8,128)S(1)}, f32[3,96,256]{2,1,0:T(8,128)}, u32[]{:S(2)}) copy-start(f32[3,96,256]{2,1,0:T(8,128)} %param.23) | copy-start | bytes 884740
  23.1 15.5 %copy-start.26 = (f32[3,256]{0,1:T(8,128)S(1)}, f32[3,256]{0,1:T(8,128)}, u32[]{:S(2)}) copy-start(f32[3,256]{0,1:T(8,128)} %copy-done.25) | copy-start | bytes 9220
  23.1 19.4 %copy-start.3 = (bf16[64,12,128]{2,0,1:T(8,128)(2,1)S(1)}, bf16[64,12,128]{2,0,1:T(8,128)(2,1)}, u32[]{:S(2)}) copy-start(bf16[64,12,128]{2,0,1:T(8,128)(2,1)} %param.29) | copy-start | bytes 589828
  26.2 21.5 %all-to-all-start = ((f32[8,1,768]{2,1,0:T(1,128)}), f32[8,1,768]{2,1,0:T(1,128)S(1)}, u32[]{:S(2)}, u32[]{:S(2)}) async-start(f32[8,1,768]{2,1,0:T(1,128)} %reshape.192), calls=%async_computation | async-start | bytes 49152 | tf_op jit(solution)/shard_map/all_to_all | solution.py:21
  38.4 7.5 %copy-start.13 = (f32[3,96,64]{2,1,0:T(8,128)}, f32[3,96,64]{2,1,0:T(8,128)S(1)}, u32[]{:S(2)}) copy-start(f32[3,96,64]{2,1,0:T(8,128)S(1)} %copy.435) | copy-start | bytes 221188
  46.7 18.1 %copy-start.37 = (u32[256]{0:T(256)S(1)}, u32[256]{0:T(256)}, u32[]{:S(2)}) copy-start(u32[256]{0:T(256)} %constant.67) | copy-start | bytes 3076
  47.7 34.8 %copy-start.19 = (f32[192,64]{1,0:T(8,128)}, f32[192,64]{1,0:T(8,128)S(1)}, u32[]{:S(2)}) copy-start(f32[192,64]{1,0:T(8,128)S(1)} %copy.433) | copy-start | bytes 147460
  49.0 33.5 %copy-start.23 = (f32[12,64]{1,0:T(8,128)}, f32[12,64]{1,0:T(8,128)S(1)}, u32[]{:S(2)}) copy-start(f32[12,64]{1,0:T(8,128)S(1)} %reduce_max.19) | copy-start | bytes 9220
  53.2 32.2 %copy-start.8 = (f32[192,64]{1,0:T(8,128)S(1)}, f32[192,64]{1,0:T(8,128)}, u32[]{:S(2)}) copy-start(f32[192,64]{1,0:T(8,128)} %copy-done.7) | copy-start | bytes 147460
  54.5 27.6 %all-to-all-start.1 = ((f32[8,1,19968]{2,1,0:T(1,128)}), f32[8,1,19968]{2,1,0:T(1,128)S(1)}, u32[]{:S(2)}, u32[]{:S(2)}) async-start(f32[8,1,19968]{2,1,0:T(1,128)} %broadcast_in_dim.25), calls=%async_computation.1 | async-start | bytes 1277952 | tf_op jit(solution)/shard_map/all_to_all | solution.py:21
  99.1 77.3 %all-to-all-start.3 = ((f32[8,1,1152]{2,1,0:T(1,128)}), f32[8,1,1152]{2,1,0:T(1,128)}, u32[]{:S(2)}, u32[]{:S(2)}) async-start(f32[8,1,1152]{2,1,0:T(1,128)} %reshape.194), calls=%async_computation.3 | async-start | bytes 73728 | tf_op jit(solution)/shard_map/all_to_all | solution.py:49
  103.0 297.8 %all-reduce.9.cloned.1.call-start = ((), (), s32[]{:S(2)}) async-start(), calls=%async_computation.4 | async-start | bytes 1835008
  119.9 46.4 %copy-start.4 = (bf16[64,12,128]{2,0,1:T(8,128)(2,1)S(1)}, bf16[64,12,128]{2,0,1:T(8,128)(2,1)}, u32[]{:S(2)}) copy-start(bf16[64,12,128]{2,0,1:T(8,128)(2,1)} %param.29) | copy-start | bytes 589828
  166.3 7.5 %copy-start.27 = (f32[3,96,8]{1,0,2:T(4,128)S(1)}, f32[3,96,8]{1,0,2:T(4,128)}, u32[]{:S(2)}) copy-start(f32[3,96,8]{1,0,2:T(4,128)} %copy.460) | copy-start | bytes 27652
  166.3 8.4 %copy-start.36 = (f32[12]{0:T(128)S(1)}, f32[12]{0:T(128)}, u32[]{:S(2)}) copy-start(f32[12]{0:T(128)} %param.17) | copy-start | bytes 148
  166.3 9.1 %copy-start.18 = (f32[12,16,64]{2,1,0:T(8,128)S(1)}, f32[12,16,64]{2,1,0:T(8,128)}, u32[]{:S(2)}) copy-start(f32[12,16,64]{2,1,0:T(8,128)} %fusion.13) | copy-start | bytes 147460
  166.3 21.2 %copy-start.28 = (f32[3,3,8]{0,1,2:T(4,128)S(1)}, f32[3,3,8]{0,1,2:T(4,128)}, u32[]{:S(2)}) copy-start(f32[3,3,8]{0,1,2:T(4,128)} %copy.508) | copy-start | bytes 868
  166.3 242.5 %copy-start.32 = (f32[3,1,8]{2,1,0:T(1,128)S(1)}, f32[3,1,8]{2,1,0:T(1,128)}, u32[]{:S(2)}) copy-start(f32[3,1,8]{2,1,0:T(1,128)} %copy.463) | copy-start | bytes 292
  176.4 18.1 %all-to-all-start.2 = ((f32[8,192,8]{1,2,0:T(8,128)}), f32[8,192,8]{1,2,0:T(8,128)S(1)}, u32[]{:S(2)}, u32[]{:S(2)}) async-start(f32[8,192,8]{1,2,0:T(8,128)} %bitcast.21), calls=%async_computation.2 | async-start | bytes 131072 | tf_op jit(solution)/shard_map/all_to_all | solution.py:49
  (19 other events, 72.9 us)
Sparse Core Ops, SparseCore 0:
  121.6 279.2 all-reduce.8
where the time goes:
time: 418 us; the launch traced here: 416 us
  waiting for transfers between devices  224 us (54%)
  local copies, waits for them, and re-layouts  45.2 us (11%)
  blocking collectives  44.8 us (11%)
  matrix products  42.1 us (10%)
  starting transfers between devices  34.6 us (8%)
  between operations  16.3 us (4%)
  other arithmetic  9.25 us (2%)
    unnamed x2, waiting for transfers between devices  206 us
    psum x5, blocking collectives, by_axis(): return functools.reduce(lax.psum, axes, shard)  44.8 us
    all_to_all x2, starting transfers between devices, from_everyone(): lax.all_to_all(jnp.broadcast_to(shard[None], (count, *shard.shape)), axis...  21.1 us
    all_to_all x2, starting transfers between devices, sum_at_owner(): parts = lax.all_to_all(split_up(shard, dim, count), axis, 0, 0, tiled=True)  13.3 us
    all_to_all x2, waiting for transfers between devices, from_everyone(): lax.all_to_all(jnp.broadcast_to(shard[None], (count, *shard.shape)), axis...  12.9 us
    unnamed x96, local copies, waits for them, and re-layouts  11.8 us
    another operation x6, local copies, waits for them, and re-layouts, split_up(): return jnp.moveaxis(shard.reshape(*before, count, -1, *after), dim, 0)  8.47 us
  transfers between devices with their start and end apart: 5, of which 3 were waited for; matrix products, arithmetic and copies ran while one was open for 11% of the time, Pallas kernels for 0%

commit v1 on v0

v1 whole, which is shorter than its diff:
```python
import functools
import math

import jax
import jax.numpy as jnp
from jax import lax
from jax.experimental import pallas as pl
from jax.experimental.pallas import tpu as pltpu
from jax.sharding import Mesh
from jax.sharding import PartitionSpec as P

ROW = ("row_0", "row_1", "row_2")
COL = ("col_0", "col_1")
ROW_COL = ROW + COL
COL_ROW = COL + ROW
CHIPS = ("row_0", "row_1")

H, C, PQ, PV, CZ = 12, 16, 4, 8, 128
IQ, JK = 64, 256
NCOL, NROW, NCHIP = 8, 32, 16
WL = math.sqrt(1.0 / 3.0)
WC = math.sqrt(2.0 / (9.0 * PQ))
WS = 1.0 / math.sqrt(C)
MASKED = -1000000000.0

KEY0, VAL0, KPT0, VPT0, KEND = 0, 192, 384, 528, 816
QRY0, QPT0, OPT0, QEND = 0, 192, 336, 624
KW, QW = 1024, 640
QB = 8

F32, BF16 = jnp.float32, jnp.bfloat16
VMEM_SPEC = pl.BlockSpec(memory_space=pltpu.VMEM)
SMEM_SPEC = pl.BlockSpec(memory_space=pltpu.SMEM)
TN = (((0,), (0,)), ((), ()))
NT = (((1,), (1,)), ((), ()))
NN = (((1,), (0,)), ((), ()))


def mm(a, b, dims):
    return lax.dot_general(a, b, dims, preferred_element_type=F32)


def split2(x):
    hi = x.astype(BF16)
    return hi, (x - hi.astype(F32)).astype(BF16)


def split3(x):
    hi = x.astype(BF16)
    rest = x - hi.astype(F32)
    mid = rest.astype(BF16)
    return hi, mid, (rest - mid.astype(F32)).astype(BF16)


def row_index():
    return (lax.axis_index("row_0") * 4 + lax.axis_index("row_1")) * 2 + lax.axis_index("row_2")


def col_index():
    return lax.axis_index("col_0") * 2 + lax.axis_index("col_1")


def soft(hw_ref, h, lanes):
    w = jnp.full((1, lanes), hw_ref[h], F32)
    return jnp.maximum(w, 0.0) + jnp.log1p(jnp.exp(-jnp.abs(w)))


def coef_row(hw_ref, h, lanes):
    return (0.5 * WL * WC) * soft(hw_ref, h, lanes)


def rotate(rot, shift, local):
    out = []
    for x in range(3):
        g = rot[x][0] * local[0] + rot[x][1] * local[1] + rot[x][2] * local[2]
        out.append(g if shift is None else g + shift[x])
    return out


def col_frames(rot_ref, tr_ref):
    start = pl.multiple_of(col_index() * JK, JK)
    rot = [[rot_ref[x, y : y + 1, pl.ds(start, JK)] for y in range(3)] for x in range(3)]
    tr = [tr_ref[x : x + 1, pl.ds(start, JK)] for x in range(3)]
    return rot, tr


def lanes_at(block, offset, count):
    return pltpu.roll(block, lax.rem(128 - offset, 128), block.ndim - 1)[..., :count]


def row_frames(rot_ref, tr_ref, offset, count):
    at = row_index() * IQ + offset
    base = pl.multiple_of(lax.div(at, 128) * 128, 128)
    off = lax.rem(at, 128)
    rot = []
    for x in range(3):
        block = lanes_at(
            jnp.concatenate([rot_ref[x, :, pl.ds(base, 128)], jnp.zeros((5, 128), F32)], 0),
            off,
            count,
        )
        rot.append([block[y : y + 1] for y in range(3)])
    block = lanes_at(
        jnp.concatenate([tr_ref[:, pl.ds(base, 128)], jnp.zeros((5, 128), F32)], 0), off, count
    )
    return rot, [block[x : x + 1] for x in range(3)]


def logits_kernel(
    hw_ref, rc_ref, pair_ref, gp_ref, bw_ref, q_ref, k_ref, v_ref, qp_ref, kp_ref, vp_ref,
    rot_ref, tr_ref, go_ref, gpt_ref,
    e_ref, p_ref, st_ref, qg_ref, kg_ref, vg_ref, gg_ref,
    bp_ref, wt_ref,
):
    step = pl.program_id(0)

    @pl.when(step == 0)
    def _():
        wide = jnp.concatenate([bw_ref[...].astype(F32), jnp.zeros((CZ, 128 - H), F32)], 1)
        wt_ref[...] = wide.T[:16].astype(BF16)

    wt = wt_ref[...]
    for n in range(QB):
        lhs = jnp.concatenate([wt, gp_ref[n]], 0)
        res = mm(lhs, pair_ref[n], NT)
        for half in range(2):
            bp_ref[half, pl.ds(step * QB + n, 16 + H, stride=IQ), :] = res[
                :, half * 128 : half * 128 + 128
            ]

    @pl.when(step == IQ // QB - 1)
    def _():
        crot, ctr = col_frames(rot_ref, tr_ref)
        rrot, rtr = row_frames(rot_ref, tr_ref, 0, IQ)
        kg = rotate(crot, ctr, [kp_ref[y] for y in range(3)])
        vg = rotate(crot, ctr, [vp_ref[y] for y in range(3)])
        qg = rotate(rrot, rtr, [qp_ref[y] for y in range(3)])
        gg = rotate(rrot, None, [gpt_ref[y] for y in range(3)])
        for x in range(3):
            kg_ref[x], vg_ref[x], qg_ref[x], gg_ref[x] = kg[x], vg[x], qg[x], gg[x]
        real = (
            lax.broadcasted_iota(jnp.int32, (IQ, JK), 1) + col_index() * JK < rc_ref[0]
        )
        lane = lax.broadcasted_iota(jnp.int32, (IQ, 128), 1)
        stats = [jnp.zeros((IQ, 128), F32), jnp.zeros((IQ, 128), F32)]
        row4q = lax.broadcasted_iota(jnp.int32, (4, IQ), 0)
        row4k = lax.broadcasted_iota(jnp.int32, (4, JK), 0)
        for h in range(H):
            cf = coef_row(hw_ref, h, IQ)
            qgh = [qg_ref[x, 4 * h : 4 * h + 4] for x in range(3)]
            kgh = [kg_ref[x, 4 * h : 4 * h + 4] for x in range(3)]
            qn = sum(jnp.sum(t * t, axis=0, keepdims=True) for t in qgh)
            kn = sum(jnp.sum(t * t, axis=0, keepdims=True) for t in kgh)
            qtail = jnp.where(row4q == 0, -cf, jnp.where(row4q == 1, -cf * qn, 0.0))
            ktail = jnp.where(row4k == 0, kn, jnp.where(row4k == 1, 1.0, 0.0))
            qf = jnp.concatenate(
                [q_ref[C * h : C * h + C] * (WL * WS)] + [2.0 * cf * t for t in qgh] + [qtail], 0
            )
            kf = jnp.concatenate([k_ref[C * h : C * h + C]] + kgh + [ktail], 0)
            a1, a2, a3 = split3(qf)
            b1, b2, b3 = split3(kf)
            core = mm(
                jnp.concatenate([a1, a1, a2, a1, a2, a3], 0),
                jnp.concatenate([b1, b2, b1, b3, b2, b1], 0),
                TN,
            )
            gf = jnp.concatenate(
                [go_ref[C * h : C * h + C]] + [gg_ref[x, 8 * h : 8 * h + 8] for x in range(3)]
                + [jnp.zeros((8, IQ), F32)], 0
            )
            vf = jnp.concatenate(
                [v_ref[C * h : C * h + C]] + [vg_ref[x, 8 * h : 8 * h + 8] for x in range(3)]
                + [jnp.zeros((8, JK), F32)], 0
            )
            g1, g2 = split2(gf)
            v1, v2 = split2(vf)
            prod = mm(
                jnp.concatenate([g1, g1, g2], 0), jnp.concatenate([v1, v2, v1], 0), TN
            )

            def planes(base):
                return jnp.concatenate(
                    [bp_ref[half, base * IQ : base * IQ + IQ, :] for half in range(2)], 1
                )

            logit = jnp.where(real, core + WL * planes(h), MASKED)
            prod = prod + planes(16 + h)
            peak = jnp.max(logit, axis=1, keepdims=True)
            e = jnp.exp(logit - peak)
            e_ref[h] = e
            p_ref[h] = prod
            total = jnp.sum(e, axis=1, keepdims=True)
            upper = jnp.sum(e * prod, axis=1, keepdims=True)
            g, r = divmod(h, 6)
            acc = jnp.where(lane == r, peak, stats[g])
            acc = jnp.where(lane == 8 + r, total, acc)
            stats[g] = jnp.where(lane == 16 + r, upper, acc)
        packed = jnp.concatenate(stats, 0).T[:24]
        for c in range(NCOL):
            st_ref[c] = packed


def grads_kernel(
    hw_ref, e_ref, p_ref, own_ref, all_ref, q_ref, k_ref, go_ref, qg_ref, kg_ref, vg_ref, gg_ref,
    pair_ref,
    d_ref, key_ref, qry_ref,
    da_ref, kp_ref, qp_ref, w_ref, hs_ref,
):
    step = pl.program_id(0)

    @pl.when(step == 0)
    def _():
        peaks = all_ref[:, 0:8]
        top = jnp.max(peaks, axis=0)
        grow = jnp.exp(peaks - top[None])
        total = jnp.sum(all_ref[:, 8:16] * grow, axis=0)
        upper = jnp.sum(all_ref[:, 16:24] * grow, axis=0)
        scale = jnp.exp(own_ref[0, 0:8] - top) / total
        delta = upper / total
        cols = jnp.concatenate([scale, delta, jnp.zeros((112, 128), F32)], 0).T
        w_ref[...] = jnp.zeros_like(w_ref)
        for half in range(2):
            da_ref[half, H * IQ : 16 * IQ, :] = jnp.zeros((4 * IQ, 128), F32)
            da_ref[half, 28 * IQ : 32 * IQ, :] = jnp.zeros((4 * IQ, 128), F32)
        row4q = lax.broadcasted_iota(jnp.int32, (4, IQ), 0)
        row4k = lax.broadcasted_iota(jnp.int32, (4, JK), 0)
        lane = lax.broadcasted_iota(jnp.int32, (8, 128), 1)
        hs = jnp.zeros((8, 128), F32)
        for h in range(H):
            g, r = divmod(h, 6)
            sc = cols[IQ * g : IQ * g + IQ, r : r + 1]
            dl = cols[IQ * g : IQ * g + IQ, 8 + r : 9 + r]
            a = e_ref[h] * sc
            d = a * (p_ref[h] - dl)
            for half in range(2):
                piece = slice(half * 128, half * 128 + 128)
                da_ref[half, h * IQ : h * IQ + IQ, :] = d[:, piece]
                da_ref[half, (16 + h) * IQ : (17 + h) * IQ, :] = a[:, piece]
            d1, d2 = split2(d)
            a1, a2 = split2(a)
            cfq = coef_row(hw_ref, h, IQ)
            cfk = coef_row(hw_ref, h, JK)
            qgh = [qg_ref[x, 4 * h : 4 * h + 4] for x in range(3)]
            kgh = [kg_ref[x, 4 * h : 4 * h + 4] for x in range(3)]
            qf = jnp.concatenate(
                [q_ref[C * h : C * h + C] * (WL * WS)] + qgh + [jnp.where(row4q == 0, 1.0, 0.0)], 0
            )
            kf = jnp.concatenate(
                [k_ref[C * h : C * h + C] * (WL * WS)] + kgh + [jnp.where(row4k == 0, 1.0, 0.0)], 0
            )
            gf = jnp.concatenate(
                [go_ref[C * h : C * h + C]] + [gg_ref[x, 8 * h : 8 * h + 8] for x in range(3)], 0
            )
            vf = jnp.concatenate([vg_ref[x, 8 * h : 8 * h + 8] for x in range(3)], 0)

            def three(left, n, right1, right2, dims):
                hi, lo = split2(left)
                both = mm(jnp.concatenate([hi, lo], 0), right1, dims)
                return both[:n] + both[n:] + mm(hi, right2, dims)

            kside = three(qf, 32, d1, d2, NN)
            vside = three(gf, 40, a1, a2, NN)
            qside = three(kf, 32, d1, d2, NT)
            oside = three(vf, 24, a1, a2, NT)
            csum, rsum = kside[28:29], qside[28:29]
            kp_ref[KEY0 + C * h : KEY0 + C * h + C] = kside[0:16]
            kp_ref[VAL0 + C * h : VAL0 + C * h + C] = vside[0:16]
            qp_ref[QRY0 + C * h : QRY0 + C * h + C] = qside[0:16]
            tk = jnp.zeros((1, JK), F32)
            tq = jnp.zeros((1, IQ), F32)
            for x in range(3):
                kq = kside[16 + 4 * x : 20 + 4 * x]
                qk = qside[16 + 4 * x : 20 + 4 * x]
                kp_ref[KPT0 + 48 * x + 4 * h : KPT0 + 48 * x + 4 * h + 4] = (2.0 * cfk) * (
                    kq - kgh[x] * csum
                )
                qp_ref[QPT0 + 48 * x + 4 * h : QPT0 + 48 * x + 4 * h + 4] = (-2.0 * cfq) * (
                    qgh[x] * rsum - qk
                )
                kp_ref[VPT0 + 96 * x + 8 * h : VPT0 + 96 * x + 8 * h + 8] = vside[
                    16 + 8 * x : 24 + 8 * x
                ]
                qp_ref[OPT0 + 96 * x + 8 * h : OPT0 + 96 * x + 8 * h + 8] = oside[
                    8 * x : 8 * x + 8
                ]
                tk = tk + jnp.sum(kgh[x] * (kgh[x] * csum - 2.0 * kq), axis=0, keepdims=True)
                tq = tq + jnp.sum(qgh[x] * qgh[x], axis=0, keepdims=True)
            part = jnp.sum(tk, axis=1, keepdims=True) + jnp.sum(tq * rsum, axis=1, keepdims=True)
            hs = jnp.where(lane == 48 + h, part, hs)
        hs_ref[...] = hs

    dlogs = []
    for n in range(QB):
        rows = jnp.concatenate(
            [da_ref[half, pl.ds(step * QB + n, 32, stride=IQ), :] for half in range(2)], 1
        ).astype(BF16)
        d_ref[n] = rows
        dlogs.append(rows[:16])
    w_ref[...] += mm(
        jnp.concatenate(dlogs, 1), pair_ref[...].reshape(QB * JK, CZ), NN
    )

    @pl.when(step == IQ // QB - 1)
    def _():
        core = lax.axis_index("row_2")
        w0 = w_ref[0:8]
        w1 = w_ref[8:16]
        lane = lax.broadcasted_iota(jnp.int32, (8, 128), 1)
        sub = lax.broadcasted_iota(jnp.int32, (8, 128), 0)
        fold = jnp.where(sub < 4, pltpu.roll(w1, 64, 1), pltpu.roll(w1, 4, 0))
        extra = jnp.where(lane < 64, hs_ref[...], fold)
        keys = [
            [kp_ref[128 * t : 128 * t + 128, 128 * b : 128 * b + 128].T for t in range(7)]
            for b in range(2)
        ]
        for b in range(2):
            for s in range(16):
                zone, parity = divmod(16 * b + s, 2)
                spot = core if parity else 1 - core
                spot = jnp.abs(parity - core)
                for t in range(6):
                    key_ref[spot, zone, :, 128 * t : 128 * t + 128] = keys[b][t][8 * s : 8 * s + 8]
                key_ref[spot, zone, :, 768:896] = jnp.where(
                    lane < 48, keys[b][6][8 * s : 8 * s + 8], extra
                )
                key_ref[spot, zone, :, 896:1024] = w0
        for t in range(5):
            block = qp_ref[128 * t : 128 * t + 128]
            turned = jnp.concatenate([block, jnp.zeros((128, 64), F32)], 1).T
            for c in range(NCOL):
                qry_ref[c, :, 128 * t : 128 * t + 128] = turned[8 * c : 8 * c + 8]


def pair_kernel(d_ref, gp_ref, bw_ref, out_ref, wt_ref):
    @pl.when(pl.program_id(0) == 0)
    def _():
        wide = jnp.concatenate([bw_ref[...].astype(F32), jnp.zeros((CZ, 128 - H), F32)], 1)
        hi, lo = split2(wide.T[:16] * WL)
        wt_ref[0:16] = hi
        wt_ref[16:32] = lo

    pad = jnp.zeros((4, CZ), BF16)
    for n in range(QB):
        rows = d_ref[n]
        lhs = jnp.concatenate([rows[:16], rows], 0)
        rhs = jnp.concatenate([wt_ref[...], jnp.concatenate([gp_ref[n], pad], 0)], 0)
        out_ref[n] = mm(lhs, rhs, TN).astype(BF16)


def mid_kernel(parts_ref, qry_ref, keys_ref, send_ref):
    total = jnp.sum(parts_ref[...], axis=0)
    keys_ref[...] = total
    for c in range(NCOL):
        send_ref[c, :, 0:QW] = qry_ref[c]
        send_ref[c, :, QW : QW + 128] = total[:, 896:1024]
        send_ref[c, :, QW + 128 : QW + 256] = total[:, 768:896]


def turn(block):
    return jnp.concatenate([block, jnp.zeros((120, 128), F32)], 0).T[:, :8]


def own_lanes(ref, offset):
    base = pl.multiple_of(lax.div(offset, 128) * 128, 128)
    off = lax.rem(offset, 128)
    return [lanes_at(ref[y, :, pl.ds(base, 128)], off, 8) for y in range(3)]


def sum0(x):
    return jnp.sum(x, axis=0, keepdims=True)


def key_kernel(keys_ref, kp_ref, vp_ref, rot_ref, kgr_ref, vgr_ref, kpg_ref, vpg_ref, kfr_ref):
    flat = jnp.concatenate([turn(keys_ref[:, 128 * t : 128 * t + 128]) for t in range(7)], 0)
    kgr_ref[...] = flat[KEY0:VAL0]
    vgr_ref[...] = flat[VAL0:KPT0]
    dk = [flat[KPT0 + 48 * x : KPT0 + 48 * x + 48] for x in range(3)]
    dv = [flat[VPT0 + 96 * x : VPT0 + 96 * x + 96] for x in range(3)]
    offset = row_index() * 8
    kp = own_lanes(kp_ref, offset)
    vp = own_lanes(vp_ref, offset)
    base = pl.multiple_of(col_index() * JK + lax.div(offset, 128) * 128, 128)
    rot = []
    for x in range(3):
        block = lanes_at(
            jnp.concatenate([rot_ref[x, :, pl.ds(base, 128)], jnp.zeros((5, 128), F32)], 0),
            lax.rem(offset, 128),
            8,
        )
        rot.append([block[y : y + 1] for y in range(3)])
    for y in range(3):
        kpg_ref[y] = rot[0][y] * dk[0] + rot[1][y] * dk[1] + rot[2][y] * dk[2]
        vpg_ref[y] = rot[0][y] * dv[0] + rot[1][y] * dv[1] + rot[2][y] * dv[2]
    for x in range(3):
        for y in range(3):
            kfr_ref[x, y : y + 1] = sum0(dk[x] * kp[y]) + sum0(dv[x] * vp[y])
        kfr_ref[x, 3:4] = sum0(dk[x]) + sum0(dv[x])


def last_kernel(
    hw_ref, parts_ref, qp_ref, gpt_ref, gg_ref, rot_ref, tr_ref,
    qgr_ref, qpg_ref, qfr_ref, wg_ref, hg_ref,
):
    total = jnp.sum(parts_ref[...], axis=0)
    flat = jnp.concatenate([turn(total[:, 128 * t : 128 * t + 128]) for t in range(5)], 0)
    qgr_ref[...] = flat[QRY0:QPT0]
    dq = [flat[QPT0 + 48 * x : QPT0 + 48 * x + 48] for x in range(3)]
    opt = [flat[OPT0 + 96 * x : OPT0 + 96 * x + 96] for x in range(3)]
    offset = col_index() * 8
    rot, tr = row_frames(rot_ref, tr_ref, offset, 8)

    def own(ref):
        return [
            lanes_at(jnp.concatenate([ref[y], ref[y]], 1), offset, 8) for y in range(3)
        ]

    qp, gpt, gg = own(qp_ref), own(gpt_ref), own(gg_ref)
    for y in range(3):
        qpg_ref[y] = rot[0][y] * dq[0] + rot[1][y] * dq[1] + rot[2][y] * dq[2]
    for x in range(3):
        away = opt[x] - tr[x]
        for y in range(3):
            qfr_ref[x, y : y + 1] = sum0(dq[x] * qp[y]) + sum0(away * gpt[y])
        qfr_ref[x, 3:4] = sum0(dq[x]) - sum0(gg[x])
    w0 = total[:, QW : QW + 128]
    extra = total[:, QW + 128 : QW + 256]
    lane4 = lax.broadcasted_iota(jnp.int32, (4, 128), 1)
    w1 = jnp.where(lane4 < 64, pltpu.roll(extra, 64, 1)[0:4], extra[4:8])
    wide = jnp.concatenate([w0, w1, jnp.zeros((116, 128), F32)], 0).T
    wg_ref[...] = (WL * wide)[:, :H]
    lane = lax.broadcasted_iota(jnp.int32, (1, 128), 1)
    raw = jnp.zeros((1, 128), F32)
    for h in range(H):
        raw = jnp.where(lane == h, hw_ref[h], raw)
    sig = 1.0 / (1.0 + jnp.exp(-raw))
    sums = pltpu.roll(extra, 128 - 48, 1)[0:1]
    hg_ref[...] = ((-0.5 * WL * WC) * sums * sig)[:, :H]


def struct(shape, dtype=F32):
    return jax.ShapeDtypeStruct(shape, dtype)


def cost(us, nbytes):
    return pl.CostEstimate(flops=int(us * 4e6), bytes_accessed=int(nbytes), transcendentals=0)


def per_device(
    pair_rep, bias_weight, head_weight, queries, key_vectors, values, query_points, key_points,
    value_points, rotations, translations, residue_count, grad_output, grad_points, grad_pair,
):
    steps = IQ // QB
    pair_spec = pl.BlockSpec((QB, JK, CZ), lambda i: (i, 0, 0))
    gp_spec = pl.BlockSpec((QB, H, CZ), lambda i: (i, 0, 0))
    e, p, st, qg, kg, vg, gg = pl.pallas_call(
        logits_kernel,
        name="logits",
        grid=(steps,),
        in_specs=[SMEM_SPEC, SMEM_SPEC, pair_spec, gp_spec] + [VMEM_SPEC] * 11,
        out_specs=[VMEM_SPEC] * 7,
        out_shape=[
            struct((H, IQ, JK)), struct((H, IQ, JK)), struct((NCOL, 24, 128)),
            struct((3, 48, IQ)), struct((3, 48, JK)), struct((3, 96, JK)), struct((3, 96, IQ)),
        ],
        scratch_shapes=[pltpu.VMEM((2, 32 * IQ, 128), F32), pltpu.VMEM((16, CZ), BF16)],
        cost_estimate=cost(8, 6e6),
    )(
        head_weight, residue_count, pair_rep, grad_pair, bias_weight, queries, key_vectors, values,
        query_points, key_points, value_points, rotations, translations, grad_output, grad_points,
    )
    everyone = lax.all_to_all(st, COL, 0, 0, tiled=True)
    d, keys, qry = pl.pallas_call(
        grads_kernel,
        name="grads",
        grid=(steps,),
        in_specs=[SMEM_SPEC] + [VMEM_SPEC] * 11 + [pair_spec],
        out_specs=[pl.BlockSpec((QB, 32, JK), lambda i: (i, 0, 0)), VMEM_SPEC, VMEM_SPEC],
        out_shape=[
            struct((IQ, 32, JK), BF16), struct((2, NCHIP, 8, KW)), struct((NCOL, 8, QW)),
        ],
        scratch_shapes=[
            pltpu.VMEM((2, 32 * IQ, 128), F32), pltpu.VMEM((896, JK), F32),
            pltpu.VMEM((QW, IQ), F32), pltpu.VMEM((16, CZ), F32), pltpu.VMEM((8, 128), F32),
        ],
        cost_estimate=cost(8, 8e6),
    )(
        head_weight, e, p, st, everyone, queries, key_vectors, grad_output, qg, kg, vg, gg, pair_rep,
    )
    swapped = lax.ppermute(keys[1], "row_2", [(0, 1), (1, 0)])
    parts = lax.all_to_all(keys[0] + swapped, CHIPS, 0, 0, tiled=True)
    pair_grad = pl.pallas_call(
        pair_kernel,
        name="pair",
        grid=(steps,),
        in_specs=[pl.BlockSpec((QB, 32, JK), lambda i: (i, 0, 0)), gp_spec, VMEM_SPEC],
        out_specs=pair_spec,
        out_shape=struct((IQ, JK, CZ), BF16),
        scratch_shapes=[pltpu.VMEM((32, CZ), BF16)],
        cost_estimate=cost(6, 6e6),
    )(d, grad_pair, bias_weight)
    keysum, send = pl.pallas_call(
        mid_kernel,
        name="mid",
        in_specs=[VMEM_SPEC] * 2,
        out_specs=[VMEM_SPEC] * 2,
        out_shape=[struct((8, KW)), struct((NCOL, 8, QW + 256))],
        cost_estimate=cost(1, 1e6),
    )(parts, qry)
    last = lax.all_to_all(send, COL, 0, 0, tiled=True)
    key_grad, value_grad, key_point_grad, value_point_grad, key_frame_grad = pl.pallas_call(
        key_kernel,
        name="keyout",
        in_specs=[VMEM_SPEC] * 4,
        out_specs=[VMEM_SPEC] * 5,
        out_shape=[
            struct((192, 8)), struct((192, 8)), struct((3, 48, 8)), struct((3, 96, 8)),
            struct((3, 4, 8)),
        ],
        cost_estimate=cost(2, 1e6),
    )(keysum, key_points, value_points, rotations)
    query_grad, query_point_grad, query_frame_grad, weight_grad, head_grad = pl.pallas_call(
        last_kernel,
        name="last",
        in_specs=[SMEM_SPEC] + [VMEM_SPEC] * 6,
        out_specs=[VMEM_SPEC] * 5,
        out_shape=[
            struct((192, 8)), struct((3, 48, 8)), struct((3, 4, 8)), struct((CZ, H)),
            struct((1, H)),
        ],
        cost_estimate=cost(2, 1e6),
    )(head_weight, last, query_points, grad_points, gg, rotations, translations)
    return (
        pair_grad, query_grad, query_point_grad, query_frame_grad, key_grad, value_grad,
        key_point_grad, value_point_grad, key_frame_grad, weight_grad, head_grad.reshape(H),
    )


def solution(mesh):
    finer = Mesh(mesh.devices.reshape(4, 4, 2, 4, 2), ROW_COL)
    in_specs = (
        P(ROW, COL, None), P(), P(), P(None, ROW), P(None, COL), P(None, COL),
        P(None, None, ROW), P(None, None, COL), P(None, None, COL), P(), P(), P(),
        P(None, ROW), P(None, None, ROW), P(ROW, None, None),
    )
    out_specs = (
        P(ROW, COL, None), P(None, ROW_COL), P(None, None, ROW_COL), P(None, None, ROW_COL),
        P(None, COL_ROW), P(None, COL_ROW), P(None, None, COL_ROW), P(None, None, COL_ROW),
        P(None, None, COL_ROW), P(), P(),
    )
    return jax.shard_map(
        per_device, mesh=finer, in_specs=in_specs, out_specs=out_specs, check_vma=False
    )
```

time: 418 us -> 107 us (0.26)
  waiting for transfers between devices: 224 us -> 1.9 us
  matrix products: 42.1 us -> 0 us
  Pallas kernels: 0 us -> 33.6 us
  starting transfers between devices: 34.6 us -> 4.96 us
  local copies, waits for them, and re-layouts: 45.2 us -> 20.7 us
  between operations: 16.3 us -> 1.32 us
  other arithmetic: 9.25 us -> 1.12 us
    unnamed x2 -> x0, waiting for transfers between devices: 206 us -> none
    psum x5 -> x0, blocking collectives: 44.8 us -> none  [by_axis(): return functools.reduce(lax.psum, axes, shard)]
    dot_general x27 -> x0, matrix products: 42.1 us -> none  [the longest x1 7.47 us: per_device(): jnp.einsum('hij,ihc->ijc', attn_rounded, grad_pair, preferred_element_typ...]
    all_to_all x0 -> x2, blocking collectives: none -> 42 us  [the longest x1 21.5 us: per_device(): parts = lax.all_to_all(keys[0] + swapped, CHIPS, 0, 0, tiled=True)]
    pallas_call x0 -> x6, Pallas kernels: none -> 33.6 us  [the longest x1 10.1 us: per_device(): pl.pallas_call(logits_kernel, name='logits', grid=(steps,), in_specs=[SME...]
    all_to_all x4 -> x1, starting transfers between devices: 34.3 us -> 4.87 us  [per_device(): last = lax.all_to_all(send, COL, 0, 0, tiled=True)]
    all_to_all x4 -> x1, waiting for transfers between devices: 18.2 us -> 0.01 us  [per_device(): last = lax.all_to_all(send, COL, 0, 0, tiled=True)]
    another operation x6 -> x0, local copies, waits for them, and re-layouts: 8.47 us -> none  [split_up(): return jnp.moveaxis(shard.reshape(*before, count, -1, *after), dim, 0)]
  transfers between devices with their start and end apart: 5 -> 2, of which waited for: 3 -> 1; matrix products, arithmetic and copies ran while one was open for 11% -> 6% of each run, Pallas kernels for 0% -> 9%
where the time goes in v1:
time: 107 us; the launch traced here: 106 us
  blocking collectives  42 us (39%)
  Pallas kernels  33.6 us (31%)
  local copies, waits for them, and re-layouts  20.7 us (19%)
  starting transfers between devices  4.96 us (5%)
  waiting for transfers between devices  1.9 us (2%)
  between operations  1.32 us (1%)
  other arithmetic  1.12 us (1%)
    all_to_all x1, blocking collectives, per_device(): parts = lax.all_to_all(keys[0] + swapped, CHIPS, 0, 0, tiled=True)  21.5 us
    all_to_all x1, blocking collectives, per_device(): everyone = lax.all_to_all(st, COL, 0, 0, tiled=True)  20.4 us
    unnamed x14, local copies, waits for them, and re-layouts  19.6 us
    pallas_call x1, Pallas kernels, per_device(): pl.pallas_call(logits_kernel, name='logits', grid=(steps,), in_specs=[SME...  10.1 us
    pallas_call x1, Pallas kernels, per_device(): pl.pallas_call(grads_kernel, name='grads', grid=(steps,), in_specs=[SMEM_...  9.77 us
    pallas_call x1, Pallas kernels, per_device(): pl.pallas_call(pair_kernel, name='pair', grid=(steps,), in_specs=[pl.Bloc...  7.05 us
    all_to_all x1, starting transfers between devices, per_device(): last = lax.all_to_all(send, COL, 0, 0, tiled=True)  4.87 us
    pallas_call x1, Pallas kernels, per_device(): pl.pallas_call(last_kernel, name='last', in_specs=[SMEM_SPEC] + [VMEM_SPE...  2.78 us
  transfers between devices with their start and end apart: 2, of which 1 were waited for; matrix products, arithmetic and copies ran while one was open for 6% of the time, Pallas kernels for 9%

profile of v1, /device:TPU:2, one launch (start us, length us, event | category | flops | bytes accessed | tf_op | source)
XLA Modules:
  0.0 105.5 jit_solution(18298427286542381666)
XLA Ops:
  1.3 1.4 %copy.27.bw_ref = bf16[128,12]{1,0:T(8,128)(2,1)} copy(bf16[128,12]{0,1:T(8,128)(2,1)} %param.16) | data formatting | bytes 6144 | tf_op args[1]
  2.7 1.6 %copy.28.q_ref = f32[192,64]{1,0:T(8,128)} copy(f32[192,64]{0,1:T(8,128)} %param.18) | data formatting | bytes 98304 | tf_op args[3]
  4.3 1.6 %copy.29.go_ref = f32[192,64]{1,0:T(8,128)} copy(f32[192,64]{0,1:T(8,128)} %param.27) | data formatting | bytes 98304 | tf_op args[12]
  5.9 1.7 %copy.30.gpt_ref = f32[3,96,64]{2,1,0:T(8,128)} copy(f32[3,96,64]{1,2,0:T(8,128)} %param.28) | data formatting | bytes 147456 | tf_op args[13]
  7.5 1.8 %copy.26.gp_ref = bf16[64,12,128]{2,1,0:T(8,128)(2,1)} copy(bf16[64,12,128]{2,0,1:T(8,128)(2,1)} %param.29) | data formatting | bytes 393216 | tf_op args[14]
  9.3 10.1 %logits.1 = (f32[12,64,256]{2,1,0:T(8,128)}, f32[12,64,256]{2,1,0:T(8,128)}, f32[8,24,128]{2,1,0:T(8,128)}, f32[3,48,64]{2,1,0:T(8,128)}, f32[3,48,256]{2,1,0:T(...) custom-call(f32[12]{0:T(128)} %hw_ref.5, s32[1]{0:T(128)S(6)} %copy.43.rc_ref, bf16[64,256,128]{2,1,0:T(8,128)(2,1)} %pair_ref.3, ...), custom_call_target="tpu_custom_call" | custom-call | flops 32000000 | bytes 6000000 | tf_op jit(solution)/shard_map/logits/pallas_call | solution.py:455
  19.4 20.4 %all_to_all.15.all_ref = f32[8,24,128]{2,1,0:T(8,128)} all-to-all(f32[8,24,128]{2,1,0:T(8,128)} %get-tuple-element.35.own_ref), channel_id=1, replica_groups=mesh['row_0'=4,'row_1'=4,'row_2'=2,'col_0'=4,'col_1'=2] {'col_0','col_1'}, dimensions={0} | all-to-all | bytes 196608 | tf_op jit(solution)/shard_map/all_to_all | solution.py:471
  39.8 9.8 %grads.1 = (bf16[64,32,256]{2,1,0:T(8,128)(2,1)}, f32[2,16,8,1024]{3,2,1,0:T(8,128)}, f32[8,8,640]{2,1,0:T(8,128)}) custom-call(f32[12]{0:T(128)} %hw_ref.5, f32[12,64,256]{2,1,0:T(8,128)} %get-tuple-element.33.e_ref, f32[12,64,256]{2,1,0:T(8,128)} %get-tuple-element.34.p_ref, f32[8,24,128]{2,1,0:T(8,128)} %get-tuple-element.35.own_ref, ...), custom_call_target="tpu_custom_call" | custom-call | flops 32000000 | bytes 8000000 | tf_op jit(solution)/shard_map/grads/pallas_call | solution.py:472
  49.6 1.1 %slice_bitcast_fusion = f32[16,8,1024]{2,1,0:T(8,128)S(1)} fusion(f32[2,16,8,1024]{3,2,1,0:T(8,128)} %get-tuple-element.41), kind=kLoop, calls=%fused_computation.1 | loop fusion | bytes 1048576 | tf_op jit(solution)/shard_map/squeeze | solution.py:489
  50.8 1.9 %collective-permute-done = f32[16,8,1024]{2,1,0:T(8,128)S(1)} collective-permute-done((f32[16,8,1024]{2,1,0:T(8,128)S(1)}, f32[16,8,1024]{2,1,0:T(8,128)S(1)}, u32[]{:S(2)}, u32[]{:S(2)}) %collective-permute-start) | collective-permute-done | bytes 524320 | tf_op jit(solution)/shard_map/ppermute | solution.py:489
  52.7 1.1 %bitcast_add_fusion = f32[16,8,1024]{2,1,0:T(8,128)S(1)} fusion(f32[16,8,1024]{2,1,0:T(8,128)S(1)} %collective-permute-done, f32[2,16,8,1024]{3,2,1,0:T(8,128)} %get-tuple-element.41), kind=kLoop, calls=%fused_computation | loop fusion | flops 131072 | bytes 1572864 | tf_op jit(solution)/shard_map/add | solution.py:490
  53.8 21.5 %all_to_all.16.parts_ref = f32[16,8,1024]{2,1,0:T(8,128)} all-to-all(f32[16,8,1024]{2,1,0:T(8,128)S(1)} %bitcast_add_fusion), channel_id=1, replica_groups=mesh['row_0'=4,'row_1'=4,'row_2'=2,'col_0'=4,'col_1'=2] {'row_0','row_1'}, dimensions={0} | all-to-all | bytes 1048576 | tf_op jit(solution)/shard_map/all_to_all | solution.py:490
  75.3 1.8 %mid.1 = (f32[8,1024]{1,0:T(8,128)}, f32[8,8,896]{2,1,0:T(8,128)}) custom-call(f32[16,8,1024]{2,1,0:T(8,128)} %all_to_all.16.parts_ref, f32[8,8,640]{2,1,0:T(8,128)} %get-tuple-element.42.qry_ref), custom_call_target="tpu_custom_call" | custom-call | flops 4000000 | bytes 1000000 | tf_op jit(solution)/shard_map/mid/pallas_call | solution.py:501
  77.2 4.9 %all-to-all-start.2 = ((f32[8,8,896]{2,1,0:T(8,128)}), f32[8,8,896]{2,1,0:T(8,128)S(1)}, u32[]{:S(2)}, u32[]{:S(2)}) async-start(f32[8,8,896]{2,1,0:T(8,128)} %get-tuple-element.43), calls=%async_computation.2 | async-start | bytes 458752 | tf_op jit(solution)/shard_map/all_to_all | solution.py:509
  82.0 7.1 %pair.1 = bf16[64,256,128]{2,1,0:T(8,128)(2,1)} custom-call(bf16[64,32,256]{2,1,0:T(8,128)(2,1)} %get-tuple-element.40.d_ref, bf16[64,12,128]{2,1,0:T(8,128)(2,1)} %copy.26.gp_ref, bf16[128,12]{1,0:T(8,128)(2,1)} %copy.27.bw_ref), custom_call_target="tpu_custom_call" | custom-call | flops 24000000 | bytes 6000000 | tf_op jit(solution)/shard_map/pair/pallas_call | solution.py:491
  89.1 2.1 %keyout.1 = (f32[192,8]{1,0:T(8,128)}, f32[192,8]{1,0:T(8,128)}, f32[3,48,8]{2,1,0:T(8,128)}, f32[3,96,8]{2,1,0:T(8,128)}, f32[3,4,8]{2,1,0:T(4,128)}) custom-call(f32[8,1024]{1,0:T(8,128)} %get-tuple-element.47.keys_ref, f32[3,48,256]{2,1,0:T(8,128)} %kp_ref.3, f32[3,96,256]{2,1,0:T(8,128)} %vp_ref.3, f32[3,3,2048]{2,1,0:T(4,128)} %rot_ref.5), custom_call_target="tpu_custom_call" | custom-call | flops 8000000 | bytes 1000000 | tf_op jit(solution)/shard_map/keyout/pallas_call | solution.py:510
  91.1 1.6 %copy.38 = f32[192,8]{0,1:T(8,128)} copy(f32[192,8]{1,0:T(8,128)} %get-tuple-element.59) | data formatting | bytes 12288
  92.7 1.6 %copy.39 = f32[192,8]{0,1:T(8,128)} copy(f32[192,8]{1,0:T(8,128)} %get-tuple-element.60) | data formatting | bytes 12288
  94.3 1.6 %copy.40 = f32[3,48,8]{1,2,0:T(8,128)} copy(f32[3,48,8]{2,1,0:T(8,128)} %get-tuple-element.61) | data formatting | bytes 9216
  95.8 1.6 %copy.41 = f32[3,96,8]{1,2,0:T(8,128)} copy(f32[3,96,8]{2,1,0:T(8,128)} %get-tuple-element.62) | data formatting | bytes 18432
  98.1 2.8 %last.1 = (f32[192,8]{1,0:T(8,128)}, f32[3,48,8]{2,1,0:T(8,128)}, f32[3,4,8]{2,1,0:T(4,128)}, f32[128,12]{1,0:T(8,128)}, f32[1,12]{1,0:T(1,128)}) custom-call(f32[12]{0:T(128)} %hw_ref.5, f32[8,8,896]{2,1,0:T(8,128)} %copy-done, f32[3,48,64]{2,1,0:T(8,128)} %qp_ref.3, f32[3,96,64]{2,1,0:T(8,128)} %copy.30.gpt_ref, f32[3,96,64]{2,1,0:T(8,128)} %get-tuple-element.39.gg_ref, ...), custom_call_target="tpu_custom_call" | custom-call | flops 8000000 | bytes 1000000 | tf_op jit(solution)/shard_map/last/pallas_call | solution.py:521
  100.9 1.6 %copy.36 = f32[192,8]{0,1:T(8,128)} copy(f32[192,8]{1,0:T(8,128)} %get-tuple-element.56) | data formatting | bytes 12288
  102.5 1.5 %copy.42 = f32[128,12]{0,1:T(8,128)} copy(f32[128,12]{1,0:T(8,128)} %get-tuple-element.64) | data formatting | bytes 12288
  104.0 1.6 %copy.37 = f32[3,48,8]{1,2,0:T(8,128)} copy(f32[3,48,8]{2,1,0:T(8,128)} %get-tuple-element.57) | data formatting | bytes 9216
  (4 shorter events, 0.8 us)
Async XLA Ops:
  50.7 2.0 %collective-permute-start = (f32[16,8,1024]{2,1,0:T(8,128)S(1)}, f32[16,8,1024]{2,1,0:T(8,128)S(1)}, u32[]{:S(2)}, u32[]{:S(2)}) collective-permute-start(f32[16,8,1024]{2,1,0:T(8,128)S(1)} %slice_bitcast_fusion), channel_id=1, source_target_pairs={{0,8},{8,0},{1,9},{9,1},{2,10},{10,2},{3,11},{11,3},{4,12},{12,4},... | collective-permute-start | bytes 1572872 | tf_op jit(solution)/shard_map/ppermute | solution.py:489
  77.2 20.3 %all-to-all-start.2 = ((f32[8,8,896]{2,1,0:T(8,128)}), f32[8,8,896]{2,1,0:T(8,128)S(1)}, u32[]{:S(2)}, u32[]{:S(2)}) async-start(f32[8,8,896]{2,1,0:T(8,128)} %get-tuple-element.43), calls=%async_computation.2 | async-start | bytes 458752 | tf_op jit(solution)/shard_map/all_to_all | solution.py:509
  97.4 0.7 copy-start

commit v2 on v1

--- a/solution.py
+++ b/solution.py
@@ -75,6 +75,17 @@
         g = rot[x][0] * local[0] + rot[x][1] * local[1] + rot[x][2] * local[2]
         out.append(g if shift is None else g + shift[x])
     return out
+
+
+def flip(x):
+    rows, lanes = x.shape
+    full = -(-lanes // 128) * 128
+    if full > lanes:
+        x = jnp.concatenate([x, jnp.zeros((rows, full - lanes), F32)], 1)
+    x = jnp.concatenate([x, jnp.zeros((128 - rows, full), F32)], 0)
+    return jnp.concatenate(
+        [x[:, t : t + 128].T for t in range(0, full, 128)], 0
+    )[:, :rows]
 
 
 def col_frames(rot_ref, tr_ref):
@@ -107,21 +118,16 @@
 
 
 def logits_kernel(
-    hw_ref, rc_ref, pair_ref, gp_ref, bw_ref, q_ref, k_ref, v_ref, qp_ref, kp_ref, vp_ref,
-    rot_ref, tr_ref, go_ref, gpt_ref,
-    e_ref, p_ref, st_ref, qg_ref, kg_ref, vg_ref, gg_ref,
-    bp_ref, wt_ref,
+    hw_ref, rc_ref, pair_ref, gp_ref, bw_ref, qt_ref, k_ref, v_ref, qp_ref, kp_ref, vp_ref,
+    rot_ref, tr_ref, got_ref, gpt_ref,
+    e_ref, p_ref, st_ref, q_ref, go_ref, qg_ref, kg_ref, vg_ref, gg_ref,
+    bp_ref, gs_ref,
 ):
     step = pl.program_id(0)
-
-    @pl.when(step == 0)
-    def _():
-        wide = jnp.concatenate([bw_ref[...].astype(F32), jnp.zeros((CZ, 128 - H), F32)], 1)
-        wt_ref[...] = wide.T[:16].astype(BF16)
-
-    wt = wt_ref[...]
+    wt = jnp.concatenate([bw_ref[...].astype(F32), jnp.zeros((4, CZ), F32)], 0)
+    gs_ref[...] = gp_ref[...].astype(F32).reshape(H * QB, CZ)
     for n in range(QB):
-        lhs = jnp.concatenate([wt, gp_ref[n]], 0)
+        lhs = jnp.concatenate([wt, gs_ref[pl.ds(n, H, stride=QB), :]], 0).astype(BF16)
         res = mm(lhs, pair_ref[n], NT)
         for half in range(2):
             bp_ref[half, pl.ds(step * QB + n, 16 + H, stride=IQ), :] = res[
@@ -135,7 +141,9 @@
         kg = rotate(crot, ctr, [kp_ref[y] for y in range(3)])
         vg = rotate(crot, ctr, [vp_ref[y] for y in range(3)])
         qg = rotate(rrot, rtr, [qp_ref[y] for y in range(3)])
-        gg = rotate(rrot, None, [gpt_ref[y] for y in range(3)])
+        gg = rotate(rrot, None, [flip(gpt_ref[y])[: H * PV] for y in range(3)])
+        q_ref[...] = flip(qt_ref[...])[: H * C]
+        go_ref[...] = flip(got_ref[...])[: H * C]
         for x in range(3):
             kg_ref[x], vg_ref[x], qg_ref[x], gg_ref[x] = kg[x], vg[x], qg[x], gg[x]
         real = (
@@ -203,7 +211,7 @@
 def grads_kernel(
     hw_ref, e_ref, p_ref, own_ref, all_ref, q_ref, k_ref, go_ref, qg_ref, kg_ref, vg_ref, gg_ref,
     pair_ref,
-    d_ref, key_ref, qry_ref,
+    d_ref, keep_ref, give_ref, qry_ref,
     da_ref, kp_ref, qp_ref, w_ref, hs_ref,
 ):
     step = pl.program_id(0)
@@ -313,17 +321,19 @@
             [kp_ref[128 * t : 128 * t + 128, 128 * b : 128 * b + 128].T for t in range(7)]
             for b in range(2)
         ]
-        for b in range(2):
-            for s in range(16):
-                zone, parity = divmod(16 * b + s, 2)
-                spot = core if parity else 1 - core
-                spot = jnp.abs(parity - core)
-                for t in range(6):
-                    key_ref[spot, zone, :, 128 * t : 128 * t + 128] = keys[b][t][8 * s : 8 * s + 8]
-                key_ref[spot, zone, :, 768:896] = jnp.where(
-                    lane < 48, keys[b][6][8 * s : 8 * s + 8], extra
-                )
-                key_ref[spot, zone, :, 896:1024] = w0
+        def tile(j, t):
+            b, r = divmod(j, 16)
+            if t == 7:
+                return w0
+            piece = keys[b][t][8 * r : 8 * r + 8]
+            return jnp.where(lane < 48, piece, extra) if t == 6 else piece
+
+        first = core == 0
+        for zone in range(NCHIP):
+            for t in range(8):
+                even, odd = tile(2 * zone, t), tile(2 * zone + 1, t)
+                keep_ref[zone, :, 128 * t : 128 * t + 128] = jnp.where(first, even, odd)
+                give_ref[zone, :, 128 * t : 128 * t + 128] = jnp.where(first, odd, even)
         for t in range(5):
             block = qp_ref[128 * t : 128 * t + 128]
             turned = jnp.concatenate([block, jnp.zeros((128, 64), F32)], 1).T
@@ -331,19 +341,16 @@
                 qry_ref[c, :, 128 * t : 128 * t + 128] = turned[8 * c : 8 * c + 8]
 
 
-def pair_kernel(d_ref, gp_ref, bw_ref, out_ref, wt_ref):
-    @pl.when(pl.program_id(0) == 0)
-    def _():
-        wide = jnp.concatenate([bw_ref[...].astype(F32), jnp.zeros((CZ, 128 - H), F32)], 1)
-        hi, lo = split2(wide.T[:16] * WL)
-        wt_ref[0:16] = hi
-        wt_ref[16:32] = lo
-
-    pad = jnp.zeros((4, CZ), BF16)
+def pair_kernel(d_ref, gp_ref, bw_ref, out_ref, gs_ref):
+    wide = jnp.concatenate([bw_ref[...].astype(F32) * WL, jnp.zeros((4, CZ), F32)], 0)
+    hi, lo = split2(wide)
+    gs_ref[...] = gp_ref[...].astype(F32).reshape(H * QB, CZ)
+    pad = jnp.zeros((4, CZ), F32)
     for n in range(QB):
         rows = d_ref[n]
         lhs = jnp.concatenate([rows[:16], rows], 0)
-        rhs = jnp.concatenate([wt_ref[...], jnp.concatenate([gp_ref[n], pad], 0)], 0)
+        part = jnp.concatenate([gs_ref[pl.ds(n, H, stride=QB), :], pad], 0).astype(BF16)
+        rhs = jnp.concatenate([hi, lo, part], 0)
         out_ref[n] = mm(lhs, rhs, TN).astype(BF16)
 
 
@@ -356,78 +363,100 @@
         send_ref[c, :, QW + 128 : QW + 256] = total[:, 768:896]
 
 
-def turn(block):
-    return jnp.concatenate([block, jnp.zeros((120, 128), F32)], 0).T[:, :8]
-
-
-def own_lanes(ref, offset):
+def own_lanes(ref, offset, rows):
     base = pl.multiple_of(lax.div(offset, 128) * 128, 128)
     off = lax.rem(offset, 128)
-    return [lanes_at(ref[y, :, pl.ds(base, 128)], off, 8) for y in range(3)]
-
-
-def sum0(x):
-    return jnp.sum(x, axis=0, keepdims=True)
-
-
-def key_kernel(keys_ref, kp_ref, vp_ref, rot_ref, kgr_ref, vgr_ref, kpg_ref, vpg_ref, kfr_ref):
-    flat = jnp.concatenate([turn(keys_ref[:, 128 * t : 128 * t + 128]) for t in range(7)], 0)
-    kgr_ref[...] = flat[KEY0:VAL0]
-    vgr_ref[...] = flat[VAL0:KPT0]
-    dk = [flat[KPT0 + 48 * x : KPT0 + 48 * x + 48] for x in range(3)]
-    dv = [flat[VPT0 + 96 * x : VPT0 + 96 * x + 96] for x in range(3)]
+    return [lanes_at(ref[y, :, pl.ds(base, 128)], off, 128) for y in range(3)]
+
+
+def sum1(x):
+    return jnp.sum(x, axis=1, keepdims=True)
+
+
+def frame_cols(rot_ref, tr_ref, at):
+    base = pl.multiple_of(lax.div(at, 128) * 128, 128)
+    rows = [rot_ref[x, :, pl.ds(base, 128)] for x in range(3)] + [tr_ref[:, pl.ds(base, 128)]]
+    block = jnp.concatenate(rows + [jnp.zeros((116, 128), F32)], 0)
+    return lanes_at(block, lax.rem(at, 128), 128).T[:8]
+
+
+def tall(rows):
+    x = jnp.concatenate(rows, 0)
+    full = -(-x.shape[0] // 128) * 128
+    if full > x.shape[0]:
+        x = jnp.concatenate([x, jnp.zeros((full - x.shape[0], 128), F32)], 0)
+    return jnp.concatenate([x[t : t + 128].T[:8] for t in range(0, full, 128)], 1)
+
+
+def frame_out(ref, table):
+    lane = lax.broadcasted_iota(jnp.int32, (8, 128), 1)
+    block = jnp.zeros((8, 128), F32)
+    for (x, y), column in table.items():
+        block = jnp.where(lane == 4 * x + y, column, block)
+    block = jnp.concatenate([block, jnp.zeros((120, 128), F32)], 0).T
+    for x in range(3):
+        ref[x] = block[4 * x : 4 * x + 4, :8]
+
+
+def key_kernel(
+    keys_ref, kp_ref, vp_ref, qp_ref, rot_ref, tr_ref,
+    kgr_ref, vgr_ref, kpg_ref, vpg_ref, kfr_ref, qpo_ref, fr_ref,
+):
+    flat = keys_ref[...]
+    kgr_ref[...] = flat[:, KEY0:VAL0]
+    vgr_ref[...] = flat[:, VAL0:KPT0]
+    dk = [flat[:, KPT0 + 48 * x : KPT0 + 48 * x + 48] for x in range(3)]
+    dv = [flat[:, VPT0 + 96 * x : VPT0 + 96 * x + 96] for x in range(3)]
     offset = row_index() * 8
-    kp = own_lanes(kp_ref, offset)
-    vp = own_lanes(vp_ref, offset)
-    base = pl.multiple_of(col_index() * JK + lax.div(offset, 128) * 128, 128)
-    rot = []
-    for x in range(3):
-        block = lanes_at(
-            jnp.concatenate([rot_ref[x, :, pl.ds(base, 128)], jnp.zeros((5, 128), F32)], 0),
-            lax.rem(offset, 128),
-            8,
-        )
-        rot.append([block[y : y + 1] for y in range(3)])
+    local = tall(own_lanes(kp_ref, offset, 48) + own_lanes(vp_ref, offset, 96))
+    kp = [local[:, 48 * y : 48 * y + 48] for y in range(3)]
+    vp = [local[:, 144 + 96 * y : 240 + 96 * y] for y in range(3)]
+    fr = frame_cols(rot_ref, tr_ref, col_index() * JK + offset)
+    rot = [[fr[:, 3 * x + y : 3 * x + y + 1] for y in range(3)] for x in range(3)]
+    table = {}
     for y in range(3):
         kpg_ref[y] = rot[0][y] * dk[0] + rot[1][y] * dk[1] + rot[2][y] * dk[2]
         vpg_ref[y] = rot[0][y] * dv[0] + rot[1][y] * dv[1] + rot[2][y] * dv[2]
     for x in range(3):
         for y in range(3):
-            kfr_ref[x, y : y + 1] = sum0(dk[x] * kp[y]) + sum0(dv[x] * vp[y])
-        kfr_ref[x, 3:4] = sum0(dk[x]) + sum0(dv[x])
+            table[x, y] = sum1(dk[x] * kp[y]) + sum1(dv[x] * vp[y])
+        table[x, 3] = sum1(dk[x]) + sum1(dv[x])
+    frame_out(kfr_ref, table)
+    off = col_index() * 8
+    qpo_ref[...] = tall(
+        [lanes_at(jnp.concatenate([qp_ref[y], qp_ref[y]], 1), off, 128) for y in range(3)]
+    )
+    fr_ref[...] = frame_cols(rot_ref, tr_ref, row_index() * IQ + off)
 
 
 def last_kernel(
-    hw_ref, parts_ref, qp_ref, gpt_ref, gg_ref, rot_ref, tr_ref,
-    qgr_ref, qpg_ref, qfr_ref, wg_ref, hg_ref,
+    hw_ref, parts_ref, qpo_ref, fr_ref, gpt_ref, qgr_ref, qpg_ref, qfr_ref, wg_ref, hg_ref,
 ):
     total = jnp.sum(parts_ref[...], axis=0)
-    flat = jnp.concatenate([turn(total[:, 128 * t : 128 * t + 128]) for t in range(5)], 0)
-    qgr_ref[...] = flat[QRY0:QPT0]
-    dq = [flat[QPT0 + 48 * x : QPT0 + 48 * x + 48] for x in range(3)]
-    opt = [flat[OPT0 + 96 * x : OPT0 + 96 * x + 96] for x in range(3)]
-    offset = col_index() * 8
-    rot, tr = row_frames(rot_ref, tr_ref, offset, 8)
-
-    def own(ref):
-        return [
-            lanes_at(jnp.concatenate([ref[y], ref[y]], 1), offset, 8) for y in range(3)
-        ]
-
-    qp, gpt, gg = own(qp_ref), own(gpt_ref), own(gg_ref)
+    qgr_ref[...] = total[:, QRY0:QPT0]
+    dq = [total[:, QPT0 + 48 * x : QPT0 + 48 * x + 48] for x in range(3)]
+    opt = [total[:, OPT0 + 96 * x : OPT0 + 96 * x + 96] for x in range(3)]
+    fr = fr_ref[...]
+    rot = [[fr[:, 3 * x + y : 3 * x + y + 1] for y in range(3)] for x in range(3)]
+    at = pl.multiple_of(col_index() * 8, 8)
+    gpt = [gpt_ref[y, pl.ds(at, 8), :] for y in range(3)]
+    qp = [qpo_ref[:, 48 * y : 48 * y + 48] for y in range(3)]
+    gsum = [sum1(g) for g in gpt]
     for y in range(3):
         qpg_ref[y] = rot[0][y] * dq[0] + rot[1][y] * dq[1] + rot[2][y] * dq[2]
+    table = {}
     for x in range(3):
-        away = opt[x] - tr[x]
+        away = opt[x] - fr[:, 9 + x : 10 + x]
         for y in range(3):
-            qfr_ref[x, y : y + 1] = sum0(dq[x] * qp[y]) + sum0(away * gpt[y])
-        qfr_ref[x, 3:4] = sum0(dq[x]) - sum0(gg[x])
+            table[x, y] = sum1(dq[x] * qp[y]) + sum1(away * gpt[y])
+        back = rot[x][0] * gsum[0] + rot[x][1] * gsum[1] + rot[x][2] * gsum[2]
+        table[x, 3] = sum1(dq[x]) - back
+    frame_out(qfr_ref, table)
     w0 = total[:, QW : QW + 128]
     extra = total[:, QW + 128 : QW + 256]
     lane4 = lax.broadcasted_iota(jnp.int32, (4, 128), 1)
-    w1 = jnp.where(lane4 < 64, pltpu.roll(extra, 64, 1)[0:4], extra[4:8])
-    wide = jnp.concatenate([w0, w1, jnp.zeros((116, 128), F32)], 0).T
-    wg_ref[...] = (WL * wide)[:, :H]
+    wg_ref[0:8] = WL * w0
+    wg_ref[8:12] = WL * jnp.where(lane4 < 64, pltpu.roll(extra, 64, 1)[0:4], extra[4:8])
     lane = lax.broadcasted_iota(jnp.int32, (1, 128), 1)
     raw = jnp.zeros((1, 128), F32)
     for h in range(H):
@@ -451,43 +480,46 @@
 ):
     steps = IQ // QB
     pair_spec = pl.BlockSpec((QB, JK, CZ), lambda i: (i, 0, 0))
-    gp_spec = pl.BlockSpec((QB, H, CZ), lambda i: (i, 0, 0))
-    e, p, st, qg, kg, vg, gg = pl.pallas_call(
+    gp_spec = pl.BlockSpec((H, QB, CZ), lambda i: (0, i, 0))
+    gp_heads = grad_pair.transpose(1, 0, 2)
+    bw_heads = bias_weight.T
+    gpt_rows = grad_points.transpose(0, 2, 1)
+    e, p, st, q, go, qg, kg, vg, gg = pl.pallas_call(
         logits_kernel,
         name="logits",
         grid=(steps,),
         in_specs=[SMEM_SPEC, SMEM_SPEC, pair_spec, gp_spec] + [VMEM_SPEC] * 11,
-        out_specs=[VMEM_SPEC] * 7,
+        out_specs=[VMEM_SPEC] * 9,
         out_shape=[
             struct((H, IQ, JK)), struct((H, IQ, JK)), struct((NCOL, 24, 128)),
+            struct((H * C, IQ)), struct((H * C, IQ)),
             struct((3, 48, IQ)), struct((3, 48, JK)), struct((3, 96, JK)), struct((3, 96, IQ)),
         ],
-        scratch_shapes=[pltpu.VMEM((2, 32 * IQ, 128), F32), pltpu.VMEM((16, CZ), BF16)],
+        scratch_shapes=[pltpu.VMEM((2, 32 * IQ, 128), F32), pltpu.VMEM((H * QB, CZ), F32)],
         cost_estimate=cost(8, 6e6),
     )(
-        head_weight, residue_count, pair_rep, grad_pair, bias_weight, queries, key_vectors, values,
-        query_points, key_points, value_points, rotations, translations, grad_output, grad_points,
+        head_weight, residue_count, pair_rep, gp_heads, bw_heads, queries.T, key_vectors, values,
+        query_points, key_points, value_points, rotations, translations, grad_output.T, gpt_rows,
     )
     everyone = lax.all_to_all(st, COL, 0, 0, tiled=True)
-    d, keys, qry = pl.pallas_call(
+    d, keep, give, qry = pl.pallas_call(
         grads_kernel,
         name="grads",
         grid=(steps,),
         in_specs=[SMEM_SPEC] + [VMEM_SPEC] * 11 + [pair_spec],
-        out_specs=[pl.BlockSpec((QB, 32, JK), lambda i: (i, 0, 0)), VMEM_SPEC, VMEM_SPEC],
+        out_specs=[pl.BlockSpec((QB, 32, JK), lambda i: (i, 0, 0))] + [VMEM_SPEC] * 3,
         out_shape=[
-            struct((IQ, 32, JK), BF16), struct((2, NCHIP, 8, KW)), struct((NCOL, 8, QW)),
+            struct((IQ, 32, JK), BF16), struct((NCHIP, 8, KW)), struct((NCHIP, 8, KW)),
+            struct((NCOL, 8, QW)),
         ],
         scratch_shapes=[
             pltpu.VMEM((2, 32 * IQ, 128), F32), pltpu.VMEM((896, JK), F32),
             pltpu.VMEM((QW, IQ), F32), pltpu.VMEM((16, CZ), F32), pltpu.VMEM((8, 128), F32),
         ],
         cost_estimate=cost(8, 8e6),
-    )(
-        head_weight, e, p, st, everyone, queries, key_vectors, grad_output, qg, kg, vg, gg, pair_rep,
-    )
-    swapped = lax.ppermute(keys[1], "row_2", [(0, 1), (1, 0)])
-    parts = lax.all_to_all(keys[0] + swapped, CHIPS, 0, 0, tiled=True)
+    )(head_weight, e, p, st, everyone, q, key_vectors, go, qg, kg, vg, gg, pair_rep)
+    swapped = lax.ppermute(give, "row_2", [(0, 1), (1, 0)])
+    parts = lax.all_to_all(keep + swapped, CHIPS, 0, 0, tiled=True)
     pair_grad = pl.pallas_call(
         pair_kernel,
         name="pair",
@@ -495,9 +527,9 @@
         in_specs=[pl.BlockSpec((QB, 32, JK), lambda i: (i, 0, 0)), gp_spec, VMEM_SPEC],
         out_specs=pair_spec,
         out_shape=struct((IQ, JK, CZ), BF16),
-        scratch_shapes=[pltpu.VMEM((32, CZ), BF16)],
+        scratch_shapes=[pltpu.VMEM((H * QB, CZ), F32)],
         cost_estimate=cost(6, 6e6),
-    )(d, grad_pair, bias_weight)
+    )(d, gp_heads, bw_heads)
     keysum, send = pl.pallas_call(
         mid_kernel,
         name="mid",
@@ -507,31 +539,34 @@
         cost_estimate=cost(1, 1e6),
     )(parts, qry)
     last = lax.all_to_all(send, COL, 0, 0, tiled=True)
-    key_grad, value_grad, key_point_grad, value_point_grad, key_frame_grad = pl.pallas_call(
-        key_kernel,
-        name="keyout",
-        in_specs=[VMEM_SPEC] * 4,
-        out_specs=[VMEM_SPEC] * 5,
-        out_shape=[
-            struct((192, 8)), struct((192, 8)), struct((3, 48, 8)), struct((3, 96, 8)),
-            struct((3, 4, 8)),
-        ],
-        cost_estimate=cost(2, 1e6),
-    )(keysum, key_points, value_points, rotations)
+    key_grad, value_grad, key_point_grad, value_point_grad, key_frame_grad, qpo, fr = (
+        pl.pallas_call(
+            key_kernel,
+            name="keyout",
+            in_specs=[VMEM_SPEC] * 6,
+            out_specs=[VMEM_SPEC] * 7,
+            out_shape=[
+                struct((8, 192)), struct((8, 192)), struct((3, 8, 48)), struct((3, 8, 96)),
+                struct((3, 4, 8)), struct((8, 256)), struct((8, 128)),
+            ],
+            cost_estimate=cost(2, 1e6),
+        )(keysum, key_points, value_points, query_points, rotations, translations)
+    )
     query_grad, query_point_grad, query_frame_grad, weight_grad, head_grad = pl.pallas_call(
         last_kernel,
         name="last",
-        in_specs=[SMEM_SPEC] + [VMEM_SPEC] * 6,
+        in_specs=[SMEM_SPEC] + [VMEM_SPEC] * 4,
         out_specs=[VMEM_SPEC] * 5,
         out_shape=[
-            struct((192, 8)), struct((3, 48, 8)), struct((3, 4, 8)), struct((CZ, H)),
+            struct((8, 192)), struct((3, 8, 48)), struct((3, 4, 8)), struct((H, CZ)),
             struct((1, H)),
         ],
         cost_estimate=cost(2, 1e6),
-    )(head_weight, last, query_points, grad_points, gg, rotations, translations)
+    )(head_weight, last, qpo, fr, gpt_rows)
     return (
-        pair_grad, query_grad, query_point_grad, query_frame_grad, key_grad, value_grad,
-        key_point_grad, value_point_grad, key_frame_grad, weight_grad, head_grad.reshape(H),
+        pair_grad, query_grad.T, query_point_grad.transpose(0, 2, 1), query_frame_grad, key_grad.T,
+        value_grad.T, key_point_grad.transpose(0, 2, 1), value_point_grad.transpose(0, 2, 1),
+        key_frame_grad, weight_grad.T, head_grad.reshape(H),
     )
 
 

time: 107 us -> 88.6 us (0.83)
  local copies, waits for them, and re-layouts: 20.7 us -> 0.68 us
  Pallas kernels: 33.6 us -> 35.2 us
    unnamed x14 -> x2, local copies, waits for them, and re-layouts: 19.6 us -> 0.68 us
    pallas_call x1, Pallas kernels: 2.07 us -> 3.83 us  [per_device(): pl.pallas_call(key_kernel, name='keyout', in_specs=[VMEM_SPEC] * 6, out_s...]
    squeeze x1 -> x0, local copies, waits for them, and re-layouts: 1.08 us -> none  [per_device(): swapped = lax.ppermute(keys[1], 'row_2', [(0, 1), (1, 0)])]
  transfers between devices with their start and end apart: 2 -> 2, of which waited for: 1 -> 1; matrix products, arithmetic and copies ran while one was open for 6% -> 0% of each run, Pallas kernels for 9% -> 12%
where the time goes in v2:
time: 88.6 us; the launch traced here: 87.4 us
  blocking collectives  42 us (47%)
  Pallas kernels  35.2 us (40%)
  starting transfers between devices  4.97 us (6%)
  waiting for transfers between devices  2.11 us (2%)
  between operations  1.31 us (1%)
  other arithmetic  1.12 us (1%)
    all_to_all x1, blocking collectives, per_device(): parts = lax.all_to_all(keep + swapped, CHIPS, 0, 0, tiled=True)  21.5 us
    all_to_all x1, blocking collectives, per_device(): everyone = lax.all_to_all(st, COL, 0, 0, tiled=True)  20.4 us
    pallas_call x1, Pallas kernels, per_device(): pl.pallas_call(logits_kernel, name='logits', grid=(steps,), in_specs=[SME...  10.1 us
    pallas_call x1, Pallas kernels, per_device(): pl.pallas_call(grads_kernel, name='grads', grid=(steps,), in_specs=[SMEM_...  9.83 us
    pallas_call x1, Pallas kernels, per_device(): pl.pallas_call(pair_kernel, name='pair', grid=(steps,), in_specs=[pl.Bloc...  6.96 us
    all_to_all x1, starting transfers between devices, per_device(): last = lax.all_to_all(send, COL, 0, 0, tiled=True)  4.87 us
    pallas_call x1, Pallas kernels, per_device(): pl.pallas_call(key_kernel, name='keyout', in_specs=[VMEM_SPEC] * 6, out_s...  3.83 us
    pallas_call x1, Pallas kernels, per_device(): pl.pallas_call(last_kernel, name='last', in_specs=[SMEM_SPEC] + [VMEM_SPE...  2.7 us
  transfers between devices with their start and end apart: 2, of which 1 were waited for; matrix products, arithmetic and copies ran while one was open for 0% of the time, Pallas kernels for 12%

profile of v2, /device:TPU:2, one launch (start us, length us, event | category | flops | bytes accessed | tf_op | source)
XLA Modules:
  0.0 87.4 jit_solution(1453825352617416968)
XLA Ops:
  1.3 10.1 %logits.1 = (f32[12,64,256]{2,1,0:T(8,128)}, f32[12,64,256]{2,1,0:T(8,128)}, f32[8,24,128]{2,1,0:T(8,128)}, f32[192,64]{1,0:T(8,128)}, f32[192,64]{1,0:T(8,128)}...) custom-call(f32[12]{0:T(128)} %hw_ref.5, s32[1]{0:T(128)S(6)} %copy.26.rc_ref, ...), custom_call_target="tpu_custom_call" | custom-call | flops 32000000 | bytes 6000000 | tf_op jit(solution)/shard_map/logits/pallas_call | solution.py:487
  11.4 20.4 %all_to_all.15.all_ref = f32[8,24,128]{2,1,0:T(8,128)} all-to-all(f32[8,24,128]{2,1,0:T(8,128)} %get-tuple-element.40.own_ref), channel_id=1, replica_groups=mesh['row_0'=4,'row_1'=4,'row_2'=2,'col_0'=4,'col_1'=2] {'col_0','col_1'}, dimensions={0} | all-to-all | bytes 196608 | tf_op jit(solution)/shard_map/all_to_all | solution.py:504
  31.8 9.8 %grads.1 = (bf16[64,32,256]{2,1,0:T(8,128)(2,1)}, f32[16,8,1024]{2,1,0:T(8,128)}, f32[16,8,1024]{2,1,0:T(8,128)}, f32[8,8,640]{2,1,0:T(8,128)}) custom-call(f32[12]{0:T(128)} %hw_ref.5, f32[12,64,256]{2,1,0:T(8,128)} %get-tuple-element.38.e_ref, f32[12,64,256]{2,1,0:T(8,128)} %get-tuple-element.39.p_ref, f32[8,24,128]{2,1,0:T(8,128)} %get-tuple-element.40.own_ref, ...), custom_call_target="tpu_custom_call" | custom-call | flops 32000000 | bytes 8000000 | tf_op jit(solution)/shard_map/grads/pallas_call | solution.py:505
  41.7 0.1 collective-permute-start
  41.8 2.1 %collective-permute-done = f32[16,8,1024]{2,1,0:T(8,128)S(1)} collective-permute-done((f32[16,8,1024]{2,1,0:T(8,128)}, f32[16,8,1024]{2,1,0:T(8,128)S(1)}, u32[]{:S(2)}, u32[]{:S(2)}) %collective-permute-start) | collective-permute-done | bytes 524320 | tf_op jit(solution)/shard_map/ppermute | solution.py:521
  43.9 1.1 %add.3 = f32[16,8,1024]{2,1,0:T(8,128)S(1)} add(f32[16,8,1024]{2,1,0:T(8,128)} %get-tuple-element.48, f32[16,8,1024]{2,1,0:T(8,128)S(1)} %collective-permute-done) | non-fusion elementwise | flops 131072 | bytes 1572864 | tf_op jit(solution)/shard_map/add | solution.py:522
  45.0 21.5 %all_to_all.16.parts_ref = f32[16,8,1024]{2,1,0:T(8,128)} all-to-all(f32[16,8,1024]{2,1,0:T(8,128)S(1)} %add.3), channel_id=1, replica_groups=mesh['row_0'=4,'row_1'=4,'row_2'=2,'col_0'=4,'col_1'=2] {'row_0','row_1'}, dimensions={0} | all-to-all | bytes 1048576 | tf_op jit(solution)/shard_map/all_to_all | solution.py:522
  66.5 1.8 %mid.1 = (f32[8,1024]{1,0:T(8,128)}, f32[8,8,896]{2,1,0:T(8,128)}) custom-call(f32[16,8,1024]{2,1,0:T(8,128)} %all_to_all.16.parts_ref, f32[8,8,640]{2,1,0:T(8,128)} %get-tuple-element.50.qry_ref), custom_call_target="tpu_custom_call" | custom-call | flops 4000000 | bytes 1000000 | tf_op jit(solution)/shard_map/mid/pallas_call | solution.py:533
  68.3 4.9 %all-to-all-start.2 = ((f32[8,8,896]{2,1,0:T(8,128)}), f32[8,8,896]{2,1,0:T(8,128)S(1)}, u32[]{:S(2)}, u32[]{:S(2)}) async-start(f32[8,8,896]{2,1,0:T(8,128)} %get-tuple-element.51), calls=%async_computation.2 | async-start | bytes 458752 | tf_op jit(solution)/shard_map/all_to_all | solution.py:541
  73.2 7.0 %pair.1 = bf16[64,256,128]{2,1,0:T(8,128)(2,1)} custom-call(bf16[64,32,256]{2,1,0:T(8,128)(2,1)} %get-tuple-element.47.d_ref, bf16[12,64,128]{2,1,0:T(8,128)(2,1)} %bitcast.14, bf16[12,128]{1,0:T(8,128)(2,1)} %bitcast.20), custom_call_target="tpu_custom_call" | custom-call | flops 24000000 | bytes 6000000 | tf_op jit(solution)/shard_map/pair/pallas_call | solution.py:523
  80.2 3.8 %keyout.1 = (f32[8,192]{1,0:T(8,128)}, f32[8,192]{1,0:T(8,128)}, f32[3,8,48]{2,1,0:T(8,128)}, f32[3,8,96]{2,1,0:T(8,128)}, f32[3,4,8]{2,1,0:T(4,128)}, /*index=5*/f32[8,256]{1,0:T(8,128)}, f32[8,128]{1,0:T(8,128)}) custom-call(f32[8,1024]{1,0:T(8,128)} %get-tuple-element.52.keys_ref, f32[3,48,256]{2,1,0:T(8,128)} %kp_ref.3, f32[3,96,256]{2,1,0:T(8,128)} %vp_ref.3, ...), custom_call_target="tpu_custom_call" | custom-call | flops 8000000 | bytes 1000000 | tf_op jit(solution)/shard_map/keyout/pallas_call | solution.py:543
  84.0 0.0 all-to-all-done.2.parts_ref
  84.0 0.0 copy-start
  84.0 0.7 copy-done
  84.7 2.7 %last.1 = (f32[8,192]{1,0:T(8,128)}, f32[3,8,48]{2,1,0:T(8,128)}, f32[3,4,8]{2,1,0:T(4,128)}, f32[12,128]{1,0:T(8,128)}, f32[1,12]{1,0:T(1,128)}) custom-call(f32[12]{0:T(128)} %hw_ref.5, f32[8,8,896]{2,1,0:T(8,128)} %copy-done, f32[8,256]{1,0:T(8,128)} %get-tuple-element.53.qpo_ref, f32[8,128]{1,0:T(8,128)} %get-tuple-element.54.fr_ref, f32[3,64,96]{2,1,0:T(8,128)} %bitcast.16), custom_call_target="tpu_custom_call" | custom-call | flops 8000000 | bytes 1000000 | tf_op jit(solution)/shard_map/last/pallas_call | solution.py:555
Async XLA Ops:
  41.7 2.2 %collective-permute-start = (f32[16,8,1024]{2,1,0:T(8,128)}, f32[16,8,1024]{2,1,0:T(8,128)S(1)}, u32[]{:S(2)}, u32[]{:S(2)}) collective-permute-start(f32[16,8,1024]{2,1,0:T(8,128)} %get-tuple-element.49), channel_id=1, source_target_pairs={{0,8},{8,0},{1,9},{9,1},{2,10},{10,2},{3,11},{11,3},{4,12},{12,4},... | collective-permute-start | bytes 1572872 | tf_op jit(solution)/shard_map/ppermute | solution.py:521
  68.3 15.7 %all-to-all-start.2 = ((f32[8,8,896]{2,1,0:T(8,128)}), f32[8,8,896]{2,1,0:T(8,128)S(1)}, u32[]{:S(2)}, u32[]{:S(2)}) async-start(f32[8,8,896]{2,1,0:T(8,128)} %get-tuple-element.51), calls=%async_computation.2 | async-start | bytes 458752 | tf_op jit(solution)/shard_map/all_to_all | solution.py:541
  84.0 0.7 copy-start

commit v3 on v2

--- a/solution.py
+++ b/solution.py
@@ -26,7 +26,9 @@
 KEY0, VAL0, KPT0, VPT0, KEND = 0, 192, 384, 528, 816
 QRY0, QPT0, OPT0, QEND = 0, 192, 336, 624
 KW, QW = 1024, 640
-QB = 8
+LIMIT = 20 << 20
+QB = 16
+PB = 8
 
 F32, BF16 = jnp.float32, jnp.bfloat16
 VMEM_SPEC = pl.BlockSpec(memory_space=pltpu.VMEM)
@@ -117,95 +119,122 @@
     return rot, [block[x : x + 1] for x in range(3)]
 
 
+HBM_SPEC = pl.BlockSpec(memory_space=pltpu.HBM)
+
+
 def logits_kernel(
-    hw_ref, rc_ref, pair_ref, gp_ref, bw_ref, qt_ref, k_ref, v_ref, qp_ref, kp_ref, vp_ref,
-    rot_ref, tr_ref, got_ref, gpt_ref,
-    e_ref, p_ref, st_ref, q_ref, go_ref, qg_ref, kg_ref, vg_ref, gg_ref,
-    bp_ref, gs_ref,
+    rc_ref, hw_hbm, pair_hbm, gp_hbm, bw_hbm, qt_hbm, k_hbm, v_hbm, qp_hbm, kp_hbm, vp_hbm,
+    rot_hbm, tr_hbm, got_hbm, gpt_hbm,
+    e_ref, p_ref, st_ref, q_ref, go_ref, qg_ref, kg_ref, vg_ref, gg_ref, pair_ref, k_ref,
+    bp_ref, gs_ref, hw_ref, gp_ref, bw_ref, qt_ref, v_ref, qp_ref, kp_ref, vp_ref, rot_ref,
+    tr_ref, got_ref, gpt_ref, sems, pair_sems,
 ):
-    step = pl.program_id(0)
+    def pair_copy(b):
+        part = pl.ds(b * PB, PB)
+        return pltpu.make_async_copy(pair_hbm.at[part], pair_ref.at[part], pair_sems.at[b])
+
+    moves = [
+        (gp_hbm, gp_ref), (bw_hbm, bw_ref), (k_hbm, k_ref), (v_hbm, v_ref), (qt_hbm, qt_ref),
+        (got_hbm, got_ref), (qp_hbm, qp_ref), (kp_hbm, kp_ref), (vp_hbm, vp_ref),
+        (gpt_hbm, gpt_ref), (rot_hbm, rot_ref), (tr_hbm, tr_ref), (hw_hbm, hw_ref),
+    ]
+    copies = [pltpu.make_async_copy(a, b, sems.at[n]) for n, (a, b) in enumerate(moves)]
+    for c in copies[:2]:
+        c.start()
+    pair_copy(0).start()
+    for c in copies[2:]:
+        c.start()
+    for b in range(1, IQ // PB):
+        pair_copy(b).start()
+    for c in copies[:2]:
+        c.wait()
     wt = jnp.concatenate([bw_ref[...].astype(F32), jnp.zeros((4, CZ), F32)], 0)
-    gs_ref[...] = gp_ref[...].astype(F32).reshape(H * QB, CZ)
-    for n in range(QB):
-        lhs = jnp.concatenate([wt, gs_ref[pl.ds(n, H, stride=QB), :]], 0).astype(BF16)
-        res = mm(lhs, pair_ref[n], NT)
-        for half in range(2):
-            bp_ref[half, pl.ds(step * QB + n, 16 + H, stride=IQ), :] = res[
-                :, half * 128 : half * 128 + 128
-            ]
-
-    @pl.when(step == IQ // QB - 1)
-    def _():
-        crot, ctr = col_frames(rot_ref, tr_ref)
-        rrot, rtr = row_frames(rot_ref, tr_ref, 0, IQ)
-        kg = rotate(crot, ctr, [kp_ref[y] for y in range(3)])
-        vg = rotate(crot, ctr, [vp_ref[y] for y in range(3)])
-        qg = rotate(rrot, rtr, [qp_ref[y] for y in range(3)])
-        gg = rotate(rrot, None, [flip(gpt_ref[y])[: H * PV] for y in range(3)])
-        q_ref[...] = flip(qt_ref[...])[: H * C]
-        go_ref[...] = flip(got_ref[...])[: H * C]
-        for x in range(3):
-            kg_ref[x], vg_ref[x], qg_ref[x], gg_ref[x] = kg[x], vg[x], qg[x], gg[x]
-        real = (
-            lax.broadcasted_iota(jnp.int32, (IQ, JK), 1) + col_index() * JK < rc_ref[0]
+    gs_ref[...] = gp_ref[...].astype(F32).reshape(H * IQ, CZ)
+
+    @pl.loop(0, IQ // PB)
+    def _(b):
+        pair_copy(b).wait()
+        for n in range(PB):
+            at = b * PB + n
+            lhs = jnp.concatenate([wt, gs_ref[pl.ds(at, H, stride=IQ), :]], 0).astype(BF16)
+            res = mm(lhs, pair_ref[at], NT)
+            for half in range(2):
+                bp_ref[half, pl.ds(at, 16 + H, stride=IQ), :] = res[
+                    :, half * 128 : half * 128 + 128
+                ]
+
+    for c in copies[2:]:
+        c.wait()
+    crot, ctr = col_frames(rot_ref, tr_ref)
+    rrot, rtr = row_frames(rot_ref, tr_ref, 0, IQ)
+    kg = rotate(crot, ctr, [kp_ref[y] for y in range(3)])
+    vg = rotate(crot, ctr, [vp_ref[y] for y in range(3)])
+    qg = rotate(rrot, rtr, [qp_ref[y] for y in range(3)])
+    gg = rotate(rrot, None, [flip(gpt_ref[y])[: H * PV] for y in range(3)])
+    q_ref[...] = flip(qt_ref[...])[: H * C]
+    go_ref[...] = flip(got_ref[...])[: H * C]
+    for x in range(3):
+        kg_ref[x], vg_ref[x], qg_ref[x], gg_ref[x] = kg[x], vg[x], qg[x], gg[x]
+    real = (
+        lax.broadcasted_iota(jnp.int32, (IQ, JK), 1) + col_index() * JK < rc_ref[0]
+    )
+    lane = lax.broadcasted_iota(jnp.int32, (IQ, 128), 1)
+    stats = [jnp.zeros((IQ, 128), F32), jnp.zeros((IQ, 128), F32)]
+    row4q = lax.broadcasted_iota(jnp.int32, (4, IQ), 0)
+    row4k = lax.broadcasted_iota(jnp.int32, (4, JK), 0)
+    for h in range(H):
+        cf = coef_row(hw_ref, h, IQ)
+        qgh = [qg_ref[x, 4 * h : 4 * h + 4] for x in range(3)]
+        kgh = [kg_ref[x, 4 * h : 4 * h + 4] for x in range(3)]
+        qn = sum(jnp.sum(t * t, axis=0, keepdims=True) for t in qgh)
+        kn = sum(jnp.sum(t * t, axis=0, keepdims=True) for t in kgh)
+        qtail = jnp.where(row4q == 0, -cf, jnp.where(row4q == 1, -cf * qn, 0.0))
+        ktail = jnp.where(row4k == 0, kn, jnp.where(row4k == 1, 1.0, 0.0))
+        qf = jnp.concatenate(
+            [q_ref[C * h : C * h + C] * (WL * WS)] + [2.0 * cf * t for t in qgh] + [qtail], 0
         )
-        lane = lax.broadcasted_iota(jnp.int32, (IQ, 128), 1)
-        stats = [jnp.zeros((IQ, 128), F32), jnp.zeros((IQ, 128), F32)]
-        row4q = lax.broadcasted_iota(jnp.int32, (4, IQ), 0)
-        row4k = lax.broadcasted_iota(jnp.int32, (4, JK), 0)
-        for h in range(H):
-            cf = coef_row(hw_ref, h, IQ)
-            qgh = [qg_ref[x, 4 * h : 4 * h + 4] for x in range(3)]
-            kgh = [kg_ref[x, 4 * h : 4 * h + 4] for x in range(3)]
-            qn = sum(jnp.sum(t * t, axis=0, keepdims=True) for t in qgh)
-            kn = sum(jnp.sum(t * t, axis=0, keepdims=True) for t in kgh)
-            qtail = jnp.where(row4q == 0, -cf, jnp.where(row4q == 1, -cf * qn, 0.0))
-            ktail = jnp.where(row4k == 0, kn, jnp.where(row4k == 1, 1.0, 0.0))
-            qf = jnp.concatenate(
-                [q_ref[C * h : C * h + C] * (WL * WS)] + [2.0 * cf * t for t in qgh] + [qtail], 0
+        kf = jnp.concatenate([k_ref[C * h : C * h + C]] + kgh + [ktail], 0)
+        a1, a2, a3 = split3(qf)
+        b1, b2, b3 = split3(kf)
+        core = mm(
+            jnp.concatenate([a1, a1, a2, a1, a2, a3], 0),
+            jnp.concatenate([b1, b2, b1, b3, b2, b1], 0),
+            TN,
+        )
+        gf = jnp.concatenate(
+            [go_ref[C * h : C * h + C]] + [gg_ref[x, 8 * h : 8 * h + 8] for x in range(3)]
+            + [jnp.zeros((8, IQ), F32)], 0
+        )
+        vf = jnp.concatenate(
+            [v_ref[C * h : C * h + C]] + [vg_ref[x, 8 * h : 8 * h + 8] for x in range(3)]
+            + [jnp.zeros((8, JK), F32)], 0
+        )
+        g1, g2 = split2(gf)
+        v1, v2 = split2(vf)
+        prod = mm(
+            jnp.concatenate([g1, g1, g2], 0), jnp.concatenate([v1, v2, v1], 0), TN
+        )
+
+        def planes(base):
+            return jnp.concatenate(
+                [bp_ref[half, base * IQ : base * IQ + IQ, :] for half in range(2)], 1
             )
-            kf = jnp.concatenate([k_ref[C * h : C * h + C]] + kgh + [ktail], 0)
-            a1, a2, a3 = split3(qf)
-            b1, b2, b3 = split3(kf)
-            core = mm(
-                jnp.concatenate([a1, a1, a2, a1, a2, a3], 0),
-                jnp.concatenate([b1, b2, b1, b3, b2, b1], 0),
-                TN,
-            )
-            gf = jnp.concatenate(
-                [go_ref[C * h : C * h + C]] + [gg_ref[x, 8 * h : 8 * h + 8] for x in range(3)]
-                + [jnp.zeros((8, IQ), F32)], 0
-            )
-            vf = jnp.concatenate(
-                [v_ref[C * h : C * h + C]] + [vg_ref[x, 8 * h : 8 * h + 8] for x in range(3)]
-                + [jnp.zeros((8, JK), F32)], 0
-            )
-            g1, g2 = split2(gf)
-            v1, v2 = split2(vf)
-            prod = mm(
-                jnp.concatenate([g1, g1, g2], 0), jnp.concatenate([v1, v2, v1], 0), TN
-            )
-
-            def planes(base):
-                return jnp.concatenate(
-                    [bp_ref[half, base * IQ : base * IQ + IQ, :] for half in range(2)], 1
-                )
-
-            logit = jnp.where(real, core + WL * planes(h), MASKED)
-            prod = prod + planes(16 + h)
-            peak = jnp.max(logit, axis=1, keepdims=True)
-            e = jnp.exp(logit - peak)
-            e_ref[h] = e
-            p_ref[h] = prod
-            total = jnp.sum(e, axis=1, keepdims=True)
-            upper = jnp.sum(e * prod, axis=1, keepdims=True)
-            g, r = divmod(h, 6)
-            acc = jnp.where(lane == r, peak, stats[g])
-            acc = jnp.where(lane == 8 + r, total, acc)
-            stats[g] = jnp.where(lane == 16 + r, upper, acc)
-        packed = jnp.concatenate(stats, 0).T[:24]
-        for c in range(NCOL):
-            st_ref[c] = packed
+
+        logit = jnp.where(real, core + WL * planes(h), MASKED)
+        prod = prod + planes(16 + h)
+        peak = jnp.max(logit, axis=1, keepdims=True)
+        e = jnp.exp(logit - peak)
+        e_ref[h] = e
+        p_ref[h] = prod
+        total = jnp.sum(e, axis=1, keepdims=True)
+        upper = jnp.sum(e * prod, axis=1, keepdims=True)
+        g, r = divmod(h, 6)
+        acc = jnp.where(lane == r, peak, stats[g])
+        acc = jnp.where(lane == 8 + r, total, acc)
+        stats[g] = jnp.where(lane == 16 + r, upper, acc)
+    packed = jnp.concatenate(stats, 0).T[:24]
+    for c in range(NCOL):
+        st_ref[c] = packed
 
 
 def grads_kernel(
@@ -214,10 +243,7 @@
     d_ref, keep_ref, give_ref, qry_ref,
     da_ref, kp_ref, qp_ref, w_ref, hs_ref,
 ):
-    step = pl.program_id(0)
-
-    @pl.when(step == 0)
-    def _():
+    if True:
         peaks = all_ref[:, 0:8]
         top = jnp.max(peaks, axis=0)
         grow = jnp.exp(peaks - top[None])
@@ -297,19 +323,21 @@
             hs = jnp.where(lane == 48 + h, part, hs)
         hs_ref[...] = hs
 
-    dlogs = []
-    for n in range(QB):
-        rows = jnp.concatenate(
-            [da_ref[half, pl.ds(step * QB + n, 32, stride=IQ), :] for half in range(2)], 1
-        ).astype(BF16)
-        d_ref[n] = rows
-        dlogs.append(rows[:16])
-    w_ref[...] += mm(
-        jnp.concatenate(dlogs, 1), pair_ref[...].reshape(QB * JK, CZ), NN
-    )
-
-    @pl.when(step == IQ // QB - 1)
-    def _():
+    @pl.loop(0, IQ // PB)
+    def _(b):
+        dlogs = []
+        for n in range(PB):
+            at = b * PB + n
+            rows = jnp.concatenate(
+                [da_ref[half, pl.ds(at, 32, stride=IQ), :] for half in range(2)], 1
+            ).astype(BF16)
+            d_ref[at] = rows
+            dlogs.append(rows[:16])
+        w_ref[...] += mm(
+            jnp.concatenate(dlogs, 1), pair_ref[pl.ds(b * PB, PB)].reshape(PB * JK, CZ), NN
+        )
+
+    if True:
         core = lax.axis_index("row_2")
         w0 = w_ref[0:8]
         w1 = w_ref[8:16]
@@ -484,30 +512,46 @@
     gp_heads = grad_pair.transpose(1, 0, 2)
     bw_heads = bias_weight.T
     gpt_rows = grad_points.transpose(0, 2, 1)
-    e, p, st, q, go, qg, kg, vg, gg = pl.pallas_call(
+    e, p, st, q, go, qg, kg, vg, gg, pair, keys = pl.pallas_call(
         logits_kernel,
         name="logits",
-        grid=(steps,),
-        in_specs=[SMEM_SPEC, SMEM_SPEC, pair_spec, gp_spec] + [VMEM_SPEC] * 11,
-        out_specs=[VMEM_SPEC] * 9,
+        in_specs=[SMEM_SPEC] + [HBM_SPEC] * 14,
+        out_specs=[VMEM_SPEC] * 11,
         out_shape=[
             struct((H, IQ, JK)), struct((H, IQ, JK)), struct((NCOL, 24, 128)),
             struct((H * C, IQ)), struct((H * C, IQ)),
             struct((3, 48, IQ)), struct((3, 48, JK)), struct((3, 96, JK)), struct((3, 96, IQ)),
+            struct((IQ, JK, CZ), BF16), struct((H * C, JK)),
         ],
-        scratch_shapes=[pltpu.VMEM((2, 32 * IQ, 128), F32), pltpu.VMEM((H * QB, CZ), F32)],
-        cost_estimate=cost(8, 6e6),
+        scratch_shapes=[
+            pltpu.VMEM((2, 32 * IQ, 128), F32), pltpu.VMEM((H * IQ, CZ), F32),
+            pltpu.SMEM((H,), F32), pltpu.VMEM((H, IQ, CZ), BF16), pltpu.VMEM((H, CZ), BF16),
+            pltpu.VMEM((IQ, H * C), F32), pltpu.VMEM((H * C, JK), F32),
+            pltpu.VMEM((3, 48, IQ), F32), pltpu.VMEM((3, 48, JK), F32),
+            pltpu.VMEM((3, 96, JK), F32), pltpu.VMEM((3, 3, 2048), F32),
+            pltpu.VMEM((3, 2048), F32), pltpu.VMEM((IQ, H * C), F32),
+            pltpu.VMEM((3, IQ, 96), F32), pltpu.SemaphoreType.DMA((13,)),
+            pltpu.SemaphoreType.DMA((IQ // PB,)),
+        ],
+        compiler_params=pltpu.CompilerParams(vmem_limit_bytes=LIMIT),
+        cost_estimate=cost(5, 6e6),
     )(
-        head_weight, residue_count, pair_rep, gp_heads, bw_heads, queries.T, key_vectors, values,
-        query_points, key_points, value_points, rotations, translations, grad_output.T, gpt_rows,
+        residue_count,
+        *(
+            pltpu.with_memory_space_constraint(x, pltpu.HBM)
+            for x in (
+                head_weight, pair_rep, gp_heads, bw_heads, queries.T, key_vectors, values,
+                query_points, key_points, value_points, rotations, translations, grad_output.T,
+                gpt_rows,
+            )
+        ),
     )
     everyone = lax.all_to_all(st, COL, 0, 0, tiled=True)
     d, keep, give, qry = pl.pallas_call(
         grads_kernel,
         name="grads",
-        grid=(steps,),
-        in_specs=[SMEM_SPEC] + [VMEM_SPEC] * 11 + [pair_spec],
-        out_specs=[pl.BlockSpec((QB, 32, JK), lambda i: (i, 0, 0))] + [VMEM_SPEC] * 3,
+        in_specs=[SMEM_SPEC] + [VMEM_SPEC] * 12,
+        out_specs=[VMEM_SPEC] * 4,
         out_shape=[
             struct((IQ, 32, JK), BF16), struct((NCHIP, 8, KW)), struct((NCHIP, 8, KW)),
             struct((NCOL, 8, QW)),
@@ -516,8 +560,9 @@
             pltpu.VMEM((2, 32 * IQ, 128), F32), pltpu.VMEM((896, JK), F32),
             pltpu.VMEM((QW, IQ), F32), pltpu.VMEM((16, CZ), F32), pltpu.VMEM((8, 128), F32),
         ],
-        cost_estimate=cost(8, 8e6),
-    )(head_weight, e, p, st, everyone, q, key_vectors, go, qg, kg, vg, gg, pair_rep)
+        compiler_params=pltpu.CompilerParams(vmem_limit_bytes=LIMIT),
+        cost_estimate=cost(5, 8e6),
+    )(head_weight, e, p, st, everyone, q, keys, go, qg, kg, vg, gg, pair)
     swapped = lax.ppermute(give, "row_2", [(0, 1), (1, 0)])
     parts = lax.all_to_all(keep + swapped, CHIPS, 0, 0, tiled=True)
     pair_grad = pl.pallas_call(
@@ -528,14 +573,17 @@
         out_specs=pair_spec,
         out_shape=struct((IQ, JK, CZ), BF16),
         scratch_shapes=[pltpu.VMEM((H * QB, CZ), F32)],
+        compiler_params=pltpu.CompilerParams(vmem_limit_bytes=LIMIT),
         cost_estimate=cost(6, 6e6),
     )(d, gp_heads, bw_heads)
+    parts, pair_grad = lax.optimization_barrier((parts, pair_grad))
     keysum, send = pl.pallas_call(
         mid_kernel,
         name="mid",
         in_specs=[VMEM_SPEC] * 2,
         out_specs=[VMEM_SPEC] * 2,
         out_shape=[struct((8, KW)), struct((NCOL, 8, QW + 256))],
+        compiler_params=pltpu.CompilerParams(vmem_limit_bytes=LIMIT),
         cost_estimate=cost(1, 1e6),
     )(parts, qry)
     last = lax.all_to_all(send, COL, 0, 0, tiled=True)
@@ -549,7 +597,8 @@
                 struct((8, 192)), struct((8, 192)), struct((3, 8, 48)), struct((3, 8, 96)),
                 struct((3, 4, 8)), struct((8, 256)), struct((8, 128)),
             ],
-            cost_estimate=cost(2, 1e6),
+            compiler_params=pltpu.CompilerParams(vmem_limit_bytes=LIMIT),
+        cost_estimate=cost(2, 1e6),
         )(keysum, key_points, value_points, query_points, rotations, translations)
     )
     query_grad, query_point_grad, query_frame_grad, weight_grad, head_grad = pl.pallas_call(
@@ -561,6 +610,7 @@
             struct((8, 192)), struct((3, 8, 48)), struct((3, 4, 8)), struct((H, CZ)),
             struct((1, H)),
         ],
+        compiler_params=pltpu.CompilerParams(vmem_limit_bytes=LIMIT),
         cost_estimate=cost(2, 1e6),
     )(head_weight, last, qpo, fr, gpt_rows)
     return (

time: 88.6 us -> 76.2 us (0.86)
  the two profiles are of different devices: /device:TPU:2 before, /device:TPU:32 now
where the time goes in v3:
time: 76.2 us; the launch traced here: 75.8 us
  waiting for transfers between devices  23 us (30%)
  blocking collectives  20.3 us (27%)
  Pallas kernels  19.8 us (26%)
  starting transfers between devices  10.5 us (14%)
  between operations  1.42 us (2%)
  other arithmetic  0.87 us (1%)
    all_to_all x1, blocking collectives, per_device(): everyone = lax.all_to_all(st, COL, 0, 0, tiled=True)  20.3 us
    all_to_all x1, waiting for transfers between devices, per_device(): parts = lax.all_to_all(keep + swapped, CHIPS, 0, 0, tiled=True)  11.6 us
    all_to_all x1, waiting for transfers between devices, per_device(): last = lax.all_to_all(send, COL, 0, 0, tiled=True)  9.45 us
    all_to_all x1, starting transfers between devices, per_device(): parts = lax.all_to_all(keep + swapped, CHIPS, 0, 0, tiled=True)  6.98 us
    pallas_call x1, Pallas kernels, per_device(): pl.pallas_call(logits_kernel, name='logits', in_specs=[SMEM_SPEC] + [HBM_...  6.13 us
    pallas_call x1, Pallas kernels, per_device(): pl.pallas_call(grads_kernel, name='grads', in_specs=[SMEM_SPEC] + [VMEM_S...  4.59 us
    pallas_call x1, Pallas kernels, per_device(): pl.pallas_call(pair_kernel, name='pair', grid=(steps,), in_specs=[pl.Bloc...  3.45 us
    all_to_all x1, starting transfers between devices, per_device(): last = lax.all_to_all(send, COL, 0, 0, tiled=True)  3.4 us
  transfers between devices with their start and end apart: 3, of which 3 were waited for; matrix products, arithmetic and copies ran while one was open for 0% of the time, Pallas kernels for 8%

profile of v3, /device:TPU:32, one launch (start us, length us, event | category | flops | bytes accessed | tf_op | source)
XLA Modules:
  0.0 75.8 jit_solution(8880224184909287297)
XLA Ops:
  0.6 0.0 copy-start.8
  1.3 6.1 %logits.1 = (f32[12,64,256]{2,1,0:T(8,128)S(1)}, f32[12,64,256]{2,1,0:T(8,128)S(1)}, f32[8,24,128]{2,1,0:T(8,128)S(1)}, f32[192,64]{1,0:T(8,128)S(1)}, f32[192,6...) custom-call(s32[1]{0:T(128)S(6)} %copy.26.rc_ref, ...), custom_call_target="tpu_custom_call" | custom-call | flops 20000000 | bytes 6000000 | tf_op jit(solution)/shard_map/logits/pallas_call | solution.py:515
  7.5 20.3 %all_to_all.15.all_ref = f32[8,24,128]{2,1,0:T(8,128)S(1)} all-to-all(f32[8,24,128]{2,1,0:T(8,128)S(1)} %get-tuple-element.44.own_ref), channel_id=1, replica_groups=mesh['row_0'=4,'row_1'=4,'row_2'=2,'col_0'=4,'col_1'=2] {'col_0','col_1'}, dimensions={0} | all-to-all | bytes 196608 | tf_op jit(solution)/shard_map/all_to_all | solution.py:549
  27.7 0.0 copy-done.8
  27.7 4.6 %grads.1 = (bf16[64,32,256]{2,1,0:T(8,128)(2,1)S(1)}, f32[16,8,1024]{2,1,0:T(8,128)S(1)}, f32[16,8,1024]{2,1,0:T(8,128)S(1)}, f32[8,8,640]{2,1,0:T(8,128)S(1)}) custom-call(f32[12]{0:T(128)S(1)} %copy-done.8, f32[12,64,256]{2,1,0:T(8,128)S(1)} %get-tuple-element.42.e_ref, f32[12,64,256]{2,1,0:T(8,128)S(1)} %get-tuple-element.43.p_ref, ...), custom_call_target="tpu_custom_call" | custom-call | flops 20000000 | bytes 8000000 | tf_op jit(solution)/shard_map/grads/pallas_call | solution.py:550
  32.3 0.1 collective-permute-start
  32.4 1.9 %collective-permute-done = f32[16,8,1024]{2,1,0:T(8,128)S(1)} collective-permute-done((f32[16,8,1024]{2,1,0:T(8,128)S(1)}, f32[16,8,1024]{2,1,0:T(8,128)S(1)}, u32[]{:S(2)}, u32[]{:S(2)}) %collective-permute-start) | collective-permute-done | bytes 524320 | tf_op jit(solution)/shard_map/ppermute | solution.py:566
  34.3 0.9 %add.3 = f32[16,8,1024]{2,1,0:T(8,128)} add(f32[16,8,1024]{2,1,0:T(8,128)S(1)} %get-tuple-element.53, f32[16,8,1024]{2,1,0:T(8,128)S(1)} %collective-permute-done) | non-fusion elementwise | flops 131072 | bytes 1572864 | tf_op jit(solution)/shard_map/add | solution.py:567
  35.2 0.0 copy-start.6
  35.2 0.0 copy-start.3
  35.2 7.0 %all-to-all-start.1 = ((f32[16,8,1024]{2,1,0:T(8,128)}), f32[16,8,1024]{2,1,0:T(8,128)S(1)}, u32[]{:S(2)}, u32[]{:S(2)}) async-start(f32[16,8,1024]{2,1,0:T(8,128)} %add.3), calls=%async_computation.1 | async-start | bytes 1048576 | tf_op jit(solution)/shard_map/all_to_all | solution.py:567
  42.2 0.0 copy-done.1
  42.2 0.0 copy-done.7
  42.2 3.5 %pair.1 = bf16[64,256,128]{2,1,0:T(8,128)(2,1)} custom-call(bf16[64,32,256]{2,1,0:T(8,128)(2,1)S(1)} %get-tuple-element.55.d_ref, bf16[12,64,128]{2,1,0:T(8,128)(2,1)S(1)} %bitcast.14, bf16[12,128]{1,0:T(8,128)(2,1)S(1)} %bitcast.18), custom_call_target="tpu_custom_call" | custom-call | flops 24000000 | bytes 6000000 | tf_op jit(solution)/shard_map/pair/pallas_call | solution.py:568
  45.7 11.6 %all-to-all-done.1.parts_ref = f32[16,8,1024]{2,1,0:T(8,128)S(1)} async-done(((f32[16,8,1024]{2,1,0:T(8,128)}), f32[16,8,1024]{2,1,0:T(8,128)S(1)}, u32[]{:S(2)}, u32[]{:S(2)}) %all-to-all-start.1) | async-done | bytes 524320 | tf_op jit(solution)/shard_map/all_to_all | solution.py:567
  57.3 0.7 mid.1
  58.0 3.4 %all-to-all-start.2 = ((f32[8,8,896]{2,1,0:T(8,128)}), f32[8,8,896]{2,1,0:T(8,128)S(1)}, u32[]{:S(2)}, u32[]{:S(2)}) async-start(f32[8,8,896]{2,1,0:T(8,128)} %get-tuple-element.59), calls=%async_computation.2 | async-start | bytes 458752 | tf_op jit(solution)/shard_map/all_to_all | solution.py:589
  61.4 0.0 copy-done
  61.5 0.0 copy-done.2
  61.5 0.0 copy-done.4
  61.5 2.7 %keyout.1 = (f32[8,192]{1,0:T(8,128)}, f32[8,192]{1,0:T(8,128)}, f32[3,8,48]{2,1,0:T(8,128)}, f32[3,8,96]{2,1,0:T(8,128)}, f32[3,4,8]{2,1,0:T(4,128)}, /*index=5*/f32[8,256]{1,0:T(8,128)S(1)}, f32[8,128]{1,0:T(8,128)S(1)}) custom-call(f32[8,1024]{1,0:T(8,128)S(1)} %get-tuple-element.60.keys_ref, f32[3,48,256]{2,1,0:T(8,128)S(1)} %copy-done.2, ...), custom_call_target="tpu_custom_call" | custom-call | flops 8000000 | bytes 1000000 | tf_op jit(solution)/shard_map/keyout/pallas_call | solution.py:591
  64.2 9.5 %all-to-all-done.2.parts_ref = f32[8,8,896]{2,1,0:T(8,128)S(1)} async-done(((f32[8,8,896]{2,1,0:T(8,128)}), f32[8,8,896]{2,1,0:T(8,128)S(1)}, u32[]{:S(2)}, u32[]{:S(2)}) %all-to-all-start.2) | async-done | bytes 229408 | tf_op jit(solution)/shard_map/all_to_all | solution.py:589
  73.6 0.0 copy-done.3
  73.6 2.2 %last.1 = (f32[8,192]{1,0:T(8,128)}, f32[3,8,48]{2,1,0:T(8,128)}, f32[3,4,8]{2,1,0:T(4,128)}, f32[12,128]{1,0:T(8,128)}, f32[1,12]{1,0:T(1,128)}) custom-call(f32[12]{0:T(128)S(1)} %copy-done.8, f32[8,8,896]{2,1,0:T(8,128)S(1)} %all-to-all-done.2.parts_ref, f32[8,256]{1,0:T(8,128)S(1)} %get-tuple-element.61.qpo_ref, f32[8,128]{1,0:T(8,128)S(1)} %get-tuple-element.62.fr_ref, ...), custom_call_target="tpu_custom_call" | custom-call | flops 8000000 | bytes 1000000 | tf_op jit(solution)/shard_map/last/pallas_call | solution.py:604
  (8 shorter events, 0.0 us)
Async XLA Ops:
  0.6 27.1 %copy-start.8 = (f32[12]{0:T(128)S(1)}, f32[12]{0:T(128)}, u32[]{:S(2)}) copy-start(f32[12]{0:T(128)} %hw_ref.3) | copy-start | bytes 148
  27.7 14.5 %copy-start.1 = (bf16[64,12,128]{2,0,1:T(8,128)(2,1)S(1)}, bf16[64,12,128]{2,0,1:T(8,128)(2,1)}, u32[]{:S(2)}) copy-start(bf16[64,12,128]{2,0,1:T(8,128)(2,1)} %param.29) | copy-start | bytes 589828
  27.7 14.5 %copy-start.7 = (bf16[128,12]{0,1:T(8,128)(2,1)S(1)}, bf16[128,12]{0,1:T(8,128)(2,1)}, u32[]{:S(2)}) copy-start(bf16[128,12]{0,1:T(8,128)(2,1)} %param.16) | copy-start | bytes 9220
  32.3 2.0 %collective-permute-start = (f32[16,8,1024]{2,1,0:T(8,128)S(1)}, f32[16,8,1024]{2,1,0:T(8,128)S(1)}, u32[]{:S(2)}, u32[]{:S(2)}) collective-permute-start(f32[16,8,1024]{2,1,0:T(8,128)S(1)} %get-tuple-element.54), channel_id=1, source_target_pairs={{0,8},{8,0},{1,9},{9,1},{2,10},{10,2},{3,11},{11,3},{4,12},{12,4},... | collective-permute-start | bytes 1572872 | tf_op jit(solution)/shard_map/ppermute | solution.py:566
  35.2 26.2 %copy-start = (f32[3,96,256]{2,1,0:T(8,128)S(1)}, f32[3,96,256]{2,1,0:T(8,128)}, u32[]{:S(2)}) copy-start(f32[3,96,256]{2,1,0:T(8,128)} %vp_ref.1) | copy-start | bytes 884740
  35.2 26.2 %copy-start.2 = (f32[3,48,256]{2,1,0:T(8,128)S(1)}, f32[3,48,256]{2,1,0:T(8,128)}, u32[]{:S(2)}) copy-start(f32[3,48,256]{2,1,0:T(8,128)} %kp_ref.1) | copy-start | bytes 442372
  35.2 26.3 %copy-start.4 = (f32[3,3,2048]{2,1,0:T(4,128)S(1)}, f32[3,3,2048]{2,1,0:T(4,128)}, u32[]{:S(2)}) copy-start(f32[3,3,2048]{2,1,0:T(4,128)} %rot_ref.1) | copy-start | bytes 221188
  35.2 26.3 %copy-start.5 = (f32[3,48,64]{2,1,0:T(8,128)S(1)}, f32[3,48,64]{2,1,0:T(8,128)}, u32[]{:S(2)}) copy-start(f32[3,48,64]{2,1,0:T(8,128)} %qp_ref.1) | copy-start | bytes 110596
  35.2 26.3 %copy-start.6 = (f32[3,2048]{1,0:T(4,128)S(1)}, f32[3,2048]{1,0:T(4,128)}, u32[]{:S(2)}) copy-start(f32[3,2048]{1,0:T(4,128)} %tr_ref.1) | copy-start | bytes 73732
  35.2 38.4 %copy-start.3 = (f32[3,96,64]{1,2,0:T(8,128)S(1)}, f32[3,96,64]{1,2,0:T(8,128)}, u32[]{:S(2)}) copy-start(f32[3,96,64]{1,2,0:T(8,128)} %param.28) | copy-start | bytes 221188
  35.2 22.1 %all-to-all-start.1 = ((f32[16,8,1024]{2,1,0:T(8,128)}), f32[16,8,1024]{2,1,0:T(8,128)S(1)}, u32[]{:S(2)}, u32[]{:S(2)}) async-start(f32[16,8,1024]{2,1,0:T(8,128)} %add.3), calls=%async_computation.1 | async-start | bytes 1048576 | tf_op jit(solution)/shard_map/all_to_all | solution.py:567
  58.0 15.6 %all-to-all-start.2 = ((f32[8,8,896]{2,1,0:T(8,128)}), f32[8,8,896]{2,1,0:T(8,128)S(1)}, u32[]{:S(2)}, u32[]{:S(2)}) async-start(f32[8,8,896]{2,1,0:T(8,128)} %get-tuple-element.59), calls=%async_computation.2 | async-start | bytes 458752 | tf_op jit(solution)/shard_map/all_to_all | solution.py:589

commit v4 on v3

--- a/solution.py
+++ b/solution.py
@@ -357,11 +357,15 @@
             return jnp.where(lane < 48, piece, extra) if t == 6 else piece
 
         first = core == 0
+        my_z, my_y = lax.axis_index("row_0"), lax.axis_index("row_1")
         for zone in range(NCHIP):
+            z, y = divmod(zone, 4)
+            dz = lax.rem(z + 4 - my_z, 4)
+            dy = lax.rem(y + 4 - my_y, 4)
             for t in range(8):
                 even, odd = tile(2 * zone, t), tile(2 * zone + 1, t)
-                keep_ref[zone, :, 128 * t : 128 * t + 128] = jnp.where(first, even, odd)
-                give_ref[zone, :, 128 * t : 128 * t + 128] = jnp.where(first, odd, even)
+                keep_ref[dy, dz, :, 128 * t : 128 * t + 128] = jnp.where(first, even, odd)
+                give_ref[dy, dz, :, 128 * t : 128 * t + 128] = jnp.where(first, odd, even)
         for t in range(5):
             block = qp_ref[128 * t : 128 * t + 128]
             turned = jnp.concatenate([block, jnp.zeros((128, 64), F32)], 1).T
@@ -382,8 +386,8 @@
         out_ref[n] = mm(lhs, rhs, TN).astype(BF16)
 
 
-def mid_kernel(parts_ref, qry_ref, keys_ref, send_ref):
-    total = jnp.sum(parts_ref[...], axis=0)
+def mid_kernel(a_ref, b_ref, c_ref, d_ref, qry_ref, keys_ref, send_ref):
+    total = (a_ref[...] + b_ref[...]) + (c_ref[...] + d_ref[...])
     keys_ref[...] = total
     for c in range(NCOL):
         send_ref[c, :, 0:QW] = qry_ref[c]
@@ -492,6 +496,31 @@
     sig = 1.0 / (1.0 + jnp.exp(-raw))
     sums = pltpu.roll(extra, 128 - 48, 1)[0:1]
     hg_ref[...] = ((-0.5 * WL * WC) * sums * sig)[:, :H]
+
+
+def fold_kernel(count, *refs):
+    ins, outs = refs[:-count], refs[-count:]
+    for n, out in enumerate(outs):
+        out[...] = sum(r[n] for r in ins[1:]) + ins[0][n]
+
+
+def fold_call(name, count, shape):
+    def call(*parts):
+        return pl.pallas_call(
+            functools.partial(fold_kernel, count),
+            name=name,
+            in_specs=[VMEM_SPEC] * len(parts),
+            out_specs=[VMEM_SPEC] * count,
+            out_shape=[struct(shape)] * count,
+            compiler_params=pltpu.CompilerParams(vmem_limit_bytes=LIMIT),
+            cost_estimate=cost(1, 1e6),
+        )(*parts)
+
+    return call
+
+
+def onward(block, axis, step):
+    return lax.ppermute(block, axis, [(n, (n + step) % 4) for n in range(4)])
 
 
 def struct(shape, dtype=F32):
@@ -553,7 +582,7 @@
         in_specs=[SMEM_SPEC] + [VMEM_SPEC] * 12,
         out_specs=[VMEM_SPEC] * 4,
         out_shape=[
-            struct((IQ, 32, JK), BF16), struct((NCHIP, 8, KW)), struct((NCHIP, 8, KW)),
+            struct((IQ, 32, JK), BF16), struct((4, 4, 8, KW)), struct((4, 4, 8, KW)),
             struct((NCOL, 8, QW)),
         ],
         scratch_shapes=[
@@ -564,7 +593,10 @@
         cost_estimate=cost(5, 8e6),
     )(head_weight, e, p, st, everyone, q, keys, go, qg, kg, vg, gg, pair)
     swapped = lax.ppermute(give, "row_2", [(0, 1), (1, 0)])
-    parts = lax.all_to_all(keep + swapped, CHIPS, 0, 0, tiled=True)
+    chip = fold_call("chip", 4, (4, 8, KW))(keep, swapped)
+    by_y = [chip[0]] + [onward(chip[n], "row_1", n) for n in range(1, 4)]
+    line = fold_call("line", 4, (8, KW))(*by_y)
+    parts = [line[0]] + [onward(line[n], "row_0", n) for n in range(1, 4)]
     pair_grad = pl.pallas_call(
         pair_kernel,
         name="pair",
@@ -576,16 +608,15 @@
         compiler_params=pltpu.CompilerParams(vmem_limit_bytes=LIMIT),
         cost_estimate=cost(6, 6e6),
     )(d, gp_heads, bw_heads)
-    parts, pair_grad = lax.optimization_barrier((parts, pair_grad))
     keysum, send = pl.pallas_call(
         mid_kernel,
         name="mid",
-        in_specs=[VMEM_SPEC] * 2,
+        in_specs=[VMEM_SPEC] * 5,
         out_specs=[VMEM_SPEC] * 2,
         out_shape=[struct((8, KW)), struct((NCOL, 8, QW + 256))],
         compiler_params=pltpu.CompilerParams(vmem_limit_bytes=LIMIT),
         cost_estimate=cost(1, 1e6),
-    )(parts, qry)
+    )(*parts, qry)
     last = lax.all_to_all(send, COL, 0, 0, tiled=True)
     key_grad, value_grad, key_point_grad, value_point_grad, key_frame_grad, qpo, fr = (
         pl.pallas_call(

time: 76.2 us -> 70.2 us (0.921)
  the two profiles are of different devices: /device:TPU:32 before, /device:TPU:2 now
where the time goes in v4:
time: 70.2 us; the launch traced here: 69.1 us
  blocking collectives  20.1 us (29%)
  Pallas kernels  19.9 us (28%)
  starting transfers between devices  15.3 us (22%)
  waiting for transfers between devices  12.3 us (18%)
  between operations  1.42 us (2%)
    all_to_all x1, blocking collectives, per_device(): everyone = lax.all_to_all(st, COL, 0, 0, tiled=True)  20.1 us
    ppermute x6, starting transfers between devices, onward(): return lax.ppermute(block, axis, [(n, (n + step) % 4) for n in range(4)])  10.4 us
    ppermute x6, waiting for transfers between devices, onward(): return lax.ppermute(block, axis, [(n, (n + step) % 4) for n in range(4)])  7.23 us
    pallas_call x1, Pallas kernels, per_device(): pl.pallas_call(logits_kernel, name='logits', in_specs=[SMEM_SPEC] + [HBM_...  6.13 us
    all_to_all x1, starting transfers between devices, per_device(): last = lax.all_to_all(send, COL, 0, 0, tiled=True)  4.87 us
    pallas_call x1, Pallas kernels, per_device(): pl.pallas_call(grads_kernel, name='grads', in_specs=[SMEM_SPEC] + [VMEM_S...  4.61 us
    pallas_call x1, Pallas kernels, per_device(): pl.pallas_call(pair_kernel, name='pair', grid=(steps,), in_specs=[pl.Bloc...  3.45 us
    all_to_all x1, waiting for transfers between devices, per_device(): last = lax.all_to_all(send, COL, 0, 0, tiled=True)  3.18 us
  transfers between devices with their start and end apart: 8, of which 6 were waited for; matrix products, arithmetic and copies ran while one was open for 0% of the time, Pallas kernels for 9%

profile of v4, /device:TPU:2, one launch (start us, length us, event | category | flops | bytes accessed | tf_op | source)
XLA Modules:
  0.0 69.1 jit_solution(12565648165664428001)
XLA Ops:
  1.3 6.1 %logits.1 = (f32[12,64,256]{2,1,0:T(8,128)S(1)}, f32[12,64,256]{2,1,0:T(8,128)S(1)}, f32[8,24,128]{2,1,0:T(8,128)S(1)}, f32[192,64]{1,0:T(8,128)S(1)}, f32[192,6...) custom-call(s32[1]{0:T(128)S(6)} %copy.26.rc_ref, ...), custom_call_target="tpu_custom_call" | custom-call | flops 20000000 | bytes 6000000 | tf_op jit(solution)/shard_map/logits/pallas_call | solution.py:544
  7.5 20.1 %all_to_all.10.all_ref = f32[8,24,128]{2,1,0:T(8,128)S(1)} all-to-all(f32[8,24,128]{2,1,0:T(8,128)S(1)} %get-tuple-element.50.own_ref), channel_id=1, replica_groups=mesh['row_0'=4,'row_1'=4,'row_2'=2,'col_0'=4,'col_1'=2] {'col_0','col_1'}, dimensions={0} | all-to-all | bytes 196608 | tf_op jit(solution)/shard_map/all_to_all | solution.py:578
  27.6 4.6 %grads.1 = (bf16[64,32,256]{2,1,0:T(8,128)(2,1)S(1)}, f32[4,4,8,1024]{3,2,1,0:T(8,128)S(1)}, f32[4,4,8,1024]{3,2,1,0:T(8,128)S(1)}, f32[8,8,640]{2,1,0:T(8,128)S(1)}) custom-call(f32[12]{0:T(128)S(1)} %copy-done.8, f32[12,64,256]{2,1,0:T(8,128)S(1)} %get-tuple-element.48.e_ref, f32[12,64,256]{2,1,0:T(8,128)S(1)} %get-tuple-element.49.p_ref, ...), custom_call_target="tpu_custom_call" | custom-call | flops 20000000 | bytes 8000000 | tf_op jit(solution)/shard_map/grads/pallas_call | solution.py:579
  32.2 0.0 copy-start
  32.3 0.1 collective-permute-start
  32.4 1.9 %collective-permute-done.refs_1_ = f32[4,4,8,1024]{3,2,1,0:T(8,128)S(1)} collective-permute-done((f32[4,4,8,1024]{3,2,1,0:T(8,128)S(1)}, f32[4,4,8,1024]{3,2,1,0:T(8,128)S(1)}, u32[]{:S(2)}, u32[]{:S(2)}) %collective-permute-start) | collective-permute-done | bytes 524320 | tf_op jit(solution)/shard_map/ppermute | solution.py:595
  34.3 0.1 chip.1
  34.3 1.7 %collective-permute-start.1 = (f32[4,8,1024]{2,1,0:T(8,128)S(1)}, f32[4,8,1024]{2,1,0:T(8,128)S(1)}, u32[]{:S(2)}, u32[]{:S(2)}) collective-permute-start(f32[4,8,1024]{2,1,0:T(8,128)S(1)} %get-tuple-element.63), channel_id=1, source_target_pairs={{0,16},{16,32},{32,48},{48,0},{1,17},{17,33},{33,49},{49,1},{2,18}... | collective-permute-start | bytes 393224 | tf_op jit(solution)/shard_map/ppermute | solution.py:523
  36.0 2.9 %collective-permute-start.2 = (f32[4,8,1024]{2,1,0:T(8,128)S(1)}, f32[4,8,1024]{2,1,0:T(8,128)S(1)}, u32[]{:S(2)}, u32[]{:S(2)}) collective-permute-start(f32[4,8,1024]{2,1,0:T(8,128)S(1)} %get-tuple-element.64), channel_id=1, source_target_pairs={{0,32},{16,48},{32,0},{48,16},{1,33},{17,49},{33,1},{49,17},{2,34}... | collective-permute-start | bytes 393224 | tf_op jit(solution)/shard_map/ppermute | solution.py:523
  38.9 1.3 %collective-permute-start.3 = (f32[4,8,1024]{2,1,0:T(8,128)S(1)}, f32[4,8,1024]{2,1,0:T(8,128)S(1)}, u32[]{:S(2)}, u32[]{:S(2)}) collective-permute-start(f32[4,8,1024]{2,1,0:T(8,128)S(1)} %get-tuple-element.65), channel_id=1, source_target_pairs={{0,48},{16,0},{32,16},{48,32},{1,49},{17,1},{33,17},{49,33},{2,50}... | collective-permute-start | bytes 393224 | tf_op jit(solution)/shard_map/ppermute | solution.py:523
  40.2 1.0 %collective-permute-done.1.refs_1_ = f32[4,8,1024]{2,1,0:T(8,128)S(1)} collective-permute-done((f32[4,8,1024]{2,1,0:T(8,128)S(1)}, f32[4,8,1024]{2,1,0:T(8,128)S(1)}, u32[]{:S(2)}, u32[]{:S(2)}) %collective-permute-start.1) | collective-permute-done | bytes 131104 | tf_op jit(solution)/shard_map/ppermute | solution.py:523
  41.2 4.0 %collective-permute-done.2.refs_2_ = f32[4,8,1024]{2,1,0:T(8,128)S(1)} collective-permute-done((f32[4,8,1024]{2,1,0:T(8,128)S(1)}, f32[4,8,1024]{2,1,0:T(8,128)S(1)}, u32[]{:S(2)}, u32[]{:S(2)}) %collective-permute-start.2) | collective-permute-done | bytes 131104 | tf_op jit(solution)/shard_map/ppermute | solution.py:523
  45.2 1.1 %collective-permute-start.4 = (f32[8,1024]{1,0:T(8,128)S(1)}, f32[8,1024]{1,0:T(8,128)S(1)}, u32[]{:S(2)}, u32[]{:S(2)}) collective-permute-start(f32[8,1024]{1,0:T(8,128)S(1)} %get-tuple-element.67), channel_id=1, source_target_pairs={{0,64},{64,128},{128,192},{192,0},{1,65},{65,129},{129,193},{193,1... | collective-permute-start | bytes 98312 | tf_op jit(solution)/shard_map/ppermute | solution.py:523
  46.3 1.5 %collective-permute-start.5 = (f32[8,1024]{1,0:T(8,128)S(1)}, f32[8,1024]{1,0:T(8,128)S(1)}, u32[]{:S(2)}, u32[]{:S(2)}) collective-permute-start(f32[8,1024]{1,0:T(8,128)S(1)} %get-tuple-element.68), channel_id=1, source_target_pairs={{0,128},{64,192},{128,0},{192,64},{1,129},{65,193},{129,1},{193,65... | collective-permute-start | bytes 98312 | tf_op jit(solution)/shard_map/ppermute | solution.py:523
  47.8 1.9 %collective-permute-start.6 = (f32[8,1024]{1,0:T(8,128)S(1)}, f32[8,1024]{1,0:T(8,128)S(1)}, u32[]{:S(2)}, u32[]{:S(2)}) collective-permute-start(f32[8,1024]{1,0:T(8,128)S(1)} %get-tuple-element.69), channel_id=1, source_target_pairs={{0,192},{64,0},{128,64},{192,128},{1,193},{65,1},{129,65},{193,129... | collective-permute-start | bytes 98312 | tf_op jit(solution)/shard_map/ppermute | solution.py:523
  49.7 1.4 %collective-permute-done.4.b_ref = f32[8,1024]{1,0:T(8,128)S(1)} collective-permute-done((f32[8,1024]{1,0:T(8,128)S(1)}, f32[8,1024]{1,0:T(8,128)S(1)}, u32[]{:S(2)}, u32[]{:S(2)}) %collective-permute-start.4) | collective-permute-done | bytes 32800 | tf_op jit(solution)/shard_map/ppermute | solution.py:523
  51.1 0.8 %collective-permute-done.5.c_ref = f32[8,1024]{1,0:T(8,128)S(1)} collective-permute-done((f32[8,1024]{1,0:T(8,128)S(1)}, f32[8,1024]{1,0:T(8,128)S(1)}, u32[]{:S(2)}, u32[]{:S(2)}) %collective-permute-start.5) | collective-permute-done | bytes 32800 | tf_op jit(solution)/shard_map/ppermute | solution.py:523
  52.0 0.0 collective-permute-done.6.d_ref
  52.0 0.7 %mid.1 = (f32[8,1024]{1,0:T(8,128)S(1)}, f32[8,8,896]{2,1,0:T(8,128)}) custom-call(f32[8,1024]{1,0:T(8,128)S(1)} %get-tuple-element.66.a_ref, f32[8,1024]{1,0:T(8,128)S(1)} %collective-permute-done.4.b_ref, f32[8,1024]{1,0:T(8,128)S(1)} %collective-permute-done.5.c_ref, f32[8,1024]{1,0:T(8,128)S(1)} %collective-permute-done.6.d_ref, ...), custom_call_target="tpu_custom_call" | custom-call | flops 4000000 | bytes 1000000 | tf_op jit(solution)/shard_map/mid/pallas_call | solution.py:611
  52.7 4.9 %all-to-all-start.1 = ((f32[8,8,896]{2,1,0:T(8,128)}), f32[8,8,896]{2,1,0:T(8,128)S(1)}, u32[]{:S(2)}, u32[]{:S(2)}) async-start(f32[8,8,896]{2,1,0:T(8,128)} %get-tuple-element.71), calls=%async_computation.1 | async-start | bytes 458752 | tf_op jit(solution)/shard_map/all_to_all | solution.py:620
  57.6 3.5 %pair.1 = bf16[64,256,128]{2,1,0:T(8,128)(2,1)} custom-call(bf16[64,32,256]{2,1,0:T(8,128)(2,1)S(1)} %get-tuple-element.59.d_ref, bf16[12,64,128]{2,1,0:T(8,128)(2,1)S(1)} %bitcast.14, bf16[12,128]{1,0:T(8,128)(2,1)S(1)} %bitcast.18), custom_call_target="tpu_custom_call" | custom-call | flops 24000000 | bytes 6000000 | tf_op jit(solution)/shard_map/pair/pallas_call | solution.py:600
  61.0 2.7 %keyout.1 = (f32[8,192]{1,0:T(8,128)}, f32[8,192]{1,0:T(8,128)}, f32[3,8,48]{2,1,0:T(8,128)}, f32[3,8,96]{2,1,0:T(8,128)}, f32[3,4,8]{2,1,0:T(4,128)}, /*index=5*/f32[8,256]{1,0:T(8,128)S(1)}, f32[8,128]{1,0:T(8,128)S(1)}) custom-call(f32[8,1024]{1,0:T(8,128)S(1)} %get-tuple-element.72.keys_ref, f32[3,48,256]{2,1,0:T(8,128)S(1)} %copy-done.2, ...), custom_call_target="tpu_custom_call" | custom-call | flops 8000000 | bytes 1000000 | tf_op jit(solution)/shard_map/keyout/pallas_call | solution.py:622
  63.7 3.2 %all-to-all-done.1.parts_ref = f32[8,8,896]{2,1,0:T(8,128)S(1)} async-done(((f32[8,8,896]{2,1,0:T(8,128)}), f32[8,8,896]{2,1,0:T(8,128)S(1)}, u32[]{:S(2)}, u32[]{:S(2)}) %all-to-all-start.1) | async-done | bytes 229408 | tf_op jit(solution)/shard_map/all_to_all | solution.py:620
  66.9 2.2 %last.1 = (f32[8,192]{1,0:T(8,128)}, f32[3,8,48]{2,1,0:T(8,128)}, f32[3,4,8]{2,1,0:T(4,128)}, f32[12,128]{1,0:T(8,128)}, f32[1,12]{1,0:T(1,128)}) custom-call(f32[12]{0:T(128)S(1)} %copy-done.8, f32[8,8,896]{2,1,0:T(8,128)S(1)} %all-to-all-done.1.parts_ref, f32[8,256]{1,0:T(8,128)S(1)} %get-tuple-element.73.qpo_ref, f32[8,128]{1,0:T(8,128)S(1)} %get-tuple-element.74.fr_ref, ...), custom_call_target="tpu_custom_call" | custom-call | flops 8000000 | bytes 1000000 | tf_op jit(solution)/shard_map/last/pallas_call | solution.py:635
  (19 shorter events, 0.1 us)
Async XLA Ops:
  0.6 26.9 %copy-start.8 = (f32[12]{0:T(128)S(1)}, f32[12]{0:T(128)}, u32[]{:S(2)}) copy-start(f32[12]{0:T(128)} %hw_ref.3) | copy-start | bytes 148
  27.6 30.0 %copy-start.1 = (bf16[64,12,128]{2,0,1:T(8,128)(2,1)S(1)}, bf16[64,12,128]{2,0,1:T(8,128)(2,1)}, u32[]{:S(2)}) copy-start(bf16[64,12,128]{2,0,1:T(8,128)(2,1)} %param.29) | copy-start | bytes 589828
  27.6 30.0 %copy-start.7 = (bf16[128,12]{0,1:T(8,128)(2,1)S(1)}, bf16[128,12]{0,1:T(8,128)(2,1)}, u32[]{:S(2)}) copy-start(bf16[128,12]{0,1:T(8,128)(2,1)} %param.16) | copy-start | bytes 9220
  32.2 28.8 %copy-start = (f32[3,96,256]{2,1,0:T(8,128)S(1)}, f32[3,96,256]{2,1,0:T(8,128)}, u32[]{:S(2)}) copy-start(f32[3,96,256]{2,1,0:T(8,128)} %vp_ref.1) | copy-start | bytes 884740
  32.2 28.8 %copy-start.2 = (f32[3,48,256]{2,1,0:T(8,128)S(1)}, f32[3,48,256]{2,1,0:T(8,128)}, u32[]{:S(2)}) copy-start(f32[3,48,256]{2,1,0:T(8,128)} %kp_ref.1) | copy-start | bytes 442372
  32.2 28.8 %copy-start.4 = (f32[3,3,2048]{2,1,0:T(4,128)S(1)}, f32[3,3,2048]{2,1,0:T(4,128)}, u32[]{:S(2)}) copy-start(f32[3,3,2048]{2,1,0:T(4,128)} %rot_ref.1) | copy-start | bytes 221188
  32.2 28.8 %copy-start.5 = (f32[3,48,64]{2,1,0:T(8,128)S(1)}, f32[3,48,64]{2,1,0:T(8,128)}, u32[]{:S(2)}) copy-start(f32[3,48,64]{2,1,0:T(8,128)} %qp_ref.1) | copy-start | bytes 110596
  32.3 28.8 %copy-start.6 = (f32[3,2048]{1,0:T(4,128)S(1)}, f32[3,2048]{1,0:T(4,128)}, u32[]{:S(2)}) copy-start(f32[3,2048]{1,0:T(4,128)} %tr_ref.1) | copy-start | bytes 73732
  32.3 2.0 %collective-permute-start = (f32[4,4,8,1024]{3,2,1,0:T(8,128)S(1)}, f32[4,4,8,1024]{3,2,1,0:T(8,128)S(1)}, u32[]{:S(2)}, u32[]{:S(2)}) collective-permute-start(f32[4,4,8,1024]{3,2,1,0:T(8,128)S(1)} %get-tuple-element.61), channel_id=1, source_target_pairs={{0,8},{8,0},{1,9},{9,1},{2,10},{10,2},{3,11},{11,3},{4,12},{12,4},... | collective-permute-start | bytes 1572872 | tf_op jit(solution)/shard_map/ppermute | solution.py:595
  34.3 32.6 %copy-start.3 = (f32[3,96,64]{1,2,0:T(8,128)S(1)}, f32[3,96,64]{1,2,0:T(8,128)}, u32[]{:S(2)}) copy-start(f32[3,96,64]{1,2,0:T(8,128)} %param.28) | copy-start | bytes 221188
  34.3 6.9 %collective-permute-start.1 = (f32[4,8,1024]{2,1,0:T(8,128)S(1)}, f32[4,8,1024]{2,1,0:T(8,128)S(1)}, u32[]{:S(2)}, u32[]{:S(2)}) collective-permute-start(f32[4,8,1024]{2,1,0:T(8,128)S(1)} %get-tuple-element.63), channel_id=1, source_target_pairs={{0,16},{16,32},{32,48},{48,0},{1,17},{17,33},{33,49},{49,1},{2,18}... | collective-permute-start | bytes 393224 | tf_op jit(solution)/shard_map/ppermute | solution.py:523
  36.0 9.2 %collective-permute-start.2 = (f32[4,8,1024]{2,1,0:T(8,128)S(1)}, f32[4,8,1024]{2,1,0:T(8,128)S(1)}, u32[]{:S(2)}, u32[]{:S(2)}) collective-permute-start(f32[4,8,1024]{2,1,0:T(8,128)S(1)} %get-tuple-element.64), channel_id=1, source_target_pairs={{0,32},{16,48},{32,0},{48,16},{1,33},{17,49},{33,1},{49,17},{2,34}... | collective-permute-start | bytes 393224 | tf_op jit(solution)/shard_map/ppermute | solution.py:523
  38.9 6.3 %collective-permute-start.3 = (f32[4,8,1024]{2,1,0:T(8,128)S(1)}, f32[4,8,1024]{2,1,0:T(8,128)S(1)}, u32[]{:S(2)}, u32[]{:S(2)}) collective-permute-start(f32[4,8,1024]{2,1,0:T(8,128)S(1)} %get-tuple-element.65), channel_id=1, source_target_pairs={{0,48},{16,0},{32,16},{48,32},{1,49},{17,1},{33,17},{49,33},{2,50}... | collective-permute-start | bytes 393224 | tf_op jit(solution)/shard_map/ppermute | solution.py:523
  45.2 5.9 %collective-permute-start.4 = (f32[8,1024]{1,0:T(8,128)S(1)}, f32[8,1024]{1,0:T(8,128)S(1)}, u32[]{:S(2)}, u32[]{:S(2)}) collective-permute-start(f32[8,1024]{1,0:T(8,128)S(1)} %get-tuple-element.67), channel_id=1, source_target_pairs={{0,64},{64,128},{128,192},{192,0},{1,65},{65,129},{129,193},{193,1... | collective-permute-start | bytes 98312 | tf_op jit(solution)/shard_map/ppermute | solution.py:523
  46.3 5.6 %collective-permute-start.5 = (f32[8,1024]{1,0:T(8,128)S(1)}, f32[8,1024]{1,0:T(8,128)S(1)}, u32[]{:S(2)}, u32[]{:S(2)}) collective-permute-start(f32[8,1024]{1,0:T(8,128)S(1)} %get-tuple-element.68), channel_id=1, source_target_pairs={{0,128},{64,192},{128,0},{192,64},{1,129},{65,193},{129,1},{193,65... | collective-permute-start | bytes 98312 | tf_op jit(solution)/shard_map/ppermute | solution.py:523
  47.8 4.2 %collective-permute-start.6 = (f32[8,1024]{1,0:T(8,128)S(1)}, f32[8,1024]{1,0:T(8,128)S(1)}, u32[]{:S(2)}, u32[]{:S(2)}) collective-permute-start(f32[8,1024]{1,0:T(8,128)S(1)} %get-tuple-element.69), channel_id=1, source_target_pairs={{0,192},{64,0},{128,64},{192,128},{1,193},{65,1},{129,65},{193,129... | collective-permute-start | bytes 98312 | tf_op jit(solution)/shard_map/ppermute | solution.py:523
  52.7 14.2 %all-to-all-start.1 = ((f32[8,8,896]{2,1,0:T(8,128)}), f32[8,8,896]{2,1,0:T(8,128)S(1)}, u32[]{:S(2)}, u32[]{:S(2)}) async-start(f32[8,8,896]{2,1,0:T(8,128)} %get-tuple-element.71), calls=%async_computation.1 | async-start | bytes 458752 | tf_op jit(solution)/shard_map/all_to_all | solution.py:620

commit v5 on v4

--- a/solution.py
+++ b/solution.py
@@ -28,7 +28,7 @@
 KW, QW = 1024, 640
 LIMIT = 20 << 20
 QB = 16
-PB = 8
+PB = 16
 
 F32, BF16 = jnp.float32, jnp.bfloat16
 VMEM_SPEC = pl.BlockSpec(memory_space=pltpu.VMEM)
@@ -125,7 +125,7 @@
 def logits_kernel(
     rc_ref, hw_hbm, pair_hbm, gp_hbm, bw_hbm, qt_hbm, k_hbm, v_hbm, qp_hbm, kp_hbm, vp_hbm,
     rot_hbm, tr_hbm, got_hbm, gpt_hbm,
-    e_ref, p_ref, st_ref, q_ref, go_ref, qg_ref, kg_ref, vg_ref, gg_ref, pair_ref, k_ref,
+    e_ref, p_ref, st_ref, q_ref, go_ref, qg_ref, kg_ref, vg_ref, gg_ref, pair_ref, k_ref, cf_ref, sig_ref,
     bp_ref, gs_ref, hw_ref, gp_ref, bw_ref, qt_ref, v_ref, qp_ref, kp_ref, vp_ref, rot_ref,
     tr_ref, got_ref, gpt_ref, sems, pair_sems,
 ):
@@ -182,8 +182,14 @@
     stats = [jnp.zeros((IQ, 128), F32), jnp.zeros((IQ, 128), F32)]
     row4q = lax.broadcasted_iota(jnp.int32, (4, IQ), 0)
     row4k = lax.broadcasted_iota(jnp.int32, (4, JK), 0)
+    lane8 = lax.broadcasted_iota(jnp.int32, (8, 128), 1)
+    raw = jnp.zeros((8, 128), F32)
     for h in range(H):
-        cf = coef_row(hw_ref, h, IQ)
+        raw = jnp.where(lane8 == h, hw_ref[h], raw)
+        cf_ref[h : h + 1] = coef_row(hw_ref, h, 128)
+    sig_ref[...] = (-0.5 * WL * WC) / (1.0 + jnp.exp(-raw))
+    for h in range(H):
+        cf = cf_ref[h : h + 1, :IQ]
         qgh = [qg_ref[x, 4 * h : 4 * h + 4] for x in range(3)]
         kgh = [kg_ref[x, 4 * h : 4 * h + 4] for x in range(3)]
         qn = sum(jnp.sum(t * t, axis=0, keepdims=True) for t in qgh)
@@ -238,10 +244,10 @@
 
 
 def grads_kernel(
-    hw_ref, e_ref, p_ref, own_ref, all_ref, q_ref, k_ref, go_ref, qg_ref, kg_ref, vg_ref, gg_ref,
+    cf_ref, e_ref, p_ref, own_ref, all_ref, q_ref, k_ref, go_ref, qg_ref, kg_ref, vg_ref, gg_ref,
     pair_ref,
-    d_ref, keep_ref, give_ref, qry_ref,
-    da_ref, kp_ref, qp_ref, w_ref, hs_ref,
+    da_ref, keep_ref, give_ref, qry_ref,
+    kp_ref, qp_ref, w_ref, hs_ref,
 ):
     if True:
         peaks = all_ref[:, 0:8]
@@ -272,8 +278,8 @@
                 da_ref[half, (16 + h) * IQ : (17 + h) * IQ, :] = a[:, piece]
             d1, d2 = split2(d)
             a1, a2 = split2(a)
-            cfq = coef_row(hw_ref, h, IQ)
-            cfk = coef_row(hw_ref, h, JK)
+            cfq = cf_ref[h : h + 1, :IQ]
+            cfk = jnp.concatenate([cf_ref[h : h + 1]] * 2, 1)
             qgh = [qg_ref[x, 4 * h : 4 * h + 4] for x in range(3)]
             kgh = [kg_ref[x, 4 * h : 4 * h + 4] for x in range(3)]
             qf = jnp.concatenate(
@@ -328,11 +334,11 @@
         dlogs = []
         for n in range(PB):
             at = b * PB + n
-            rows = jnp.concatenate(
-                [da_ref[half, pl.ds(at, 32, stride=IQ), :] for half in range(2)], 1
-            ).astype(BF16)
-            d_ref[at] = rows
-            dlogs.append(rows[:16])
+            dlogs.append(
+                jnp.concatenate(
+                    [da_ref[half, pl.ds(at, 16, stride=IQ), :] for half in range(2)], 1
+                ).astype(BF16)
+            )
         w_ref[...] += mm(
             jnp.concatenate(dlogs, 1), pair_ref[pl.ds(b * PB, PB)].reshape(PB * JK, CZ), NN
         )
@@ -373,13 +379,16 @@
                 qry_ref[c, :, 128 * t : 128 * t + 128] = turned[8 * c : 8 * c + 8]
 
 
-def pair_kernel(d_ref, gp_ref, bw_ref, out_ref, gs_ref):
+def pair_kernel(da_ref, gp_ref, bw_ref, out_ref, gs_ref):
     wide = jnp.concatenate([bw_ref[...].astype(F32) * WL, jnp.zeros((4, CZ), F32)], 0)
     hi, lo = split2(wide)
     gs_ref[...] = gp_ref[...].astype(F32).reshape(H * QB, CZ)
     pad = jnp.zeros((4, CZ), F32)
     for n in range(QB):
-        rows = d_ref[n]
+        at = pl.program_id(0) * QB + n
+        rows = jnp.concatenate(
+            [da_ref[half, pl.ds(at, 32, stride=IQ), :] for half in range(2)], 1
+        ).astype(BF16)
         lhs = jnp.concatenate([rows[:16], rows], 0)
         part = jnp.concatenate([gs_ref[pl.ds(n, H, stride=QB), :], pad], 0).astype(BF16)
         rhs = jnp.concatenate([hi, lo, part], 0)
@@ -462,7 +471,7 @@
 
 
 def last_kernel(
-    hw_ref, parts_ref, qpo_ref, fr_ref, gpt_ref, qgr_ref, qpg_ref, qfr_ref, wg_ref, hg_ref,
+    sig_ref, parts_ref, qpo_ref, fr_ref, gpt_ref, qgr_ref, qpg_ref, qfr_ref, wg_ref, hg_ref,
 ):
     total = jnp.sum(parts_ref[...], axis=0)
     qgr_ref[...] = total[:, QRY0:QPT0]
@@ -489,13 +498,8 @@
     lane4 = lax.broadcasted_iota(jnp.int32, (4, 128), 1)
     wg_ref[0:8] = WL * w0
     wg_ref[8:12] = WL * jnp.where(lane4 < 64, pltpu.roll(extra, 64, 1)[0:4], extra[4:8])
-    lane = lax.broadcasted_iota(jnp.int32, (1, 128), 1)
-    raw = jnp.zeros((1, 128), F32)
-    for h in range(H):
-        raw = jnp.where(lane == h, hw_ref[h], raw)
-    sig = 1.0 / (1.0 + jnp.exp(-raw))
     sums = pltpu.roll(extra, 128 - 48, 1)[0:1]
-    hg_ref[...] = ((-0.5 * WL * WC) * sums * sig)[:, :H]
+    hg_ref[...] = (sums * sig_ref[0:1])[:, :H]
 
 
 def fold_kernel(count, *refs):
@@ -541,16 +545,16 @@
     gp_heads = grad_pair.transpose(1, 0, 2)
     bw_heads = bias_weight.T
     gpt_rows = grad_points.transpose(0, 2, 1)
-    e, p, st, q, go, qg, kg, vg, gg, pair, keys = pl.pallas_call(
+    e, p, st, q, go, qg, kg, vg, gg, pair, keys, coef, sig = pl.pallas_call(
         logits_kernel,
         name="logits",
         in_specs=[SMEM_SPEC] + [HBM_SPEC] * 14,
-        out_specs=[VMEM_SPEC] * 11,
+        out_specs=[VMEM_SPEC] * 13,
         out_shape=[
             struct((H, IQ, JK)), struct((H, IQ, JK)), struct((NCOL, 24, 128)),
             struct((H * C, IQ)), struct((H * C, IQ)),
             struct((3, 48, IQ)), struct((3, 48, JK)), struct((3, 96, JK)), struct((3, 96, IQ)),
-            struct((IQ, JK, CZ), BF16), struct((H * C, JK)),
+            struct((IQ, JK, CZ), BF16), struct((H * C, JK)), struct((16, 128)), struct((8, 128)),
         ],
         scratch_shapes=[
             pltpu.VMEM((2, 32 * IQ, 128), F32), pltpu.VMEM((H * IQ, CZ), F32),
@@ -579,19 +583,18 @@
     d, keep, give, qry = pl.pallas_call(
         grads_kernel,
         name="grads",
-        in_specs=[SMEM_SPEC] + [VMEM_SPEC] * 12,
+        in_specs=[VMEM_SPEC] * 13,
         out_specs=[VMEM_SPEC] * 4,
         out_shape=[
-            struct((IQ, 32, JK), BF16), struct((4, 4, 8, KW)), struct((4, 4, 8, KW)),
+            struct((2, 32 * IQ, 128)), struct((4, 4, 8, KW)), struct((4, 4, 8, KW)),
             struct((NCOL, 8, QW)),
         ],
         scratch_shapes=[
-            pltpu.VMEM((2, 32 * IQ, 128), F32), pltpu.VMEM((896, JK), F32),
-            pltpu.VMEM((QW, IQ), F32), pltpu.VMEM((16, CZ), F32), pltpu.VMEM((8, 128), F32),
+            pltpu.VMEM((896, JK), F32), pltpu.VMEM((QW, IQ), F32), pltpu.VMEM((16, CZ), F32), pltpu.VMEM((8, 128), F32),
         ],
         compiler_params=pltpu.CompilerParams(vmem_limit_bytes=LIMIT),
         cost_estimate=cost(5, 8e6),
-    )(head_weight, e, p, st, everyone, q, keys, go, qg, kg, vg, gg, pair)
+    )(coef, e, p, st, everyone, q, keys, go, qg, kg, vg, gg, pair)
     swapped = lax.ppermute(give, "row_2", [(0, 1), (1, 0)])
     chip = fold_call("chip", 4, (4, 8, KW))(keep, swapped)
     by_y = [chip[0]] + [onward(chip[n], "row_1", n) for n in range(1, 4)]
@@ -601,7 +604,7 @@
         pair_kernel,
         name="pair",
         grid=(steps,),
-        in_specs=[pl.BlockSpec((QB, 32, JK), lambda i: (i, 0, 0)), gp_spec, VMEM_SPEC],
+        in_specs=[VMEM_SPEC, gp_spec, VMEM_SPEC],
         out_specs=pair_spec,
         out_shape=struct((IQ, JK, CZ), BF16),
         scratch_shapes=[pltpu.VMEM((H * QB, CZ), F32)],
@@ -635,7 +638,7 @@
     query_grad, query_point_grad, query_frame_grad, weight_grad, head_grad = pl.pallas_call(
         last_kernel,
         name="last",
-        in_specs=[SMEM_SPEC] + [VMEM_SPEC] * 4,
+        in_specs=[VMEM_SPEC] * 5,
         out_specs=[VMEM_SPEC] * 5,
         out_shape=[
             struct((8, 192)), struct((3, 8, 48)), struct((3, 4, 8)), struct((H, CZ)),
@@ -643,7 +646,7 @@
         ],
         compiler_params=pltpu.CompilerParams(vmem_limit_bytes=LIMIT),
         cost_estimate=cost(2, 1e6),
-    )(head_weight, last, qpo, fr, gpt_rows)
+    )(sig, last, qpo, fr, gpt_rows)
     return (
         pair_grad, query_grad.T, query_point_grad.transpose(0, 2, 1), query_frame_grad, key_grad.T,
         value_grad.T, key_point_grad.transpose(0, 2, 1), value_point_grad.transpose(0, 2, 1),

time: 70.2 us -> 68 us (0.969)
  Pallas kernels: 19.9 us -> 18 us
    pallas_call x3, Pallas kernels: 10.3 us -> 8.3 us  [the longest x1 3.73 us: per_device(): pl.pallas_call(pair_kernel, name='pair', grid=(steps,), in_specs=[VMEM_SP...]
  transfers between devices with their start and end apart: 8 -> 8, of which waited for: 6 -> 6; matrix products, arithmetic and copies ran while one was open for 0% -> 0% of each run, Pallas kernels for 9% -> 10%
where the time goes in v5:
time: 68 us; the launch traced here: 66.9 us
  blocking collectives  20.1 us (30%)
  Pallas kernels  18 us (26%)
  starting transfers between devices  15.3 us (22%)
  waiting for transfers between devices  12 us (18%)
  between operations  1.37 us (2%)
    all_to_all x1, blocking collectives, per_device(): everyone = lax.all_to_all(st, COL, 0, 0, tiled=True)  20.1 us
    ppermute x6, starting transfers between devices, onward(): return lax.ppermute(block, axis, [(n, (n + step) % 4) for n in range(4)])  10.4 us
    ppermute x6, waiting for transfers between devices, onward(): return lax.ppermute(block, axis, [(n, (n + step) % 4) for n in range(4)])  7.21 us
    pallas_call x1, Pallas kernels, per_device(): pl.pallas_call(logits_kernel, name='logits', in_specs=[SMEM_SPEC] + [HBM_...  6.22 us
    all_to_all x1, starting transfers between devices, per_device(): last = lax.all_to_all(send, COL, 0, 0, tiled=True)  4.87 us
    pallas_call x1, Pallas kernels, per_device(): pl.pallas_call(pair_kernel, name='pair', grid=(steps,), in_specs=[VMEM_SP...  3.73 us
    all_to_all x1, waiting for transfers between devices, per_device(): last = lax.all_to_all(send, COL, 0, 0, tiled=True)  2.92 us
    pallas_call x1, Pallas kernels, per_device(): pl.pallas_call(grads_kernel, name='grads', in_specs=[VMEM_SPEC] * 13, out...  2.91 us
  transfers between devices with their start and end apart: 8, of which 6 were waited for; matrix products, arithmetic and copies ran while one was open for 0% of the time, Pallas kernels for 10%

profile of v5, /device:TPU:2, one launch (start us, length us, event | category | flops | bytes accessed | tf_op | source)
XLA Modules:
  0.0 66.9 jit_solution(12206327016747029271)
XLA Ops:
  1.3 6.2 %logits.1 = (f32[12,64,256]{2,1,0:T(8,128)S(1)}, f32[12,64,256]{2,1,0:T(8,128)S(1)}, f32[8,24,128]{2,1,0:T(8,128)S(1)}, f32[192,64]{1,0:T(8,128)S(1)}, f32[192,6...) custom-call(s32[1]{0:T(128)S(6)} %copy.26.rc_ref, ...), custom_call_target="tpu_custom_call" | custom-call | flops 20000000 | bytes 6000000 | tf_op jit(solution)/shard_map/logits/pallas_call | solution.py:548
  7.5 20.1 %all_to_all.10.all_ref = f32[8,24,128]{2,1,0:T(8,128)S(1)} all-to-all(f32[8,24,128]{2,1,0:T(8,128)S(1)} %get-tuple-element.53.own_ref), channel_id=1, replica_groups=mesh['row_0'=4,'row_1'=4,'row_2'=2,'col_0'=4,'col_1'=2] {'col_0','col_1'}, dimensions={0} | all-to-all | bytes 196608 | tf_op jit(solution)/shard_map/all_to_all | solution.py:582
  27.7 2.9 %grads.1 = (f32[2,2048,128]{2,1,0:T(8,128)S(1)}, f32[4,4,8,1024]{3,2,1,0:T(8,128)S(1)}, f32[4,4,8,1024]{3,2,1,0:T(8,128)S(1)}, f32[8,8,640]{2,1,0:T(8,128)S(1)}) custom-call(f32[16,128]{1,0:T(8,128)S(1)} %get-tuple-element.50.cf_ref, f32[12,64,256]{2,1,0:T(8,128)S(1)} %get-tuple-element.51.e_ref, f32[12,64,256]{2,1,0:T(8,128)S(1)} %get-tuple-element.52.p_ref, ...), custom_call_target="tpu_custom_call" | custom-call | flops 20000000 | bytes 8000000 | tf_op jit(solution)/shard_map/grads/pallas_call | solution.py:583
  30.6 0.1 collective-permute-start
  30.7 1.9 %collective-permute-done.refs_1_ = f32[4,4,8,1024]{3,2,1,0:T(8,128)S(1)} collective-permute-done((f32[4,4,8,1024]{3,2,1,0:T(8,128)S(1)}, f32[4,4,8,1024]{3,2,1,0:T(8,128)S(1)}, u32[]{:S(2)}, u32[]{:S(2)}) %collective-permute-start) | collective-permute-done | bytes 524320 | tf_op jit(solution)/shard_map/ppermute | solution.py:598
  32.6 0.0 copy-start.6
  32.6 0.1 chip.1
  32.6 1.7 %collective-permute-start.1 = (f32[4,8,1024]{2,1,0:T(8,128)S(1)}, f32[4,8,1024]{2,1,0:T(8,128)S(1)}, u32[]{:S(2)}, u32[]{:S(2)}) collective-permute-start(f32[4,8,1024]{2,1,0:T(8,128)S(1)} %get-tuple-element.67), channel_id=1, source_target_pairs={{0,16},{16,32},{32,48},{48,0},{1,17},{17,33},{33,49},{49,1},{2,18}... | collective-permute-start | bytes 393224 | tf_op jit(solution)/shard_map/ppermute | solution.py:527
  34.3 2.9 %collective-permute-start.2 = (f32[4,8,1024]{2,1,0:T(8,128)S(1)}, f32[4,8,1024]{2,1,0:T(8,128)S(1)}, u32[]{:S(2)}, u32[]{:S(2)}) collective-permute-start(f32[4,8,1024]{2,1,0:T(8,128)S(1)} %get-tuple-element.68), channel_id=1, source_target_pairs={{0,32},{16,48},{32,0},{48,16},{1,33},{17,49},{33,1},{49,17},{2,34}... | collective-permute-start | bytes 393224 | tf_op jit(solution)/shard_map/ppermute | solution.py:527
  37.2 1.3 %collective-permute-start.3 = (f32[4,8,1024]{2,1,0:T(8,128)S(1)}, f32[4,8,1024]{2,1,0:T(8,128)S(1)}, u32[]{:S(2)}, u32[]{:S(2)}) collective-permute-start(f32[4,8,1024]{2,1,0:T(8,128)S(1)} %get-tuple-element.69), channel_id=1, source_target_pairs={{0,48},{16,0},{32,16},{48,32},{1,49},{17,1},{33,17},{49,33},{2,50}... | collective-permute-start | bytes 393224 | tf_op jit(solution)/shard_map/ppermute | solution.py:527
  38.6 1.0 %collective-permute-done.1.refs_1_ = f32[4,8,1024]{2,1,0:T(8,128)S(1)} collective-permute-done((f32[4,8,1024]{2,1,0:T(8,128)S(1)}, f32[4,8,1024]{2,1,0:T(8,128)S(1)}, u32[]{:S(2)}, u32[]{:S(2)}) %collective-permute-start.1) | collective-permute-done | bytes 131104 | tf_op jit(solution)/shard_map/ppermute | solution.py:527
  39.5 4.0 %collective-permute-done.2.refs_2_ = f32[4,8,1024]{2,1,0:T(8,128)S(1)} collective-permute-done((f32[4,8,1024]{2,1,0:T(8,128)S(1)}, f32[4,8,1024]{2,1,0:T(8,128)S(1)}, u32[]{:S(2)}, u32[]{:S(2)}) %collective-permute-start.2) | collective-permute-done | bytes 131104 | tf_op jit(solution)/shard_map/ppermute | solution.py:527
  43.6 1.1 %collective-permute-start.4 = (f32[8,1024]{1,0:T(8,128)S(1)}, f32[8,1024]{1,0:T(8,128)S(1)}, u32[]{:S(2)}, u32[]{:S(2)}) collective-permute-start(f32[8,1024]{1,0:T(8,128)S(1)} %get-tuple-element.71), channel_id=1, source_target_pairs={{0,64},{64,128},{128,192},{192,0},{1,65},{65,129},{129,193},{193,1... | collective-permute-start | bytes 98312 | tf_op jit(solution)/shard_map/ppermute | solution.py:527
  44.7 1.4 %collective-permute-start.5 = (f32[8,1024]{1,0:T(8,128)S(1)}, f32[8,1024]{1,0:T(8,128)S(1)}, u32[]{:S(2)}, u32[]{:S(2)}) collective-permute-start(f32[8,1024]{1,0:T(8,128)S(1)} %get-tuple-element.72), channel_id=1, source_target_pairs={{0,128},{64,192},{128,0},{192,64},{1,129},{65,193},{129,1},{193,65... | collective-permute-start | bytes 98312 | tf_op jit(solution)/shard_map/ppermute | solution.py:527
  46.1 1.9 %collective-permute-start.6 = (f32[8,1024]{1,0:T(8,128)S(1)}, f32[8,1024]{1,0:T(8,128)S(1)}, u32[]{:S(2)}, u32[]{:S(2)}) collective-permute-start(f32[8,1024]{1,0:T(8,128)S(1)} %get-tuple-element.73), channel_id=1, source_target_pairs={{0,192},{64,0},{128,64},{192,128},{1,193},{65,1},{129,65},{193,129... | collective-permute-start | bytes 98312 | tf_op jit(solution)/shard_map/ppermute | solution.py:527
  48.0 1.4 %collective-permute-done.4.b_ref = f32[8,1024]{1,0:T(8,128)S(1)} collective-permute-done((f32[8,1024]{1,0:T(8,128)S(1)}, f32[8,1024]{1,0:T(8,128)S(1)}, u32[]{:S(2)}, u32[]{:S(2)}) %collective-permute-start.4) | collective-permute-done | bytes 32800 | tf_op jit(solution)/shard_map/ppermute | solution.py:527
  49.4 0.8 %collective-permute-done.5.c_ref = f32[8,1024]{1,0:T(8,128)S(1)} collective-permute-done((f32[8,1024]{1,0:T(8,128)S(1)}, f32[8,1024]{1,0:T(8,128)S(1)}, u32[]{:S(2)}, u32[]{:S(2)}) %collective-permute-start.5) | collective-permute-done | bytes 32800 | tf_op jit(solution)/shard_map/ppermute | solution.py:527
  50.3 0.0 collective-permute-done.6.d_ref
  50.3 0.7 %mid.1 = (f32[8,1024]{1,0:T(8,128)S(1)}, f32[8,8,896]{2,1,0:T(8,128)}) custom-call(f32[8,1024]{1,0:T(8,128)S(1)} %get-tuple-element.70.a_ref, f32[8,1024]{1,0:T(8,128)S(1)} %collective-permute-done.4.b_ref, f32[8,1024]{1,0:T(8,128)S(1)} %collective-permute-done.5.c_ref, f32[8,1024]{1,0:T(8,128)S(1)} %collective-permute-done.6.d_ref, ...), custom_call_target="tpu_custom_call" | custom-call | flops 4000000 | bytes 1000000 | tf_op jit(solution)/shard_map/mid/pallas_call | solution.py:614
  51.0 4.9 %all-to-all-start.1 = ((f32[8,8,896]{2,1,0:T(8,128)}), f32[8,8,896]{2,1,0:T(8,128)S(1)}, u32[]{:S(2)}, u32[]{:S(2)}) async-start(f32[8,8,896]{2,1,0:T(8,128)} %get-tuple-element.75), calls=%async_computation.1 | async-start | bytes 458752 | tf_op jit(solution)/shard_map/all_to_all | solution.py:623
  55.9 3.7 %pair.1 = bf16[64,256,128]{2,1,0:T(8,128)(2,1)} custom-call(f32[2,2048,128]{2,1,0:T(8,128)S(1)} %get-tuple-element.62.da_ref, bf16[12,64,128]{2,1,0:T(8,128)(2,1)S(1)} %bitcast.14, bf16[12,128]{1,0:T(8,128)(2,1)S(1)} %bitcast.18), custom_call_target="tpu_custom_call" | custom-call | flops 24000000 | bytes 6000000 | tf_op jit(solution)/shard_map/pair/pallas_call | solution.py:603
  59.6 2.7 %keyout.1 = (f32[8,192]{1,0:T(8,128)}, f32[8,192]{1,0:T(8,128)}, f32[3,8,48]{2,1,0:T(8,128)}, f32[3,8,96]{2,1,0:T(8,128)}, f32[3,4,8]{2,1,0:T(4,128)}, /*index=5*/f32[8,256]{1,0:T(8,128)S(1)}, f32[8,128]{1,0:T(8,128)S(1)}) custom-call(f32[8,1024]{1,0:T(8,128)S(1)} %get-tuple-element.76.keys_ref, f32[3,48,256]{2,1,0:T(8,128)S(1)} %copy-done.2, ...), custom_call_target="tpu_custom_call" | custom-call | flops 8000000 | bytes 1000000 | tf_op jit(solution)/shard_map/keyout/pallas_call | solution.py:625
  62.3 2.9 %all-to-all-done.1.parts_ref = f32[8,8,896]{2,1,0:T(8,128)S(1)} async-done(((f32[8,8,896]{2,1,0:T(8,128)}), f32[8,8,896]{2,1,0:T(8,128)S(1)}, u32[]{:S(2)}, u32[]{:S(2)}) %all-to-all-start.1) | async-done | bytes 229408 | tf_op jit(solution)/shard_map/all_to_all | solution.py:623
  65.2 1.7 %last.1 = (f32[8,192]{1,0:T(8,128)}, f32[3,8,48]{2,1,0:T(8,128)}, f32[3,4,8]{2,1,0:T(4,128)}, f32[12,128]{1,0:T(8,128)}, f32[1,12]{1,0:T(1,128)}) custom-call(f32[8,128]{1,0:T(8,128)S(1)} %get-tuple-element.63.sig_ref, f32[8,8,896]{2,1,0:T(8,128)S(1)} %all-to-all-done.1.parts_ref, f32[8,256]{1,0:T(8,128)S(1)} %get-tuple-element.77.qpo_ref, ...), custom_call_target="tpu_custom_call" | custom-call | flops 8000000 | bytes 1000000 | tf_op jit(solution)/shard_map/last/pallas_call | solution.py:638
  (17 shorter events, 0.1 us)
Async XLA Ops:
  27.6 28.2 %copy-start.1 = (bf16[64,12,128]{2,0,1:T(8,128)(2,1)S(1)}, bf16[64,12,128]{2,0,1:T(8,128)(2,1)}, u32[]{:S(2)}) copy-start(bf16[64,12,128]{2,0,1:T(8,128)(2,1)} %param.29) | copy-start | bytes 589828
  27.6 28.2 %copy-start.7 = (bf16[128,12]{0,1:T(8,128)(2,1)S(1)}, bf16[128,12]{0,1:T(8,128)(2,1)}, u32[]{:S(2)}) copy-start(bf16[128,12]{0,1:T(8,128)(2,1)} %param.16) | copy-start | bytes 9220
  30.6 2.0 %collective-permute-start = (f32[4,4,8,1024]{3,2,1,0:T(8,128)S(1)}, f32[4,4,8,1024]{3,2,1,0:T(8,128)S(1)}, u32[]{:S(2)}, u32[]{:S(2)}) collective-permute-start(f32[4,4,8,1024]{3,2,1,0:T(8,128)S(1)} %get-tuple-element.65), channel_id=1, source_target_pairs={{0,8},{8,0},{1,9},{9,1},{2,10},{10,2},{3,11},{11,3},{4,12},{12,4},... | collective-permute-start | bytes 1572872 | tf_op jit(solution)/shard_map/ppermute | solution.py:598
  32.6 27.0 %copy-start = (f32[3,96,256]{2,1,0:T(8,128)S(1)}, f32[3,96,256]{2,1,0:T(8,128)}, u32[]{:S(2)}) copy-start(f32[3,96,256]{2,1,0:T(8,128)} %vp_ref.1) | copy-start | bytes 884740
  32.6 27.0 %copy-start.2 = (f32[3,48,256]{2,1,0:T(8,128)S(1)}, f32[3,48,256]{2,1,0:T(8,128)}, u32[]{:S(2)}) copy-start(f32[3,48,256]{2,1,0:T(8,128)} %kp_ref.1) | copy-start | bytes 442372
  32.6 27.0 %copy-start.4 = (f32[3,3,2048]{2,1,0:T(4,128)S(1)}, f32[3,3,2048]{2,1,0:T(4,128)}, u32[]{:S(2)}) copy-start(f32[3,3,2048]{2,1,0:T(4,128)} %rot_ref.1) | copy-start | bytes 221188
  32.6 27.0 %copy-start.5 = (f32[3,48,64]{2,1,0:T(8,128)S(1)}, f32[3,48,64]{2,1,0:T(8,128)}, u32[]{:S(2)}) copy-start(f32[3,48,64]{2,1,0:T(8,128)} %qp_ref.1) | copy-start | bytes 110596
  32.6 27.1 %copy-start.6 = (f32[3,2048]{1,0:T(4,128)S(1)}, f32[3,2048]{1,0:T(4,128)}, u32[]{:S(2)}) copy-start(f32[3,2048]{1,0:T(4,128)} %tr_ref.1) | copy-start | bytes 73732
  32.6 6.9 %collective-permute-start.1 = (f32[4,8,1024]{2,1,0:T(8,128)S(1)}, f32[4,8,1024]{2,1,0:T(8,128)S(1)}, u32[]{:S(2)}, u32[]{:S(2)}) collective-permute-start(f32[4,8,1024]{2,1,0:T(8,128)S(1)} %get-tuple-element.67), channel_id=1, source_target_pairs={{0,16},{16,32},{32,48},{48,0},{1,17},{17,33},{33,49},{49,1},{2,18}... | collective-permute-start | bytes 393224 | tf_op jit(solution)/shard_map/ppermute | solution.py:527
  34.3 9.2 %collective-permute-start.2 = (f32[4,8,1024]{2,1,0:T(8,128)S(1)}, f32[4,8,1024]{2,1,0:T(8,128)S(1)}, u32[]{:S(2)}, u32[]{:S(2)}) collective-permute-start(f32[4,8,1024]{2,1,0:T(8,128)S(1)} %get-tuple-element.68), channel_id=1, source_target_pairs={{0,32},{16,48},{32,0},{48,16},{1,33},{17,49},{33,1},{49,17},{2,34}... | collective-permute-start | bytes 393224 | tf_op jit(solution)/shard_map/ppermute | solution.py:527
  37.2 6.3 %collective-permute-start.3 = (f32[4,8,1024]{2,1,0:T(8,128)S(1)}, f32[4,8,1024]{2,1,0:T(8,128)S(1)}, u32[]{:S(2)}, u32[]{:S(2)}) collective-permute-start(f32[4,8,1024]{2,1,0:T(8,128)S(1)} %get-tuple-element.69), channel_id=1, source_target_pairs={{0,48},{16,0},{32,16},{48,32},{1,49},{17,1},{33,17},{49,33},{2,50}... | collective-permute-start | bytes 393224 | tf_op jit(solution)/shard_map/ppermute | solution.py:527
  43.5 21.7 %copy-start.3 = (f32[3,96,64]{1,2,0:T(8,128)S(1)}, f32[3,96,64]{1,2,0:T(8,128)}, u32[]{:S(2)}) copy-start(f32[3,96,64]{1,2,0:T(8,128)} %param.28) | copy-start | bytes 221188
  43.6 5.9 %collective-permute-start.4 = (f32[8,1024]{1,0:T(8,128)S(1)}, f32[8,1024]{1,0:T(8,128)S(1)}, u32[]{:S(2)}, u32[]{:S(2)}) collective-permute-start(f32[8,1024]{1,0:T(8,128)S(1)} %get-tuple-element.71), channel_id=1, source_target_pairs={{0,64},{64,128},{128,192},{192,0},{1,65},{65,129},{129,193},{193,1... | collective-permute-start | bytes 98312 | tf_op jit(solution)/shard_map/ppermute | solution.py:527
  44.7 5.6 %collective-permute-start.5 = (f32[8,1024]{1,0:T(8,128)S(1)}, f32[8,1024]{1,0:T(8,128)S(1)}, u32[]{:S(2)}, u32[]{:S(2)}) collective-permute-start(f32[8,1024]{1,0:T(8,128)S(1)} %get-tuple-element.72), channel_id=1, source_target_pairs={{0,128},{64,192},{128,0},{192,64},{1,129},{65,193},{129,1},{193,65... | collective-permute-start | bytes 98312 | tf_op jit(solution)/shard_map/ppermute | solution.py:527
  46.1 4.2 %collective-permute-start.6 = (f32[8,1024]{1,0:T(8,128)S(1)}, f32[8,1024]{1,0:T(8,128)S(1)}, u32[]{:S(2)}, u32[]{:S(2)}) collective-permute-start(f32[8,1024]{1,0:T(8,128)S(1)} %get-tuple-element.73), channel_id=1, source_target_pairs={{0,192},{64,0},{128,64},{192,128},{1,193},{65,1},{129,65},{193,129... | collective-permute-start | bytes 98312 | tf_op jit(solution)/shard_map/ppermute | solution.py:527
  51.0 14.2 %all-to-all-start.1 = ((f32[8,8,896]{2,1,0:T(8,128)}), f32[8,8,896]{2,1,0:T(8,128)S(1)}, u32[]{:S(2)}, u32[]{:S(2)}) async-start(f32[8,8,896]{2,1,0:T(8,128)} %get-tuple-element.75), calls=%async_computation.1 | async-start | bytes 458752 | tf_op jit(solution)/shard_map/all_to_all | solution.py:623

commit v6 on v5

--- a/solution.py
+++ b/solution.py
@@ -25,7 +25,7 @@
 
 KEY0, VAL0, KPT0, VPT0, KEND = 0, 192, 384, 528, 816
 QRY0, QPT0, OPT0, QEND = 0, 192, 336, 624
-KW, QW = 1024, 640
+KW, QW, LW = 1024, 640, 3712
 LIMIT = 20 << 20
 QB = 16
 PB = 16
@@ -151,8 +151,7 @@
     wt = jnp.concatenate([bw_ref[...].astype(F32), jnp.zeros((4, CZ), F32)], 0)
     gs_ref[...] = gp_ref[...].astype(F32).reshape(H * IQ, CZ)
 
-    @pl.loop(0, IQ // PB)
-    def _(b):
+    for b in range(IQ // PB):
         pair_copy(b).wait()
         for n in range(PB):
             at = b * PB + n
@@ -329,8 +328,7 @@
             hs = jnp.where(lane == 48 + h, part, hs)
         hs_ref[...] = hs
 
-    @pl.loop(0, IQ // PB)
-    def _(b):
+    for b in range(IQ // PB):
         dlogs = []
         for n in range(PB):
             at = b * PB + n
@@ -357,8 +355,6 @@
         ]
         def tile(j, t):
             b, r = divmod(j, 16)
-            if t == 7:
-                return w0
             piece = keys[b][t][8 * r : 8 * r + 8]
             return jnp.where(lane < 48, piece, extra) if t == 6 else piece
 
@@ -368,10 +364,14 @@
             z, y = divmod(zone, 4)
             dz = lax.rem(z + 4 - my_z, 4)
             dy = lax.rem(y + 4 - my_y, 4)
-            for t in range(8):
+            for t in range(7):
                 even, odd = tile(2 * zone, t), tile(2 * zone + 1, t)
-                keep_ref[dy, dz, :, 128 * t : 128 * t + 128] = jnp.where(first, even, odd)
-                give_ref[dy, dz, :, 128 * t : 128 * t + 128] = jnp.where(first, odd, even)
+                spot = pl.ds(pl.multiple_of(dz * 896 + 128 * t, 128), 128)
+                keep_ref[dy, :, spot] = jnp.where(first, even, odd)
+                give_ref[dy, :, spot] = jnp.where(first, odd, even)
+        for n in range(4):
+            keep_ref[n, :, 3584:LW] = w0
+            give_ref[n, :, 3584:LW] = w0
         for t in range(5):
             block = qp_ref[128 * t : 128 * t + 128]
             turned = jnp.concatenate([block, jnp.zeros((128, 64), F32)], 1).T
@@ -502,20 +502,26 @@
     hg_ref[...] = (sums * sig_ref[0:1])[:, :H]
 
 
-def fold_kernel(count, *refs):
-    ins, outs = refs[:-count], refs[-count:]
+def chip_kernel(keep_ref, got_ref, *outs):
     for n, out in enumerate(outs):
-        out[...] = sum(r[n] for r in ins[1:]) + ins[0][n]
-
-
-def fold_call(name, count, shape):
+        out[...] = keep_ref[n] + got_ref[n]
+
+
+def line_kernel(a_ref, b_ref, c_ref, d_ref, *outs):
+    total = (a_ref[...] + b_ref[...]) + (c_ref[...] + d_ref[...])
+    for n, out in enumerate(outs):
+        out[:, 0:896] = total[:, 896 * n : 896 * n + 896]
+        out[:, 896:KW] = total[:, 3584:LW]
+
+
+def fold_call(body, name, shape):
     def call(*parts):
         return pl.pallas_call(
-            functools.partial(fold_kernel, count),
+            body,
             name=name,
             in_specs=[VMEM_SPEC] * len(parts),
-            out_specs=[VMEM_SPEC] * count,
-            out_shape=[struct(shape)] * count,
+            out_specs=[VMEM_SPEC] * 4,
+            out_shape=[struct(shape)] * 4,
             compiler_params=pltpu.CompilerParams(vmem_limit_bytes=LIMIT),
             cost_estimate=cost(1, 1e6),
         )(*parts)
@@ -586,7 +592,7 @@
         in_specs=[VMEM_SPEC] * 13,
         out_specs=[VMEM_SPEC] * 4,
         out_shape=[
-            struct((2, 32 * IQ, 128)), struct((4, 4, 8, KW)), struct((4, 4, 8, KW)),
+            struct((2, 32 * IQ, 128)), struct((4, 8, LW)), struct((4, 8, LW)),
             struct((NCOL, 8, QW)),
         ],
         scratch_shapes=[
@@ -596,9 +602,9 @@
         cost_estimate=cost(5, 8e6),
     )(coef, e, p, st, everyone, q, keys, go, qg, kg, vg, gg, pair)
     swapped = lax.ppermute(give, "row_2", [(0, 1), (1, 0)])
-    chip = fold_call("chip", 4, (4, 8, KW))(keep, swapped)
+    chip = fold_call(chip_kernel, "chip", (8, LW))(keep, swapped)
     by_y = [chip[0]] + [onward(chip[n], "row_1", n) for n in range(1, 4)]
-    line = fold_call("line", 4, (8, KW))(*by_y)
+    line = fold_call(line_kernel, "line", (8, KW))(*by_y)
     parts = [line[0]] + [onward(line[n], "row_0", n) for n in range(1, 4)]
     pair_grad = pl.pallas_call(
         pair_kernel,

time: 68 us -> 66.7 us (0.981)
  Pallas kernels: 18 us -> 17.2 us
where the time goes in v6:
time: 66.7 us; the launch traced here: 65.6 us
  blocking collectives  20.1 us (30%)
  Pallas kernels  17.2 us (26%)
  starting transfers between devices  15.3 us (23%)
  waiting for transfers between devices  11.4 us (17%)
  between operations  1.37 us (2%)
    all_to_all x1, blocking collectives, per_device(): everyone = lax.all_to_all(st, COL, 0, 0, tiled=True)  20.1 us
    ppermute x6, starting transfers between devices, onward(): return lax.ppermute(block, axis, [(n, (n + step) % 4) for n in range(4)])  10.4 us
    ppermute x6, waiting for transfers between devices, onward(): return lax.ppermute(block, axis, [(n, (n + step) % 4) for n in range(4)])  6.69 us
    pallas_call x1, Pallas kernels, per_device(): pl.pallas_call(logits_kernel, name='logits', in_specs=[SMEM_SPEC] + [HBM_...  6.08 us
    all_to_all x1, starting transfers between devices, per_device(): last = lax.all_to_all(send, COL, 0, 0, tiled=True)  4.87 us
    pallas_call x1, Pallas kernels, per_device(): pl.pallas_call(pair_kernel, name='pair', grid=(steps,), in_specs=[VMEM_SP...  3.73 us
    all_to_all x1, waiting for transfers between devices, per_device(): last = lax.all_to_all(send, COL, 0, 0, tiled=True)  2.93 us
    pallas_call x1, Pallas kernels, per_device(): pl.pallas_call(key_kernel, name='keyout', in_specs=[VMEM_SPEC] * 6, out_s...  2.68 us
  transfers between devices with their start and end apart: 8, of which 6 were waited for; matrix products, arithmetic and copies ran while one was open for 0% of the time, Pallas kernels for 10%

profile of v6, /device:TPU:2, one launch (start us, length us, event | category | flops | bytes accessed | tf_op | source)
XLA Modules:
  0.0 65.6 jit_solution(6695362614092645769)
XLA Ops:
  1.3 6.1 %logits.1 = (f32[12,64,256]{2,1,0:T(8,128)S(1)}, f32[12,64,256]{2,1,0:T(8,128)S(1)}, f32[8,24,128]{2,1,0:T(8,128)S(1)}, f32[192,64]{1,0:T(8,128)S(1)}, f32[192,6...) custom-call(s32[1]{0:T(128)S(6)} %copy.26.rc_ref, ...), custom_call_target="tpu_custom_call" | custom-call | flops 20000000 | bytes 6000000 | tf_op jit(solution)/shard_map/logits/pallas_call | solution.py:554
  7.4 20.1 %all_to_all.10.all_ref = f32[8,24,128]{2,1,0:T(8,128)S(1)} all-to-all(f32[8,24,128]{2,1,0:T(8,128)S(1)} %get-tuple-element.53.own_ref), channel_id=1, replica_groups=mesh['row_0'=4,'row_1'=4,'row_2'=2,'col_0'=4,'col_1'=2] {'col_0','col_1'}, dimensions={0} | all-to-all | bytes 196608 | tf_op jit(solution)/shard_map/all_to_all | solution.py:588
  27.5 2.3 %grads.1 = (f32[2,2048,128]{2,1,0:T(8,128)S(1)}, f32[4,8,3712]{2,1,0:T(8,128)S(1)}, f32[4,8,3712]{2,1,0:T(8,128)S(1)}, f32[8,8,640]{2,1,0:T(8,128)S(1)}) custom-call(f32[16,128]{1,0:T(8,128)S(1)} %get-tuple-element.50.cf_ref, f32[12,64,256]{2,1,0:T(8,128)S(1)} %get-tuple-element.51.e_ref, f32[12,64,256]{2,1,0:T(8,128)S(1)} %get-tuple-element.52.p_ref, ...), custom_call_target="tpu_custom_call" | custom-call | flops 20000000 | bytes 8000000 | tf_op jit(solution)/shard_map/grads/pallas_call | solution.py:589
  29.8 0.1 collective-permute-start
  29.9 1.8 %collective-permute-done.got_ref = f32[4,8,3712]{2,1,0:T(8,128)S(1)} collective-permute-done((f32[4,8,3712]{2,1,0:T(8,128)S(1)}, f32[4,8,3712]{2,1,0:T(8,128)S(1)}, u32[]{:S(2)}, u32[]{:S(2)}) %collective-permute-start) | collective-permute-done | bytes 475168 | tf_op jit(solution)/shard_map/ppermute | solution.py:604
  31.8 0.0 copy-start.6
  31.8 0.1 chip.1
  31.8 1.7 %collective-permute-start.1 = (f32[8,3712]{1,0:T(8,128)S(1)}, f32[8,3712]{1,0:T(8,128)S(1)}, u32[]{:S(2)}, u32[]{:S(2)}) collective-permute-start(f32[8,3712]{1,0:T(8,128)S(1)} %get-tuple-element.67), channel_id=1, source_target_pairs={{0,16},{16,32},{32,48},{48,0},{1,17},{17,33},{33,49},{49,1},{2,18}... | collective-permute-start | bytes 356360 | tf_op jit(solution)/shard_map/ppermute | solution.py:533
  33.5 2.9 %collective-permute-start.2 = (f32[8,3712]{1,0:T(8,128)S(1)}, f32[8,3712]{1,0:T(8,128)S(1)}, u32[]{:S(2)}, u32[]{:S(2)}) collective-permute-start(f32[8,3712]{1,0:T(8,128)S(1)} %get-tuple-element.68), channel_id=1, source_target_pairs={{0,32},{16,48},{32,0},{48,16},{1,33},{17,49},{33,1},{49,17},{2,34}... | collective-permute-start | bytes 356360 | tf_op jit(solution)/shard_map/ppermute | solution.py:533
  36.4 1.3 %collective-permute-start.3 = (f32[8,3712]{1,0:T(8,128)S(1)}, f32[8,3712]{1,0:T(8,128)S(1)}, u32[]{:S(2)}, u32[]{:S(2)}) collective-permute-start(f32[8,3712]{1,0:T(8,128)S(1)} %get-tuple-element.69), channel_id=1, source_target_pairs={{0,48},{16,0},{32,16},{48,32},{1,49},{17,1},{33,17},{49,33},{2,50}... | collective-permute-start | bytes 356360 | tf_op jit(solution)/shard_map/ppermute | solution.py:533
  37.7 0.7 %collective-permute-done.1.b_ref = f32[8,3712]{1,0:T(8,128)S(1)} collective-permute-done((f32[8,3712]{1,0:T(8,128)S(1)}, f32[8,3712]{1,0:T(8,128)S(1)}, u32[]{:S(2)}, u32[]{:S(2)}) %collective-permute-start.1) | collective-permute-done | bytes 118816 | tf_op jit(solution)/shard_map/ppermute | solution.py:533
  38.5 3.7 %collective-permute-done.2.c_ref = f32[8,3712]{1,0:T(8,128)S(1)} collective-permute-done((f32[8,3712]{1,0:T(8,128)S(1)}, f32[8,3712]{1,0:T(8,128)S(1)}, u32[]{:S(2)}, u32[]{:S(2)}) %collective-permute-start.2) | collective-permute-done | bytes 118816 | tf_op jit(solution)/shard_map/ppermute | solution.py:533
  42.2 1.1 %collective-permute-start.4 = (f32[8,1024]{1,0:T(8,128)S(1)}, f32[8,1024]{1,0:T(8,128)S(1)}, u32[]{:S(2)}, u32[]{:S(2)}) collective-permute-start(f32[8,1024]{1,0:T(8,128)S(1)} %get-tuple-element.71), channel_id=1, source_target_pairs={{0,64},{64,128},{128,192},{192,0},{1,65},{65,129},{129,193},{193,1... | collective-permute-start | bytes 98312 | tf_op jit(solution)/shard_map/ppermute | solution.py:533
  43.3 1.4 %collective-permute-start.5 = (f32[8,1024]{1,0:T(8,128)S(1)}, f32[8,1024]{1,0:T(8,128)S(1)}, u32[]{:S(2)}, u32[]{:S(2)}) collective-permute-start(f32[8,1024]{1,0:T(8,128)S(1)} %get-tuple-element.72), channel_id=1, source_target_pairs={{0,128},{64,192},{128,0},{192,64},{1,129},{65,193},{129,1},{193,65... | collective-permute-start | bytes 98312 | tf_op jit(solution)/shard_map/ppermute | solution.py:533
  44.8 1.9 %collective-permute-start.6 = (f32[8,1024]{1,0:T(8,128)S(1)}, f32[8,1024]{1,0:T(8,128)S(1)}, u32[]{:S(2)}, u32[]{:S(2)}) collective-permute-start(f32[8,1024]{1,0:T(8,128)S(1)} %get-tuple-element.73), channel_id=1, source_target_pairs={{0,192},{64,0},{128,64},{192,128},{1,193},{65,1},{129,65},{193,129... | collective-permute-start | bytes 98312 | tf_op jit(solution)/shard_map/ppermute | solution.py:533
  46.7 1.4 %collective-permute-done.4.b_ref = f32[8,1024]{1,0:T(8,128)S(1)} collective-permute-done((f32[8,1024]{1,0:T(8,128)S(1)}, f32[8,1024]{1,0:T(8,128)S(1)}, u32[]{:S(2)}, u32[]{:S(2)}) %collective-permute-start.4) | collective-permute-done | bytes 32800 | tf_op jit(solution)/shard_map/ppermute | solution.py:533
  48.1 0.8 %collective-permute-done.5.c_ref = f32[8,1024]{1,0:T(8,128)S(1)} collective-permute-done((f32[8,1024]{1,0:T(8,128)S(1)}, f32[8,1024]{1,0:T(8,128)S(1)}, u32[]{:S(2)}, u32[]{:S(2)}) %collective-permute-start.5) | collective-permute-done | bytes 32800 | tf_op jit(solution)/shard_map/ppermute | solution.py:533
  48.9 0.0 collective-permute-done.6.d_ref
  48.9 0.7 %mid.1 = (f32[8,1024]{1,0:T(8,128)S(1)}, f32[8,8,896]{2,1,0:T(8,128)}) custom-call(f32[8,1024]{1,0:T(8,128)S(1)} %get-tuple-element.70.a_ref, f32[8,1024]{1,0:T(8,128)S(1)} %collective-permute-done.4.b_ref, f32[8,1024]{1,0:T(8,128)S(1)} %collective-permute-done.5.c_ref, f32[8,1024]{1,0:T(8,128)S(1)} %collective-permute-done.6.d_ref, ...), custom_call_target="tpu_custom_call" | custom-call | flops 4000000 | bytes 1000000 | tf_op jit(solution)/shard_map/mid/pallas_call | solution.py:620
  49.6 4.9 %all-to-all-start.1 = ((f32[8,8,896]{2,1,0:T(8,128)}), f32[8,8,896]{2,1,0:T(8,128)S(1)}, u32[]{:S(2)}, u32[]{:S(2)}) async-start(f32[8,8,896]{2,1,0:T(8,128)} %get-tuple-element.75), calls=%async_computation.1 | async-start | bytes 458752 | tf_op jit(solution)/shard_map/all_to_all | solution.py:629
  54.5 3.7 %pair.1 = bf16[64,256,128]{2,1,0:T(8,128)(2,1)} custom-call(f32[2,2048,128]{2,1,0:T(8,128)S(1)} %get-tuple-element.62.da_ref, bf16[12,64,128]{2,1,0:T(8,128)(2,1)S(1)} %bitcast.14, bf16[12,128]{1,0:T(8,128)(2,1)S(1)} %bitcast.18), custom_call_target="tpu_custom_call" | custom-call | flops 24000000 | bytes 6000000 | tf_op jit(solution)/shard_map/pair/pallas_call | solution.py:609
  58.3 2.7 %keyout.1 = (f32[8,192]{1,0:T(8,128)}, f32[8,192]{1,0:T(8,128)}, f32[3,8,48]{2,1,0:T(8,128)}, f32[3,8,96]{2,1,0:T(8,128)}, f32[3,4,8]{2,1,0:T(4,128)}, /*index=5*/f32[8,256]{1,0:T(8,128)S(1)}, f32[8,128]{1,0:T(8,128)S(1)}) custom-call(f32[8,1024]{1,0:T(8,128)S(1)} %get-tuple-element.76.keys_ref, f32[3,48,256]{2,1,0:T(8,128)S(1)} %copy-done.2, ...), custom_call_target="tpu_custom_call" | custom-call | flops 8000000 | bytes 1000000 | tf_op jit(solution)/shard_map/keyout/pallas_call | solution.py:631
  61.0 2.9 %all-to-all-done.1.parts_ref = f32[8,8,896]{2,1,0:T(8,128)S(1)} async-done(((f32[8,8,896]{2,1,0:T(8,128)}), f32[8,8,896]{2,1,0:T(8,128)S(1)}, u32[]{:S(2)}, u32[]{:S(2)}) %all-to-all-start.1) | async-done | bytes 229408 | tf_op jit(solution)/shard_map/all_to_all | solution.py:629
  63.9 1.7 %last.1 = (f32[8,192]{1,0:T(8,128)}, f32[3,8,48]{2,1,0:T(8,128)}, f32[3,4,8]{2,1,0:T(4,128)}, f32[12,128]{1,0:T(8,128)}, f32[1,12]{1,0:T(1,128)}) custom-call(f32[8,128]{1,0:T(8,128)S(1)} %get-tuple-element.63.sig_ref, f32[8,8,896]{2,1,0:T(8,128)S(1)} %all-to-all-done.1.parts_ref, f32[8,256]{1,0:T(8,128)S(1)} %get-tuple-element.77.qpo_ref, ...), custom_call_target="tpu_custom_call" | custom-call | flops 8000000 | bytes 1000000 | tf_op jit(solution)/shard_map/last/pallas_call | solution.py:644
  (17 shorter events, 0.1 us)
Async XLA Ops:
  27.5 27.0 %copy-start.1 = (bf16[64,12,128]{2,0,1:T(8,128)(2,1)S(1)}, bf16[64,12,128]{2,0,1:T(8,128)(2,1)}, u32[]{:S(2)}) copy-start(bf16[64,12,128]{2,0,1:T(8,128)(2,1)} %param.29) | copy-start | bytes 589828
  27.5 27.0 %copy-start.7 = (bf16[128,12]{0,1:T(8,128)(2,1)S(1)}, bf16[128,12]{0,1:T(8,128)(2,1)}, u32[]{:S(2)}) copy-start(bf16[128,12]{0,1:T(8,128)(2,1)} %param.16) | copy-start | bytes 9220
  29.8 1.9 %collective-permute-start = (f32[4,8,3712]{2,1,0:T(8,128)S(1)}, f32[4,8,3712]{2,1,0:T(8,128)S(1)}, u32[]{:S(2)}, u32[]{:S(2)}) collective-permute-start(f32[4,8,3712]{2,1,0:T(8,128)S(1)} %get-tuple-element.65), channel_id=1, source_target_pairs={{0,8},{8,0},{1,9},{9,1},{2,10},{10,2},{3,11},{11,3},{4,12},{12,4},... | collective-permute-start | bytes 1425416 | tf_op jit(solution)/shard_map/ppermute | solution.py:604
  31.7 26.5 %copy-start = (f32[3,96,256]{2,1,0:T(8,128)S(1)}, f32[3,96,256]{2,1,0:T(8,128)}, u32[]{:S(2)}) copy-start(f32[3,96,256]{2,1,0:T(8,128)} %vp_ref.1) | copy-start | bytes 884740
  31.8 26.5 %copy-start.2 = (f32[3,48,256]{2,1,0:T(8,128)S(1)}, f32[3,48,256]{2,1,0:T(8,128)}, u32[]{:S(2)}) copy-start(f32[3,48,256]{2,1,0:T(8,128)} %kp_ref.1) | copy-start | bytes 442372
  31.8 26.5 %copy-start.4 = (f32[3,3,2048]{2,1,0:T(4,128)S(1)}, f32[3,3,2048]{2,1,0:T(4,128)}, u32[]{:S(2)}) copy-start(f32[3,3,2048]{2,1,0:T(4,128)} %rot_ref.1) | copy-start | bytes 221188
  31.8 26.5 %copy-start.5 = (f32[3,48,64]{2,1,0:T(8,128)S(1)}, f32[3,48,64]{2,1,0:T(8,128)}, u32[]{:S(2)}) copy-start(f32[3,48,64]{2,1,0:T(8,128)} %qp_ref.1) | copy-start | bytes 110596
  31.8 26.5 %copy-start.6 = (f32[3,2048]{1,0:T(4,128)S(1)}, f32[3,2048]{1,0:T(4,128)}, u32[]{:S(2)}) copy-start(f32[3,2048]{1,0:T(4,128)} %tr_ref.1) | copy-start | bytes 73732
  31.8 6.6 %collective-permute-start.1 = (f32[8,3712]{1,0:T(8,128)S(1)}, f32[8,3712]{1,0:T(8,128)S(1)}, u32[]{:S(2)}, u32[]{:S(2)}) collective-permute-start(f32[8,3712]{1,0:T(8,128)S(1)} %get-tuple-element.67), channel_id=1, source_target_pairs={{0,16},{16,32},{32,48},{48,0},{1,17},{17,33},{33,49},{49,1},{2,18}... | collective-permute-start | bytes 356360 | tf_op jit(solution)/shard_map/ppermute | solution.py:533
  33.5 8.7 %collective-permute-start.2 = (f32[8,3712]{1,0:T(8,128)S(1)}, f32[8,3712]{1,0:T(8,128)S(1)}, u32[]{:S(2)}, u32[]{:S(2)}) collective-permute-start(f32[8,3712]{1,0:T(8,128)S(1)} %get-tuple-element.68), channel_id=1, source_target_pairs={{0,32},{16,48},{32,0},{48,16},{1,33},{17,49},{33,1},{49,17},{2,34}... | collective-permute-start | bytes 356360 | tf_op jit(solution)/shard_map/ppermute | solution.py:533
  36.4 5.8 %collective-permute-start.3 = (f32[8,3712]{1,0:T(8,128)S(1)}, f32[8,3712]{1,0:T(8,128)S(1)}, u32[]{:S(2)}, u32[]{:S(2)}) collective-permute-start(f32[8,3712]{1,0:T(8,128)S(1)} %get-tuple-element.69), channel_id=1, source_target_pairs={{0,48},{16,0},{32,16},{48,32},{1,49},{17,1},{33,17},{49,33},{2,50}... | collective-permute-start | bytes 356360 | tf_op jit(solution)/shard_map/ppermute | solution.py:533
  42.2 21.7 %copy-start.3 = (f32[3,96,64]{1,2,0:T(8,128)S(1)}, f32[3,96,64]{1,2,0:T(8,128)}, u32[]{:S(2)}) copy-start(f32[3,96,64]{1,2,0:T(8,128)} %param.28) | copy-start | bytes 221188
  42.2 5.9 %collective-permute-start.4 = (f32[8,1024]{1,0:T(8,128)S(1)}, f32[8,1024]{1,0:T(8,128)S(1)}, u32[]{:S(2)}, u32[]{:S(2)}) collective-permute-start(f32[8,1024]{1,0:T(8,128)S(1)} %get-tuple-element.71), channel_id=1, source_target_pairs={{0,64},{64,128},{128,192},{192,0},{1,65},{65,129},{129,193},{193,1... | collective-permute-start | bytes 98312 | tf_op jit(solution)/shard_map/ppermute | solution.py:533
  43.3 5.6 %collective-permute-start.5 = (f32[8,1024]{1,0:T(8,128)S(1)}, f32[8,1024]{1,0:T(8,128)S(1)}, u32[]{:S(2)}, u32[]{:S(2)}) collective-permute-start(f32[8,1024]{1,0:T(8,128)S(1)} %get-tuple-element.72), channel_id=1, source_target_pairs={{0,128},{64,192},{128,0},{192,64},{1,129},{65,193},{129,1},{193,65... | collective-permute-start | bytes 98312 | tf_op jit(solution)/shard_map/ppermute | solution.py:533
  44.8 4.2 %collective-permute-start.6 = (f32[8,1024]{1,0:T(8,128)S(1)}, f32[8,1024]{1,0:T(8,128)S(1)}, u32[]{:S(2)}, u32[]{:S(2)}) collective-permute-start(f32[8,1024]{1,0:T(8,128)S(1)} %get-tuple-element.73), channel_id=1, source_target_pairs={{0,192},{64,0},{128,64},{192,128},{1,193},{65,1},{129,65},{193,129... | collective-permute-start | bytes 98312 | tf_op jit(solution)/shard_map/ppermute | solution.py:533
  49.6 14.2 %all-to-all-start.1 = ((f32[8,8,896]{2,1,0:T(8,128)}), f32[8,8,896]{2,1,0:T(8,128)S(1)}, u32[]{:S(2)}, u32[]{:S(2)}) async-start(f32[8,8,896]{2,1,0:T(8,128)} %get-tuple-element.75), calls=%async_computation.1 | async-start | bytes 458752 | tf_op jit(solution)/shard_map/all_to_all | solution.py:629
